TPU v7x, 32 devices: a whole 2x2x4 slice. The times are simulated.
32 devices in a mesh: grp: 4 (over y, x), sub: 8 (over z, core).
Axes of the slice: x: 2, y: 2, z: 4, core: 2. Of those that a mesh axis runs over, the one named last changes fastest.
Arguments:
- reg_disp: float32 [4, 8, 3, 384], P('grp', 'sub'), may hold values from -6 to 6
- reg_vel: float32 [4, 8, 3, 384], P('grp', 'sub'), may hold values from -0.6 to 0.6
- site_disp: float32 [4, 8, 3, 1536], P('grp', 'sub'), may hold values from -6 to 6
- site_vel: float32 [4, 8, 3, 1536], P('grp', 'sub'), may hold values from -0.6 to 0.6
- reg_nodes: int32 [4, 8, 10, 256], P('grp', 'sub'), may hold values from 0 to 383
- site_nodes: int32 [4, 8, 35, 128], P('grp', 'sub'), may hold values from 0 to 1535
- reg_coefs: float32 [4, 8, 3, 3, 4, 256], P('grp', 'sub'), may hold values from -1.5 to 6, as said below
- site_coefs: float32 [4, 8, 3, 3, 24, 128], P('grp', 'sub'), may hold values from -1.5 to 6, as said below
- reg_table: float32 [12, 10], replicated, may hold values from -2 to 2
- site_table: float32 [72, 35], replicated, may hold values from -1 to 1
- reg_minv: float32 [4, 8, 384], P('grp', 'sub'), may hold values from 0.003 to 0.015
- site_minv: float32 [4, 8, 1536], P('grp', 'sub'), may hold values from 0.003 to 0.015
- reg_send: int32 [4, 8, 2, 128], P('grp', 'sub'), may hold values from 0 to 383
- reg_recv: int32 [4, 8, 2, 128], P('grp', 'sub'), may hold values from 0 to 383
- site_send: int32 [4, 8, 2, 128], P('grp', 'sub'), may hold values from 0 to 1535
- site_recv: int32 [4, 8, 2, 128], P('grp', 'sub'), may hold values from 0 to 1535
- slot_fill: int32 [4, 8, 4], P('grp', 'sub'), may hold values from 1 to 128, 384 in all within a row
- layer_src: int32 [4, 8, 128], P('grp', 'sub'), may hold values from 0 to 383
- layer_fill: int32 [4, 8], P('grp', 'sub'), may hold values from 64 to 128, as said below
- layer_dst: int32 [4, 8, 3, 128], P('grp', 'sub'), may hold values from 0 to 1535
- layer_stiff: float32 [4, 8, 3, 128], P('grp', 'sub'), may hold values from 0.5 to 2
Outputs:
- reg_final: float32 [4, 8, 3, 384], P('grp', 'sub')
- site_final: float32 [4, 8, 3, 1536], P('grp', 'sub')
Inputs may be any that keep to these rules, and one draw needn't show every extreme that they name: `slot_fill`: per partition the four entries count live slots toward the lower and higher neighbour, regional then site; they sum to 384. `layer_fill`: partition index 0 of every group fills all 128 slots. `reg_coefs`: each 3 x 3 tensor over the first two dimensions is symmetric positive definite. `site_coefs`: each 3 x 3 tensor over the first two dimensions is symmetric positive definite.
All inputs are finite; a program needn't handle non-finite values.
Results may differ from a plain program's by a relative error of at most 0.0003.
Values sent between devices are 32-bit elements; how exact they have to be, the bound alone decides.
No kernel may reach another device: no remote copies, remote signals or barrier semaphores. Data moves between devices by JAX's collectives and lax.ppermute only.
A program may use at most 64 MiB of HBM per device.

v0:
```python
import jax
import jax.numpy as jnp
from jax import lax
from jax.sharding import PartitionSpec as P

STEPS = 8
MB_STEPS = 2


PRECISE = lax.Precision.HIGHEST


def with_halo(value, sides, width):
    for axis, dim in sides:
        count, length = (lax.axis_size(axis), value.shape[dim])
        up = [(i, (i + 1) % count) for i in range(count - 1)]
        down = [(j, i) for i, j in up]
        last = lax.slice_in_dim(value, length - width, length, axis=dim)
        leading = lax.slice_in_dim(value, 0, width, axis=dim)
        before = lax.ppermute(last, axis, up)
        after = lax.ppermute(leading, axis, down)
        value = jnp.concatenate([before, value, after], axis=dim)
    return value


def shifted(block, axis, distance):
    devices = range(lax.axis_size(axis))
    route = [(i - distance, i) for i in devices if i - distance in devices]
    return lax.ppermute(block, axis, route)


def stiff_force(displaced, element_nodes, coef_block, deriv_table):
    quad_count = coef_block.shape[2]
    node_count = element_nodes.shape[0]
    elem_count = element_nodes.shape[1]
    flat_nodes = element_nodes.reshape(-1)
    gathered = jnp.take(displaced, flat_nodes, axis=1).reshape(3, node_count, elem_count)
    gradient = jnp.einsum("kp,cpe->cke", deriv_table, gathered, precision=PRECISE)
    pieces = [gradient[:, b * quad_count : (b + 1) * quad_count] for b in range(3)]
    flux_rows = [
        coef_block[a, 0][None] * pieces[0]
        + coef_block[a, 1][None] * pieces[1]
        + coef_block[a, 2][None] * pieces[2]
        for a in range(3)
    ]
    flux_terms = jnp.concatenate(flux_rows, axis=1)
    element_terms = jnp.einsum("kp,cke->cpe", deriv_table, flux_terms, precision=PRECISE)
    return -jnp.zeros_like(displaced).at[:, flat_nodes].add(element_terms.reshape(3, -1))


def pack_slots(forces, send_map, fill_pair):
    picked = jnp.take(forces, send_map, axis=1)
    live_slots = jnp.arange(send_map.shape[1], dtype=jnp.int32)[None, :] < fill_pair[:, None]
    return jnp.where(live_slots[:, None, :], jnp.transpose(picked, (1, 0, 2)), 0.0)


def take_slots(forces, recv_map, from_lower, from_upper):
    return forces.at[:, recv_map[0]].add(from_lower).at[:, recv_map[1]].add(from_upper)


def pack_layer(displaced, layer_src, layer_fill):
    picked = jnp.take(displaced, layer_src, axis=1)
    live_slots = jnp.arange(layer_src.shape[0], dtype=jnp.int32) < layer_fill
    return jnp.where(live_slots[None, :], picked, 0.0)


def add_layer(forces, layer_dst, layer_stiff, layer_block):
    for source in range(3):
        forces = forces.at[:, layer_dst[source]].add(
            layer_stiff[source][None, :] * layer_block[source]
        )
    return forces


def shards(
    reg_disp,
    reg_vel,
    site_disp,
    site_vel,
    reg_nodes,
    site_nodes,
    reg_coefs,
    site_coefs,
    reg_table,
    site_table,
    reg_minv,
    site_minv,
    reg_send,
    reg_recv,
    site_send,
    site_recv,
    slot_fill,
    layer_src,
    layer_fill,
    layer_dst,
    layer_stiff,
):
    group_count = lax.axis_size("grp")
    site_groups = group_count // 4
    reg_groups = 3 * site_groups
    grp_index = lax.axis_index("grp")
    is_site = grp_index >= reg_groups
    reg_now = reg_disp[0, 0]
    site_now = site_disp[0, 0]
    slot_counts = slot_fill[0, 0]
    blank_send = jnp.zeros((2, 3, reg_send.shape[-1]), jnp.float32)

    def advance(states, layer_block, reg_on, site_on):
        reg_pair, site_pair = states

        def reg_force():
            forces = stiff_force(reg_pair[1], reg_nodes[0, 0], reg_coefs[0, 0], reg_table)
            return (
                forces,
                jnp.zeros_like(site_pair[1]),
                pack_slots(forces, reg_send[0, 0], slot_counts[0:2]),
            )

        def site_force():
            forces = stiff_force(site_pair[1], site_nodes[0, 0], site_coefs[0, 0], site_table)
            return (
                jnp.zeros_like(reg_pair[1]),
                forces,
                pack_slots(forces, site_send[0, 0], slot_counts[2:4]),
            )

        def no_force():
            return (jnp.zeros_like(reg_pair[1]), jnp.zeros_like(site_pair[1]), blank_send)

        reg_total, site_total, outgoing = lax.cond(
            is_site, site_force if site_on else no_force, reg_force if reg_on else no_force
        )
        incoming = with_halo(outgoing, (("sub", 0),), 1)
        from_lower = incoming[0]
        from_upper = incoming[3]

        def reg_update():
            forces = take_slots(reg_total, reg_recv[0, 0], from_lower, from_upper)
            reg_next = 2.0 * reg_pair[1] - reg_pair[0] + reg_minv[0, 0][None, :] * forces
            return ((reg_pair[1], reg_next), site_pair)

        def site_update():
            forces = take_slots(site_total, site_recv[0, 0], from_lower, from_upper)
            forces = add_layer(forces, layer_dst[0, 0], layer_stiff[0, 0], layer_block)
            site_next = 2.0 * site_pair[1] - site_pair[0] + site_minv[0, 0][None, :] * forces
            return (reg_pair, (site_pair[1], site_next))

        def keep_states():
            return (reg_pair, site_pair)

        return lax.cond(
            is_site, site_update if site_on else keep_states, reg_update if reg_on else keep_states
        )

    states = ((reg_now - reg_vel[0, 0], reg_now), (site_now - site_vel[0, 0], site_now))
    batch_count = STEPS // MB_STEPS
    pending = None
    for batch_no in range(batch_count + 1):
        layer_packs = []
        for inner_step in range(MB_STEPS):
            layer_block = pending[:, inner_step] if batch_no > 0 else None
            states = advance(states, layer_block, batch_no < batch_count, batch_no > 0)
            if batch_no < batch_count:
                layer_packs.append(pack_layer(states[0][1], layer_src[0, 0], layer_fill[0, 0]))
        if batch_no < batch_count:
            layer_steps = jnp.stack(layer_packs)
            pending = jnp.stack(
                [shifted(layer_steps, "grp", (3 - source) * site_groups) for source in range(3)]
            )
    reg_final = jnp.where(is_site, 0.0, states[0][1])[None, None]
    site_final = jnp.where(is_site, states[1][1], 0.0)[None, None]
    return (reg_final, site_final)


def solution(mesh):
    return jax.shard_map(
        shards,
        mesh=mesh,
        in_specs=(
            P("grp", "sub", None, None),
            P("grp", "sub", None, None),
            P("grp", "sub", None, None),
            P("grp", "sub", None, None),
            P("grp", "sub", None, None),
            P("grp", "sub", None, None),
            P("grp", "sub", None, None, None, None),
            P("grp", "sub", None, None, None, None),
            P(),
            P(),
            P("grp", "sub", None),
            P("grp", "sub", None),
            P("grp", "sub", None, None),
            P("grp", "sub", None, None),
            P("grp", "sub", None, None),
            P("grp", "sub", None, None),
            P("grp", "sub", None),
            P("grp", "sub", None),
            P("grp", "sub"),
            P("grp", "sub", None, None),
            P("grp", "sub", None, None),
        ),
        out_specs=(P("grp", "sub", None, None), P("grp", "sub", None, None)),
        check_vma=False,
    )
```

profile of v0, /device:TPU:15, one launch (start us, length us, event | category | flops | bytes accessed | tf_op | source)
XLA Modules:
  0.0 590.9 jit_solution(15146022666100904936)
XLA Ops:
  24.6 47.2 %conditional.24 = (f32[3,384]{0,1:T(8,128)S(1)}, f32[3,1536]{1,0:T(4,128)S(1)}, f32[2,3,128]{1,2,0:T(8,128)}) conditional(s32[]{:T(128)} %convert_element_type.2, (s32[1,1,10,256]{3,1,2,0:T(1,128)S(1)}, f32[1,1,3,3,4,256]{5,4,3,2,1,0:T(4,128)S(1)}, f32[3,384]{0,1:T(8,128)S(1)}, f32[12,10]{1,0:T(8,128)S(1)}, s32[4]{0:T(128)S(1)}, ...), branch_computations={%region_14.18_spmd, %region_16.22_spmd} | conditional | flops 23513344 | bytes 1754184 | solution.py:130
  44.2 25.6 %scatter_custom_fusion.5 = f32[3,1536]{0,1:T(8,128)S(1)} fusion(s32[4480]{0:T(1024)S(1)} %fusion.289, f32[4480,3]{1,0:T(8,128)} %bitcast.1637, f32[]{:T(128)} %constant.72.clone), kind=kCustom, calls=%fused_computation.562 | custom fusion | flops 13440 | bytes 18944 | tf_op jit(solution)/shard_map/cond/branch_1_fun/scatter-add | solution.py:48
  85.3 12.6 %conditional.25 = (f32[3,384]{1,0:T(4,128)S(1)}, f32[3,384]{1,0:T(4,128)S(1)}, f32[3,1536]{0,1:T(8,128)S(1)}, f32[3,1536]{0,1:T(8,128)S(1)}, f32[3,384]{0,1:T(8,128)S(1)}) conditional(s32[]{:T(128)} %convert_element_type.2, (f32[3,384]{0,1:T(8,128)S(1)}, f32[3,384]{0,1:T(8,128)S(1)}, f32[1,1,384]{2,1,0:T(1,128)S(1)}, ...), branch_computations={%region_18.0_spmd, %region_21.32_spmd} | conditional | flops 23424 | bytes 712264 | solution.py:151
  98.8 47.2 %conditional.26 = (f32[3,384]{0,1:T(8,128)S(1)}, f32[3,1536]{1,0:T(4,128)S(1)}, f32[2,3,128]{1,2,0:T(8,128)}) conditional(s32[]{:T(128)} %convert_element_type.2, (s32[1,1,10,256]{3,1,2,0:T(1,128)S(1)}, f32[1,1,3,3,4,256]{5,4,3,2,1,0:T(4,128)S(1)}, f32[3,384]{1,0:T(4,128)S(1)}, f32[12,10]{1,0:T(8,128)S(1)}, s32[4]{0:T(128)}, ...), branch_computations={%region_27.34_spmd, %region_29.36_spmd} | conditional | flops 23513344 | bytes 1705096 | solution.py:130
  118.4 25.6 %scatter_custom_fusion.65 = f32[3,1536]{0,1:T(8,128)S(1)} fusion(s32[4480]{0:T(1024)S(1)} %fusion.315, f32[4480,3]{1,0:T(8,128)} %bitcast.1638, f32[]{:T(128)} %constant.104.clone), kind=kCustom, calls=%fused_computation.636 | custom fusion | flops 13440 | bytes 18944 | tf_op jit(solution)/shard_map/cond/branch_1_fun/scatter-add | solution.py:48
  155.6 11.4 %conditional.27 = (f32[3,384]{1,0:T(4,128)S(1)}, f32[3,384]{1,0:T(4,128)S(1)}, f32[3,1536]{0,1:T(8,128)S(1)}, f32[3,1536]{0,1:T(8,128)S(1)}, f32[3,384]{0,1:T(8,128)S(1)}) conditional(s32[]{:T(128)} %convert_element_type.2, (f32[3,384]{1,0:T(4,128)S(1)}, f32[3,384]{1,0:T(4,128)S(1)}, f32[1,1,384]{2,1,0:T(1,128)S(1)}, s32[1,1,2,128]{3,2,1,0:T(2,128)}, ...), branch_computations={%region_31.39_spmd, %region_34.45_spmd} | conditional | flops 23424 | bytes 739940 | solution.py:151
  173.4 44.3 %conditional.28 = (f32[3,384]{0,1:T(8,128)S(1)}, f32[3,1536]{1,0:T(4,128)S(1)}, f32[2,3,128]{1,2,0:T(8,128)}) conditional(s32[]{:T(128)} %convert_element_type.2, (s32[1,1,10,256]{3,1,2,0:T(1,128)S(1)}, f32[1,1,3,3,4,256]{5,4,3,2,1,0:T(4,128)S(1)}, f32[3,384]{1,0:T(4,128)S(1)}, f32[12,10]{1,0:T(8,128)S(1)}, s32[4]{0:T(128)}, ...), branch_computations={%region_40.47_spmd, %region_42.49_spmd} | conditional | flops 23513344 | bytes 1606736 | solution.py:130
  190.0 25.6 %scatter_custom_fusion.66 = f32[3,1536]{0,1:T(8,128)S(1)} fusion(s32[4480]{0:T(1024)S(1)} %fusion.341, f32[4480,3]{1,0:T(8,128)} %bitcast.1639, f32[]{:T(128)} %constant.128.clone), kind=kCustom, calls=%fused_computation.710 | custom fusion | flops 13440 | bytes 18944 | tf_op jit(solution)/shard_map/cond/branch_1_fun/scatter-add | solution.py:48
  227.4 11.3 %conditional.29 = (f32[3,384]{1,0:T(4,128)S(1)}, f32[3,384]{1,0:T(4,128)S(1)}, f32[3,1536]{0,1:T(8,128)S(1)}, f32[3,1536]{0,1:T(8,128)S(1)}, f32[3,384]{0,1:T(8,128)S(1)}) conditional(s32[]{:T(128)} %convert_element_type.2, (f32[3,384]{1,0:T(4,128)S(1)}, f32[3,384]{1,0:T(4,128)S(1)}, f32[1,1,384]{2,1,0:T(1,128)S(1)}, s32[1,1,2,128]{3,2,1,0:T(2,128)}, ...), branch_computations={%region_44.52_spmd, %region_47.58_spmd} | conditional | flops 23424 | bytes 624284 | solution.py:151
  239.7 44.3 %conditional.30 = (f32[3,384]{0,1:T(8,128)S(1)}, f32[3,1536]{1,0:T(4,128)S(1)}, f32[2,3,128]{1,2,0:T(8,128)}) conditional(s32[]{:T(128)} %convert_element_type.2, (s32[1,1,10,256]{3,1,2,0:T(1,128)S(1)}, f32[1,1,3,3,4,256]{5,4,3,2,1,0:T(4,128)S(1)}, f32[3,384]{1,0:T(4,128)S(1)}, f32[12,10]{1,0:T(8,128)S(1)}, s32[4]{0:T(128)}, ...), branch_computations={%region_53.60_spmd, %region_55.62_spmd} | conditional | flops 23513344 | bytes 1606736 | solution.py:130
  256.3 25.6 %scatter_custom_fusion.67 = f32[3,1536]{0,1:T(8,128)S(1)} fusion(s32[4480]{0:T(1024)S(1)} %fusion.367, f32[4480,3]{1,0:T(8,128)} %bitcast.1640, f32[]{:T(128)} %constant.152.clone), kind=kCustom, calls=%fused_computation.784 | custom fusion | flops 13440 | bytes 18944 | tf_op jit(solution)/shard_map/cond/branch_1_fun/scatter-add | solution.py:48
  292.4 11.4 %conditional.31 = (f32[3,384]{1,0:T(4,128)S(1)}, f32[3,384]{1,0:T(4,128)S(1)}, f32[3,1536]{0,1:T(8,128)S(1)}, f32[3,1536]{0,1:T(8,128)S(1)}, f32[3,384]{0,1:T(8,128)S(1)}) conditional(s32[]{:T(128)} %convert_element_type.2, (f32[3,384]{1,0:T(4,128)S(1)}, f32[3,384]{1,0:T(4,128)S(1)}, f32[1,1,384]{2,1,0:T(1,128)S(1)}, s32[1,1,2,128]{3,2,1,0:T(2,128)}, ...), branch_computations={%region_57.65_spmd, %region_60.71_spmd} | conditional | flops 23424 | bytes 739940 | solution.py:151
  310.2 44.3 %conditional.32 = (f32[3,384]{0,1:T(8,128)S(1)}, f32[3,1536]{1,0:T(4,128)S(1)}, f32[2,3,128]{1,2,0:T(8,128)}) conditional(s32[]{:T(128)} %convert_element_type.2, (s32[1,1,10,256]{3,1,2,0:T(1,128)S(1)}, f32[1,1,3,3,4,256]{5,4,3,2,1,0:T(4,128)S(1)}, f32[3,384]{1,0:T(4,128)S(1)}, f32[12,10]{1,0:T(8,128)S(1)}, s32[4]{0:T(128)}, ...), branch_computations={%region_66.73_spmd, %region_68.75_spmd} | conditional | flops 23513344 | bytes 1606736 | solution.py:130
  326.8 25.6 %scatter_custom_fusion.68 = f32[3,1536]{0,1:T(8,128)S(1)} fusion(s32[4480]{0:T(1024)S(1)} %fusion.393, f32[4480,3]{1,0:T(8,128)} %bitcast.1641, f32[]{:T(128)} %constant.176.clone), kind=kCustom, calls=%fused_computation.858 | custom fusion | flops 13440 | bytes 18944 | tf_op jit(solution)/shard_map/cond/branch_1_fun/scatter-add | solution.py:48
  364.6 10.7 %conditional.33 = (f32[3,384]{1,0:T(4,128)S(1)}, f32[3,384]{1,0:T(4,128)S(1)}, f32[3,1536]{0,1:T(8,128)S(1)}, f32[3,1536]{0,1:T(8,128)S(1)}, f32[3,384]{0,1:T(8,128)S(1)}) conditional(s32[]{:T(128)} %convert_element_type.2, (f32[3,384]{1,0:T(4,128)S(1)}, f32[3,384]{1,0:T(4,128)S(1)}, f32[1,1,384]{2,1,0:T(1,128)S(1)}, s32[1,1,2,128]{3,2,1,0:T(2,128)}, ...), branch_computations={%region_70.78_spmd, %region_73.84_spmd} | conditional | flops 23424 | bytes 739940 | solution.py:151
  376.2 44.3 %conditional.34 = (f32[3,384]{0,1:T(8,128)S(1)}, f32[3,1536]{1,0:T(4,128)S(1)}, f32[2,3,128]{1,2,0:T(8,128)}) conditional(s32[]{:T(128)} %convert_element_type.2, (s32[1,1,10,256]{3,1,2,0:T(1,128)S(1)}, f32[1,1,3,3,4,256]{5,4,3,2,1,0:T(4,128)S(1)}, f32[3,384]{1,0:T(4,128)S(1)}, f32[12,10]{1,0:T(8,128)S(1)}, s32[4]{0:T(128)}, ...), branch_computations={%region_79.86_spmd, %region_81.88_spmd} | conditional | flops 23513344 | bytes 1606736 | solution.py:130
  392.9 25.6 %scatter_custom_fusion.69 = f32[3,1536]{0,1:T(8,128)S(1)} fusion(s32[4480]{0:T(1024)S(1)} %fusion.419, f32[4480,3]{1,0:T(8,128)} %bitcast.1642, f32[]{:T(128)} %constant.200.clone), kind=kCustom, calls=%fused_computation.932 | custom fusion | flops 13440 | bytes 18944 | tf_op jit(solution)/shard_map/cond/branch_1_fun/scatter-add | solution.py:48
  429.0 10.5 %conditional.35 = (f32[3,384]{1,0:T(4,128)S(1)}, f32[3,1536]{0,1:T(8,128)S(1)}, f32[3,1536]{0,1:T(8,128)S(1)}, f32[3,384]{0,1:T(8,128)S(1)}) conditional(s32[]{:T(128)} %convert_element_type.2, (f32[3,384]{1,0:T(4,128)S(1)}, f32[3,384]{1,0:T(4,128)S(1)}, f32[1,1,384]{2,1,0:T(1,128)S(1)}, s32[1,1,2,128]{3,2,1,0:T(2,128)}, f32[3,384]{0,1:T(8,128)S(1)}, ...), branch_computations={%region_83.91_spmd, %region_86.97_spmd} | conditional | flops 23424 | bytes 739932 | solution.py:151
  445.9 45.4 %conditional.36 = (f32[3,1536]{0,1:T(8,128)}, f32[2,3,128]{1,2,0:T(8,128)S(1)}) conditional(s32[]{:T(128)} %convert_element_type.2, () %tuple.204, (s32[1,1,35,128]{3,1,2,0:T(1,128)S(1)}, f32[1,1,3,3,24,128]{5,4,3,2,1,0:T(8,128)S(1)}, f32[3,1536]{0,1:T(8,128)S(1)}, f32[72,35]{0,1:T(8,128)S(1)}, s32[4]{0:T(128)S(1)}, ...), branch_computations={%region_92.98_spmd, %region_93.100_spmd} | conditional | flops 23513344 | bytes 1565160 | solution.py:130
  462.5 25.6 %scatter_custom_fusion.70 = f32[3,1536]{0,1:T(8,128)S(1)} fusion(s32[4480]{0:T(1024)S(1)} %fusion.432, f32[4480,3]{1,0:T(8,128)} %bitcast.1635, f32[]{:T(128)} %constant.209.clone), kind=kCustom, calls=%fused_computation.969 | custom fusion | flops 13440 | bytes 18944 | tf_op jit(solution)/shard_map/cond/branch_1_fun/scatter-add | solution.py:48
  499.2 17.9 %conditional.37 = (f32[3,1536]{0,1:T(8,128)S(1)}, f32[3,1536]{0,1:T(8,128)S(1)}) conditional(s32[]{:T(128)} %convert_element_type.2, (f32[3,1536]{0,1:T(8,128)}, f32[3,1536]{0,1:T(8,128)S(1)}) %tuple.663, (f32[3,1536]{0,1:T(8,128)S(1)}, f32[3,1536]{0,1:T(8,128)}, f32[1,1,1536]{2,1,0:T(1,128)S(1)}, s32[1,1,2,128]{3,2,1,0:T(2,128)S(1)}, ...), branch_computations={%region_95.101_spmd.clone, %region_96.0_spmd.clone} | conditional | flops 23424 | bytes 656944 | solution.py:151
  518.0 46.0 %conditional.38 = (f32[3,1536]{0,1:T(8,128)}, f32[2,3,128]{1,2,0:T(8,128)S(1)}) conditional(s32[]{:T(128)} %convert_element_type.2, () %tuple.207, (s32[1,1,35,128]{3,1,2,0:T(1,128)S(1)}, f32[1,1,3,3,24,128]{5,4,3,2,1,0:T(8,128)S(1)}, f32[3,1536]{0,1:T(8,128)S(1)}, f32[72,35]{0,1:T(8,128)S(1)}, s32[4]{0:T(128)S(1)}, ...), branch_computations={%region_102.108_spmd, %region_103.110_spmd} | conditional | flops 23513344 | bytes 1565160 | solution.py:130
  534.9 25.6 %scatter_custom_fusion.71 = f32[3,1536]{0,1:T(8,128)S(1)} fusion(s32[4480]{0:T(1024)S(1)} %fusion.445, f32[4480,3]{1,0:T(8,128)} %bitcast.1636, f32[]{:T(128)} %constant.223.clone), kind=kCustom, calls=%fused_computation.1006 | custom fusion | flops 13440 | bytes 18944 | tf_op jit(solution)/shard_map/cond/branch_1_fun/scatter-add | solution.py:48
  571.5 18.2 %conditional.39 = (f32[3,1536]{1,0:T(4,128)S(1)}) conditional(s32[]{:T(128)} %convert_element_type.2, f32[3,1536]{0,1:T(8,128)S(1)} %get-tuple-element.900, (f32[3,1536]{0,1:T(8,128)S(1)}, f32[3,1536]{0,1:T(8,128)}, f32[1,1,1536]{2,1,0:T(1,128)S(1)}, s32[1,1,2,128]{3,2,1,0:T(2,128)S(1)}, f32[3,1536]{0,1:T(8,128)}, ...), branch_computations={%region_105.111_spmd, %region_106.0_spmd} | conditional | flops 23424 | bytes 656936 | solution.py:151
  (542 shorter events, 377.3 us)
Async XLA Ops:
  1.7 7.2 %collective-permute-start = (f32[1,3,128]{1,2,0:T(8,128)S(1)}, f32[1,3,128]{1,2,0:T(8,128)S(1)}, u32[]{:S(2)}, u32[]{:S(2)}) collective-permute-start(f32[1,3,128]{1,2,0:T(8,128)S(1)} %get-tuple-element.2092), channel_id=1, source_target_pairs={{0,1},{1,2},{2,3},{3,4},{4,5},{5,6},{6,7},{8,9},{9,10},{10,11},{11... | collective-permute-start | bytes 4616 | tf_op jit(solution)/shard_map/ppermute | solution.py:20
  11.3 6.7 %collective-permute-start.2 = (f32[1,3,128]{1,2,0:T(8,128)S(1)}, f32[1,3,128]{1,2,0:T(8,128)S(1)}, u32[]{:S(2)}, u32[]{:S(2)}) collective-permute-start(f32[1,3,128]{1,2,0:T(8,128)S(1)} %get-tuple-element.2090), channel_id=1, source_target_pairs={{0,1},{1,2},{2,3},{3,4},{4,5},{5,6},{6,7},{8,9},{9,10},{10,11},{11... | collective-permute-start | bytes 4616 | tf_op jit(solution)/shard_map/ppermute | solution.py:20
  13.3 5.6 collective-permute-start.3
  20.7 60.1 %collective-permute-start.6 = (f32[2,3,128]{2,0,1:T(2,128)}, f32[2,3,128]{2,0,1:T(2,128)}, u32[]{:S(2)}, u32[]{:S(2)}) collective-permute-start(f32[2,3,128]{2,0,1:T(2,128)} %pad_maximum_fusion.4), channel_id=1, source_target_pairs={{0,24},{1,25},{2,26},{3,27},{4,28},{5,29},{6,30},{7,31}} | collective-permute-start | bytes 9224 | tf_op jit(solution)/shard_map/ppermute | solution.py:29
  22.0 60.1 %collective-permute-start.7 = (f32[2,3,128]{2,0,1:T(2,128)}, f32[2,3,128]{2,0,1:T(2,128)}, u32[]{:S(2)}, u32[]{:S(2)}) collective-permute-start(f32[2,3,128]{2,0,1:T(2,128)} %pad_maximum_fusion.4), channel_id=1, source_target_pairs={{0,16},{8,24},{1,17},{9,25},{2,18},{10,26},{3,19},{11,27},{4,20},{... | collective-permute-start | bytes 9224 | tf_op jit(solution)/shard_map/ppermute | solution.py:29
  23.3 60.7 %collective-permute-start.8 = (f32[2,3,128]{2,0,1:T(2,128)}, f32[2,3,128]{2,0,1:T(2,128)}, u32[]{:S(2)}, u32[]{:S(2)}) collective-permute-start(f32[2,3,128]{2,0,1:T(2,128)} %pad_maximum_fusion.4), channel_id=1, source_target_pairs={{0,8},{8,16},{16,24},{1,9},{9,17},{17,25},{2,10},{10,18},{18,26},{... | collective-permute-start | bytes 9224 | tf_op jit(solution)/shard_map/ppermute | solution.py:29
  75.1 5.6 collective-permute-start.5
  146.9 6.4 %collective-permute-start.9 = (f32[1,3,128]{1,2,0:T(8,128)S(1)}, f32[1,3,128]{1,2,0:T(8,128)S(1)}, u32[]{:S(2)}, u32[]{:S(2)}) collective-permute-start(f32[1,3,128]{1,2,0:T(8,128)S(1)} %get-tuple-element.2086), channel_id=1, source_target_pairs={{0,1},{1,2},{2,3},{3,4},{4,5},{5,6},{6,7},{8,9},{9,10},{10,11},{11... | collective-permute-start | bytes 4616 | tf_op jit(solution)/shard_map/ppermute | solution.py:20
  150.0 5.6 collective-permute-start.10
  169.5 56.6 %collective-permute-start.13 = (f32[2,3,128]{2,0,1:T(2,128)}, f32[2,3,128]{2,0,1:T(2,128)}, u32[]{:S(2)}, u32[]{:S(2)}) collective-permute-start(f32[2,3,128]{2,0,1:T(2,128)} %pad_maximum_fusion.5), channel_id=1, source_target_pairs={{0,24},{1,25},{2,26},{3,27},{4,28},{5,29},{6,30},{7,31}} | collective-permute-start | bytes 9224 | tf_op jit(solution)/shard_map/ppermute | solution.py:29
  170.8 55.4 %collective-permute-start.14 = (f32[2,3,128]{2,0,1:T(2,128)}, f32[2,3,128]{2,0,1:T(2,128)}, u32[]{:S(2)}, u32[]{:S(2)}) collective-permute-start(f32[2,3,128]{2,0,1:T(2,128)} %pad_maximum_fusion.5), channel_id=1, source_target_pairs={{0,16},{8,24},{1,17},{9,25},{2,18},{10,26},{3,19},{11,27},{4,20},{... | collective-permute-start | bytes 9224 | tf_op jit(solution)/shard_map/ppermute | solution.py:29
  172.1 54.1 %collective-permute-start.15 = (f32[2,3,128]{2,0,1:T(2,128)}, f32[2,3,128]{2,0,1:T(2,128)}, u32[]{:S(2)}, u32[]{:S(2)}) collective-permute-start(f32[2,3,128]{2,0,1:T(2,128)} %pad_maximum_fusion.5), channel_id=1, source_target_pairs={{0,8},{8,16},{16,24},{1,9},{9,17},{17,25},{2,10},{10,18},{18,26},{... | collective-permute-start | bytes 9224 | tf_op jit(solution)/shard_map/ppermute | solution.py:29
  220.6 5.6 collective-permute-start.12
  284.9 6.6 %collective-permute-start.16 = (f32[1,3,128]{1,2,0:T(8,128)S(1)}, f32[1,3,128]{1,2,0:T(8,128)S(1)}, u32[]{:S(2)}, u32[]{:S(2)}) collective-permute-start(f32[1,3,128]{1,2,0:T(8,128)S(1)} %get-tuple-element.2082), channel_id=1, source_target_pairs={{0,1},{1,2},{2,3},{3,4},{4,5},{5,6},{6,7},{8,9},{9,10},{10,11},{11... | collective-permute-start | bytes 4616 | tf_op jit(solution)/shard_map/ppermute | solution.py:20
  286.8 5.6 collective-permute-start.17
  306.3 57.0 %collective-permute-start.20 = (f32[2,3,128]{2,0,1:T(2,128)}, f32[2,3,128]{2,0,1:T(2,128)}, u32[]{:S(2)}, u32[]{:S(2)}) collective-permute-start(f32[2,3,128]{2,0,1:T(2,128)} %pad_maximum_fusion.6), channel_id=1, source_target_pairs={{0,24},{1,25},{2,26},{3,27},{4,28},{5,29},{6,30},{7,31}} | collective-permute-start | bytes 9224 | tf_op jit(solution)/shard_map/ppermute | solution.py:29
  307.6 55.7 %collective-permute-start.21 = (f32[2,3,128]{2,0,1:T(2,128)}, f32[2,3,128]{2,0,1:T(2,128)}, u32[]{:S(2)}, u32[]{:S(2)}) collective-permute-start(f32[2,3,128]{2,0,1:T(2,128)} %pad_maximum_fusion.6), channel_id=1, source_target_pairs={{0,16},{8,24},{1,17},{9,25},{2,18},{10,26},{3,19},{11,27},{4,20},{... | collective-permute-start | bytes 9224 | tf_op jit(solution)/shard_map/ppermute | solution.py:29
  308.9 54.4 %collective-permute-start.22 = (f32[2,3,128]{2,0,1:T(2,128)}, f32[2,3,128]{2,0,1:T(2,128)}, u32[]{:S(2)}, u32[]{:S(2)}) collective-permute-start(f32[2,3,128]{2,0,1:T(2,128)} %pad_maximum_fusion.6), channel_id=1, source_target_pairs={{0,8},{8,16},{16,24},{1,9},{9,17},{17,25},{2,10},{10,18},{18,26},{... | collective-permute-start | bytes 9224 | tf_op jit(solution)/shard_map/ppermute | solution.py:29
  357.7 5.6 collective-permute-start.19
  421.5 6.6 %collective-permute-start.23 = (f32[1,3,128]{1,2,0:T(8,128)S(1)}, f32[1,3,128]{1,2,0:T(8,128)S(1)}, u32[]{:S(2)}, u32[]{:S(2)}) collective-permute-start(f32[1,3,128]{1,2,0:T(8,128)S(1)} %get-tuple-element.2078), channel_id=1, source_target_pairs={{0,1},{1,2},{2,3},{3,4},{4,5},{5,6},{6,7},{8,9},{9,10},{10,11},{11... | collective-permute-start | bytes 4616 | tf_op jit(solution)/shard_map/ppermute | solution.py:20
  442.0 53.7 %collective-permute-start.27 = (f32[2,3,128]{2,0,1:T(2,128)}, f32[2,3,128]{2,0,1:T(2,128)S(1)}, u32[]{:S(2)}, u32[]{:S(2)}) collective-permute-start(f32[2,3,128]{2,0,1:T(2,128)} %pad_maximum_fusion.7), channel_id=1, source_target_pairs={{0,24},{1,25},{2,26},{3,27},{4,28},{5,29},{6,30},{7,31}} | collective-permute-start | bytes 9224 | tf_op jit(solution)/shard_map/ppermute | solution.py:29
  443.3 52.4 %collective-permute-start.28 = (f32[2,3,128]{2,0,1:T(2,128)}, f32[2,3,128]{2,0,1:T(2,128)}, u32[]{:S(2)}, u32[]{:S(2)}) collective-permute-start(f32[2,3,128]{2,0,1:T(2,128)} %pad_maximum_fusion.7), channel_id=1, source_target_pairs={{0,16},{8,24},{1,17},{9,25},{2,18},{10,26},{3,19},{11,27},{4,20},{... | collective-permute-start | bytes 9224 | tf_op jit(solution)/shard_map/ppermute | solution.py:29
  444.6 51.1 %collective-permute-start.29 = (f32[2,3,128]{2,0,1:T(2,128)}, f32[2,3,128]{2,0,1:T(2,128)}, u32[]{:S(2)}, u32[]{:S(2)}) collective-permute-start(f32[2,3,128]{2,0,1:T(2,128)} %pad_maximum_fusion.7), channel_id=1, source_target_pairs={{0,8},{8,16},{16,24},{1,9},{9,17},{17,25},{2,10},{10,18},{18,26},{... | collective-permute-start | bytes 9224 | tf_op jit(solution)/shard_map/ppermute | solution.py:29
  493.6 5.6 collective-permute-start.26
  (72 other events, 664.0 us)
where the time goes:
time: 603 us; the launch traced here: 591 us
  other arithmetic  351 us (58%)
  local copies, waits for them, and re-layouts  139 us (23%)
  starting transfers between devices  60.9 us (10%)
  waiting for transfers between devices  24.9 us (4%)
  matrix products  6.04 us (1%)
    scatter-add x8, other arithmetic, stiff_force(): jnp.zeros_like(displaced).at[:, flat_nodes]  205 us
    gather x8, local copies, waits for them, and re-layouts, stiff_force(): jnp.take(displaced, flat_nodes, axis=1).reshape(3, node_count, elem_count)  73.9 us
    scatter-add x24, other arithmetic, add_layer(): forces.at[:, layer_dst[source]]  48.8 us
    scatter-add x16, other arithmetic, take_slots(): forces.at[:, recv_map[0]].add(from_lower).at[:, recv_map[1]].add(from_upper)  34 us
    select_n x16, other arithmetic, stiff_force(): jnp.take(displaced, flat_nodes, axis=1).reshape(3, node_count, elem_count)  30.3 us
    ppermute x10, starting transfers between devices, with_halo(): before = lax.ppermute(last, axis, up)  23.4 us
    ppermute x10, starting transfers between devices, with_halo(): after = lax.ppermute(leading, axis, down)  22.1 us
    ppermute x10, waiting for transfers between devices, with_halo(): after = lax.ppermute(leading, axis, down)  21.6 us
  transfers between devices with their start and end apart: 32, of which 13 were waited for; matrix products, arithmetic and copies ran while one was open for 33% of the time, Pallas kernels for 0%

commit v1 on v0

v1 whole, which is shorter than its diff:
```python
import functools

import jax
import jax.numpy as jnp
from jax import lax
from jax.experimental import pallas as pl
from jax.experimental.pallas import tpu as pltpu
from jax.sharding import PartitionSpec as P

STEPS = 8
UNROLL = 4
LANES = 128
F32 = jnp.float32
BF16 = jnp.bfloat16
PAIRS = ((0, 0), (0, 1), (0, 2), (1, 1), (1, 2), (2, 2))
PAIR_OF = {**{ab: i for i, ab in enumerate(PAIRS)}, **{ab[::-1]: i for i, ab in enumerate(PAIRS)}}


def up_to(value, unit):
    return -(-value // unit) * unit


class Kind:
    def __init__(self, nodes, coefs, disp, slots, sources):
        self.points, self.elems = nodes.shape[-2:]
        self.quads = coefs.shape[-2]
        self.count = disp.shape[-1]
        self.blocks = self.count // LANES
        self.cuts = self.elems // LANES
        self.points_pad = up_to(self.points, 8)
        self.quads_pad = up_to(self.quads, 8)
        self.blocks_pad = up_to(self.blocks, 2)
        self.depth_in = up_to(3 * self.points_pad, 16)
        self.depth_out = up_to(9 * self.quads_pad, 16)
        self.chunks = self.points * self.cuts
        self.sources = sources
        self.tiles = up_to(self.chunks, 4) // 4
        self.extra = 2 + sources
        self.extra_tiles = up_to(self.extra, 4) // 4
        self.slots = slots
        row = 0
        for name, rows in (
            ("coefs", 6 * self.quads * self.cuts),
            ("nodes", self.points * self.cuts),
            ("disp", 3 * self.blocks),
            ("vel", 3 * self.blocks),
            ("minv", self.blocks),
            ("send", 2),
            ("recv", 2),
            ("layer", 2 * sources if sources else 1),
        ):
            setattr(self, "at_" + name, row)
            row += rows
        self.rows = up_to(row, 8)


def pack_kind(kind, out, disp, vel, nodes, coefs, minv, send, recv, fill, layer):
    for pair, (a, b) in enumerate(PAIRS):
        for cut in range(kind.cuts):
            at = kind.at_coefs + (pair * kind.cuts + cut) * kind.quads
            out[at : at + kind.quads, :] = coefs[0, 0, a, b, :, cut * LANES : (cut + 1) * LANES]
    for cut in range(kind.cuts):
        at = kind.at_nodes + cut * kind.points
        out[at : at + kind.points, :] = nodes[0, 0, :, cut * LANES : (cut + 1) * LANES].astype(F32)
    for block in range(kind.blocks):
        lanes = slice(block * LANES, (block + 1) * LANES)
        out[kind.at_disp + 3 * block : kind.at_disp + 3 * block + 3, :] = disp[0, 0, :, lanes]
        out[kind.at_vel + 3 * block : kind.at_vel + 3 * block + 3, :] = vel[0, 0, :, lanes]
        out[kind.at_minv + block : kind.at_minv + block + 1, :] = minv[0, 0:1, lanes]
    lane = lax.broadcasted_iota(jnp.int32, (1, LANES), 1)
    for side in range(2):
        live = lane < fill[side]
        row = send[0, 0, side : side + 1, :]
        out[kind.at_send + side : kind.at_send + side + 1, :] = jnp.where(live, row, -1).astype(F32)
    out[kind.at_recv : kind.at_recv + 2, :] = recv[0, 0].astype(F32)
    if kind.sources:
        layer_dst, layer_stiff = layer
        m = kind.sources
        out[kind.at_layer : kind.at_layer + m, :] = layer_dst[0, 0].astype(F32)
        out[kind.at_layer + m : kind.at_layer + 2 * m, :] = layer_stiff[0, 0]
    else:
        layer_src, layer_fill = layer
        live = lane < layer_fill
        row = layer_src[0, 0:1, :]
        out[kind.at_layer : kind.at_layer + 1, :] = jnp.where(live, row, -1).astype(F32)


def split_index(value):
    index = value.astype(jnp.int32)
    return index & (LANES - 1), index >> 7


def high_part(value):
    return value.astype(BF16).astype(F32)


def simulate(kind, width, unroll, buf, lhs_in, lhs_out, layers, emit, s):
    points, cuts, blocks = kind.points, kind.cuts, kind.blocks
    quads_pad = kind.quads_pad
    half_rows = 8 * kind.blocks_pad
    row8 = lax.broadcasted_iota(jnp.int32, (8, LANES), 0)
    low_half = row8 < 4
    row16 = lax.broadcasted_iota(jnp.int32, (16, LANES), 0)
    block_ids = [
        jnp.where(row16 < 8, 2 * j, 2 * j + 1).astype(F32).astype(BF16)
        for j in range(kind.blocks_pad // 2)
    ]
    zero16 = jnp.zeros((16, LANES), BF16)
    zero8 = jnp.zeros((8, LANES), F32)
    lane_ids = lax.broadcasted_iota(jnp.int32, (LANES, LANES), 1)
    main_rows = kind.tiles * 256

    def onehot(q, chunk_no, base_row, columns, at):
        hit = columns[:, at : at + 1] == lane_ids
        tile, half, part = chunk_no // 4, (chunk_no // 2) % 2, chunk_no % 2
        rows = pl.ds(base_row + tile * 256 + part * LANES, LANES)
        s.onehot[q, rows, half * LANES : (half + 1) * LANES] = jnp.where(hit, 1.0, 0.0).astype(BF16)

    def hold_block(q, chunk_no, hi_row):
        wide = jnp.broadcast_to(hi_row.astype(F32), (16, LANES))
        s.block_of[q, chunk_no] = wide.astype(BF16)

    def columns_of(rows):
        count = rows.shape[0]
        if count < LANES:
            rows = jnp.concatenate([rows, jnp.zeros((LANES - count, LANES), F32)], axis=0)
        return jnp.transpose(rows).astype(jnp.int32)

    def setup(q, _):
        for pair in range(6):
            for cut in range(cuts):
                at = kind.at_coefs + (pair * cuts + cut) * kind.quads
                lanes = slice(cut * LANES, (cut + 1) * LANES)
                if kind.quads_pad > kind.quads:
                    s.coefs[q, pair, :, lanes] = jnp.zeros((quads_pad, LANES), F32)
                s.coefs[q, pair, 0 : kind.quads, lanes] = buf[q, at : at + kind.quads, :]
        for cut in range(cuts):
            at = kind.at_nodes + cut * points
            value = buf[q, at : at + points, :]
            lo, hi = split_index(value)
            if kind.points_pad > points:
                s.lo[q, cut] = jnp.zeros((kind.points_pad, LANES), jnp.int32)
                s.hi[q, cut] = jnp.zeros((kind.points_pad, LANES), jnp.int32)
            s.lo[q, cut, 0:points, :] = lo
            s.hi[q, cut, 0:points, :] = hi
            columns = columns_of(lo.astype(F32))
            for p in range(points):
                onehot(q, cut * points + p, 0, columns, p)
                hold_block(q, cut * points + p, hi[p : p + 1, :])
        for chunk in range(kind.chunks, 4 * kind.tiles):
            columns = jnp.zeros((LANES, 1), jnp.int32)
            onehot(q, chunk, 0, columns, 0)
            hold_block(q, chunk, jnp.zeros((1, LANES), jnp.int32))
        extra = [buf[q, kind.at_recv : kind.at_recv + 2, :]]
        if kind.sources:
            extra.append(buf[q, kind.at_layer : kind.at_layer + kind.sources, :])
        extra.append(jnp.zeros((4 * kind.extra_tiles - kind.extra, LANES), F32))
        lo, hi = split_index(jnp.concatenate([e for e in extra if e.shape[0]], axis=0))
        columns = columns_of(lo.astype(F32))
        for chunk in range(4 * kind.extra_tiles):
            onehot(q, chunk, main_rows, columns, chunk)
            hold_block(q, 4 * kind.tiles + chunk, hi[chunk : chunk + 1, :])
        send_rows = [
            jnp.broadcast_to(buf[q, kind.at_send + side : kind.at_send + side + 1, :], (4, LANES))
            for side in range(2)
        ]
        s.send_lo[q], s.send_hi[q] = split_index(jnp.concatenate(send_rows, axis=0))
        if not kind.sources:
            row = buf[q, kind.at_layer : kind.at_layer + 1, :]
            s.layer_lo[q], s.layer_hi[q] = split_index(jnp.broadcast_to(row, (8, LANES)))
        for block in range(blocks):
            at = kind.at_disp + 3 * block
            now = buf[q, at : at + 3, :]
            at = kind.at_vel + 3 * block
            before = now - buf[q, at : at + 3, :]
            for ref, value in ((s.now, now), (s.before, before)):
                ref[q, block] = zero8
                ref[q, block, 0:3, :] = value
                ref[q, block, 4:7, :] = value
        return 0

    lax.fori_loop(0, width, setup, 0)
    for lane in range(unroll):
        s.parts[lane] = jnp.zeros(s.parts.shape[1:], F32)
        s.spread[lane] = jnp.zeros(s.spread.shape[1:], BF16)
        s.spread_extra[lane] = jnp.zeros(s.spread_extra.shape[1:], BF16)
    s.sends[0] = zero8
    s.sends[width + 1] = zero8

    def place(spread, lane, q, chunk_no, block_at, value8):
        doubled = jnp.concatenate([value8, value8], axis=0).astype(BF16)
        held = s.block_of[q, block_at]
        tile, half, part = chunk_no // 4, (chunk_no // 2) % 2, chunk_no % 2
        lanes = slice(tile * 256 + part * LANES, tile * 256 + (part + 1) * LANES)
        for j, ids in enumerate(block_ids):
            at = half * half_rows + 16 * j
            spread[lane, at : at + 16, lanes] = jnp.where(held == ids, doubled, zero16)

    def fold(total, block):
        rows = slice(block * 8, block * 8 + 8)
        other = slice(half_rows + block * 8, half_rows + block * 8 + 8)
        value = total[rows, 0:LANES] + total[other, LANES : 2 * LANES]
        return value + pltpu.roll(value, 4, 0)

    def pick(source, q, lo, hi):
        value = zero8
        for block in range(blocks):
            found = jnp.take_along_axis(source(block), lo, axis=1, mode="promise_in_bounds")
            value = jnp.where(hi == block, found, value)
        return value

    def force(q, lane):
        stacked = []
        picked = {}
        for cut in range(cuts):
            lo = s.lo[q, cut]
            hi = s.hi[q, cut]
            values = [jnp.zeros((kind.points_pad, LANES), F32)] * 3
            for block in range(blocks):
                here = hi == block
                for c in range(3):
                    row = jnp.broadcast_to(
                        s.now[q, block, c : c + 1, :], (kind.points_pad, LANES)
                    )
                    found = jnp.take_along_axis(row, lo, axis=1, mode="promise_in_bounds")
                    values[c] = jnp.where(here, found, values[c])
            for c in range(3):
                picked[c, cut] = values[c]
        order = [(c, cut) for c in range(3) for cut in range(cuts)]
        for key in order:
            high = high_part(picked[key])
            rows = [high, high, picked[key] - high]
            pad = kind.depth_in - 3 * kind.points_pad
            if pad:
                rows.append(jnp.zeros((pad, LANES), F32))
            stacked.append(jnp.concatenate(rows, axis=0).astype(BF16))
        grad = jnp.dot(
            lhs_in[...], jnp.concatenate(stacked, axis=1), preferred_element_type=F32
        )
        stacked = []
        for number, (c, cut) in enumerate(order):
            lanes = slice(number * LANES, (number + 1) * LANES)
            cut_lanes = slice(cut * LANES, (cut + 1) * LANES)
            pieces = [grad[b * quads_pad : (b + 1) * quads_pad, lanes] for b in range(3)]
            coef = [s.coefs[q, pair, :, cut_lanes] for pair in range(6)]
            flux = jnp.concatenate(
                [
                    coef[PAIR_OF[a, 0]] * pieces[0]
                    + coef[PAIR_OF[a, 1]] * pieces[1]
                    + coef[PAIR_OF[a, 2]] * pieces[2]
                    for a in range(3)
                ],
                axis=0,
            )
            high = high_part(flux)
            rows = [high, high, flux - high]
            pad = kind.depth_out - 9 * quads_pad
            if pad:
                rows.append(jnp.zeros((pad, LANES), F32))
            stacked.append(jnp.concatenate(rows, axis=0).astype(BF16))
        elem = jnp.dot(
            lhs_out[...], jnp.concatenate(stacked, axis=1), preferred_element_type=F32
        )
        for number, (c, cut) in enumerate(order):
            value = elem[:, number * LANES : (number + 1) * LANES]
            high = high_part(value)
            size = kind.points_pad
            s.parts[lane, cut, c * size : (c + 1) * size, :] = high
            s.parts[lane, cut, (c + 4) * size : (c + 5) * size, :] = value - high
        for cut in range(cuts):
            for p in range(points):
                value8 = s.parts[lane, cut, pl.ds(p, 8, stride=kind.points_pad), :]
                chunk = cut * points + p
                place(s.spread, lane, q, chunk, chunk, value8)
        total = jnp.dot(
            s.spread[lane], s.onehot[q, 0:main_rows, :], preferred_element_type=F32
        )
        folded = [fold(total, block) for block in range(blocks)]
        for block in range(blocks):
            s.force[q, block] = folded[block]
        s.sends[q + 1] = pick(lambda block: folded[block], q, s.send_lo[q], s.send_hi[q])

    def split8(value):
        high = high_part(value)
        return jnp.where(low_half, high, value - high)

    def update(q, lane, step):
        lower = s.sends[q]
        upper = s.sends[q + 2]
        values = [
            jnp.where(low_half, pltpu.roll(lower, 4, 0), lower),
            jnp.where(low_half, upper, pltpu.roll(upper, 4, 0)),
        ]
        for m in range(kind.sources):
            four = layers[m][step, q]
            at = kind.at_layer + kind.sources + m
            values.append(jnp.concatenate([four, four], axis=0) * buf[q, at : at + 1, :])
        for number, value in enumerate(values):
            place(s.spread_extra, lane, q, number, 4 * kind.tiles + number, split8(value))
        total = jnp.dot(
            s.spread_extra[lane],
            s.onehot[q, main_rows : main_rows + 256 * kind.extra_tiles, :],
            preferred_element_type=F32,
        )
        after = []
        for block in range(blocks):
            now = s.now[q, block]
            scale = buf[q, kind.at_minv + block : kind.at_minv + block + 1, :]
            whole = s.force[q, block] + fold(total, block)
            value = 2.0 * now - s.before[q, block] + scale * whole
            s.before[q, block] = now
            s.now[q, block] = value
            after.append(value)
        if emit is not None:
            picked = pick(lambda block: after[block], q, s.layer_lo[q], s.layer_hi[q])
            emit[step, q] = picked[0:4]

    def one_step(step, _):
        def forces(group, _):
            for lane in range(unroll):
                force(group * unroll + lane, lane)
            return 0

        def updates(group, _):
            for lane in range(unroll):
                update(group * unroll + lane, lane, step)
            return 0

        lax.fori_loop(0, width // unroll, forces, 0)
        lax.fori_loop(0, width // unroll, updates, 0)
        return 0

    lax.fori_loop(0, STEPS, one_step, 0)


SCRATCH = (
    "onehot", "block_of", "coefs", "lo", "hi", "send_lo", "send_hi", "layer_lo", "layer_hi",
    "now", "before", "force", "sends", "parts", "spread", "spread_extra",
)


def scratch_of(kind, width, unroll):
    tiles = kind.tiles + kind.extra_tiles
    rows = 16 * kind.blocks_pad
    return [
        pltpu.VMEM((width, tiles * 256, 256), BF16),
        pltpu.VMEM((width, 4 * tiles, 16, LANES), BF16),
        pltpu.VMEM((width, 6, kind.quads_pad, kind.elems), F32),
        pltpu.VMEM((width, kind.cuts, kind.points_pad, LANES), jnp.int32),
        pltpu.VMEM((width, kind.cuts, kind.points_pad, LANES), jnp.int32),
        pltpu.VMEM((width, 8, LANES), jnp.int32),
        pltpu.VMEM((width, 8, LANES), jnp.int32),
        pltpu.VMEM((width, 8, LANES), jnp.int32),
        pltpu.VMEM((width, 8, LANES), jnp.int32),
        pltpu.VMEM((width, kind.blocks, 8, LANES), F32),
        pltpu.VMEM((width, kind.blocks, 8, LANES), F32),
        pltpu.VMEM((width, kind.blocks, 8, LANES), F32),
        pltpu.VMEM((width + 2, 8, LANES), F32),
        pltpu.VMEM((unroll, kind.cuts, 8 * kind.points_pad, LANES), F32),
        pltpu.VMEM((unroll, rows, kind.tiles * 256), BF16),
        pltpu.VMEM((unroll, rows, kind.extra_tiles * 256), BF16),
    ]


class Refs:
    pass


def window_base(index, count, width):
    return jnp.clip(index - STEPS, 0, count - width)


def sim_kernel(kind, width, unroll, groups, offsets, has_layers, *refs):
    sub = lax.axis_index("sub")
    count = lax.axis_size("sub")
    chips = count // 2
    n_bufs = 2 * len(offsets)
    bufs, refs = refs[:n_bufs], refs[n_bufs:]
    lhs_in, lhs_out, refs = refs[0], refs[1], refs[2:]
    layers = None
    if has_layers:
        layers, refs = refs[: kind.sources], refs[kind.sources :]
    final, refs = refs[0], refs[1:]
    emit = None
    if not has_layers:
        emit, refs = refs[0], refs[1:]
    buf, sem, refs = refs[0], refs[1], refs[2:]
    s = Refs()
    for name, ref in zip(SCRATCH, refs, strict=True):
        setattr(s, name, ref)
    grp = lax.axis_index("grp")
    low, high = groups
    mine = jnp.logical_and(grp >= low, grp < high)
    base = window_base(sub, count, width)

    @pl.when(mine)
    def _():
        if width < count:
            buf[...] = jnp.zeros(buf.shape, F32)
        copies = []
        for number, offset in enumerate(offsets):
            for other in range(2):
                chip = lax.rem(sub // 2 - offset + chips, chips)
                core = lax.rem(sub, 2)
                slot = chip * 2 + (core if other == 0 else 1 - core) - base
                at = 2 * number + other
                inside = jnp.logical_and(slot >= 0, slot < width)
                slot = jnp.clip(slot, 0, width - 1)
                copy = pltpu.make_async_copy(bufs[at], buf.at[slot], sem.at[at])
                copies.append((inside, copy))
        for phase in ("start", "wait"):
            for inside, copy in copies:
                if width < count:
                    pl.when(inside)(getattr(copy, phase))
                else:
                    getattr(copy, phase)()
        simulate(kind, width, unroll, buf, lhs_in, lhs_out, layers, emit, s)
        for block in range(kind.blocks):
            final[0, 0, :, block * LANES : (block + 1) * LANES] = s.now[sub - base, block, 0:3, :]

    @pl.when(jnp.logical_not(mine))
    def _():
        final[...] = jnp.zeros(final.shape, F32)


def run_sim(kind, width, unroll, groups, offsets, bufs, tables, layers):
    has_layers = layers is not None
    out_shape = [jax.ShapeDtypeStruct((1, 1, 3, kind.count), F32)]
    if not has_layers:
        out_shape.append(jax.ShapeDtypeStruct((STEPS, width, 4, LANES), F32))
    vmem = pl.BlockSpec(memory_space=pltpu.VMEM)
    hbm = pl.BlockSpec(memory_space=pl.ANY)
    n_layers = len(layers) if has_layers else 0
    return pl.pallas_call(
        functools.partial(sim_kernel, kind, width, unroll, groups, offsets, has_layers),
        out_shape=out_shape,
        in_specs=[hbm] * len(bufs) + [vmem] * (2 + n_layers),
        out_specs=[vmem] * len(out_shape),
        scratch_shapes=[
            pltpu.VMEM((width, kind.rows, LANES), F32),
            pltpu.SemaphoreType.DMA((len(bufs),)),
        ]
        + scratch_of(kind, width, unroll),
        cost_estimate=pl.CostEstimate(flops=10**9, bytes_accessed=10**6, transcendentals=0),
        name="site_sim" if has_layers else "reg_sim",
    )(*bufs, *tables, *(layers or ()))


def pack_kernel(reg, site, site_from, *refs):
    (reg_disp, reg_vel, site_disp, site_vel, reg_nodes, site_nodes, reg_coefs, site_coefs,
     reg_minv, site_minv, reg_send, reg_recv, site_send, site_recv, slot_fill,
     layer_src, layer_fill, layer_dst, layer_stiff, reg_out, site_out) = refs
    grp = lax.axis_index("grp")

    @pl.when(grp < site_from)
    def _():
        fill = [slot_fill[0, 0, k] for k in range(2)]
        pack_kind(reg, reg_out, reg_disp, reg_vel, reg_nodes, reg_coefs, reg_minv,
                  reg_send, reg_recv, fill, (layer_src, layer_fill[0, 0]))

    @pl.when(grp >= site_from)
    def _():
        fill = [slot_fill[0, 0, k] for k in range(2, 4)]
        pack_kind(site, site_out, site_disp, site_vel, site_nodes, site_coefs, site_minv,
                  site_send, site_recv, fill, (layer_dst, layer_stiff))


def tables_of(kind, table):
    size = kind.quads_pad
    parts = [
        jnp.pad(
            table[a * kind.quads : (a + 1) * kind.quads],
            ((0, size - kind.quads), (0, kind.points_pad - kind.points)),
        )
        for a in range(3)
    ]
    whole = jnp.concatenate(parts, axis=0)
    high = lax.reduce_precision(whole, 8, 7)
    low = lax.reduce_precision(whole - high, 8, 7)
    first = jnp.concatenate([high, low, high], axis=1)
    first = jnp.pad(first, ((0, 0), (0, kind.depth_in - first.shape[1])))
    second = -jnp.concatenate([high.T, low.T, high.T], axis=1)
    second = jnp.pad(second, ((0, 0), (0, kind.depth_out - second.shape[1])))
    return first.astype(BF16), second.astype(BF16)


def gather_window(value, groups, offsets, count):
    chips = count // 2
    low, high = groups

    def moved(array, chip_shift, flip):
        route = []
        for grp in range(low, high):
            for index in range(count):
                chip, core = divmod(index, 2)
                target = ((chip + chip_shift) % chips) * 2 + (core ^ flip)
                route.append((grp * count + index, grp * count + target))
        return lax.ppermute(array, ("grp", "sub"), route)

    by_chip = [value if shift % chips == 0 else moved(value, shift, 0) for shift in offsets]
    result = []
    for array in by_chip:
        result += [array, moved(array, 0, 1)]
    return result


def shards(
    reg_disp, reg_vel, site_disp, site_vel, reg_nodes, site_nodes, reg_coefs, site_coefs,
    reg_table, site_table, reg_minv, site_minv, reg_send, reg_recv, site_send, site_recv,
    slot_fill, layer_src, layer_fill, layer_dst, layer_stiff,
):
    group_count = lax.axis_size("grp")
    count = lax.axis_size("sub")
    site_groups = group_count // 4
    reg_groups = 3 * site_groups
    slots = reg_send.shape[-1]
    reg = Kind(reg_nodes, reg_coefs, reg_disp, slots, 0)
    site = Kind(site_nodes, site_coefs, site_disp, slots, 3)
    unroll = min(UNROLL, count)
    width = min(count, up_to(2 * STEPS + 1, unroll))
    chips = count // 2
    reach = STEPS // 2
    if 2 * reach + 1 >= chips:
        offsets = tuple(range(chips))
    else:
        offsets = tuple(range(-reach, reach + 1))

    vmem = pl.BlockSpec(memory_space=pltpu.VMEM)
    smem = pl.BlockSpec(memory_space=pltpu.SMEM)
    reg_buf, site_buf = pl.pallas_call(
        functools.partial(pack_kernel, reg, site, reg_groups),
        out_shape=[
            jax.ShapeDtypeStruct((reg.rows, LANES), F32),
            jax.ShapeDtypeStruct((site.rows, LANES), F32),
        ],
        in_specs=[vmem] * 14 + [smem, vmem, smem, vmem, vmem],
        out_specs=[vmem] * 2,
        name="pack",
    )(
        reg_disp, reg_vel, site_disp, site_vel, reg_nodes, site_nodes, reg_coefs, site_coefs,
        reg_minv, site_minv, reg_send, reg_recv, site_send, site_recv, slot_fill,
        layer_src, layer_fill, layer_dst, layer_stiff,
    )
    reg_tables = tables_of(reg, reg_table)
    site_tables = tables_of(site, site_table)
    reg_bufs = gather_window(reg_buf, (0, reg_groups), offsets, count)
    site_bufs = gather_window(site_buf, (reg_groups, group_count), offsets, count)
    reg_final, layer_out = run_sim(
        reg, width, unroll, (0, reg_groups), offsets, reg_bufs, reg_tables, None
    )
    layers = [
        lax.ppermute(
            layer_out,
            "grp",
            [(m * site_groups + i, reg_groups + i) for i in range(site_groups)],
        )
        for m in range(3)
    ]
    (site_final,) = run_sim(
        site, width, unroll, (reg_groups, group_count), offsets, site_bufs, site_tables, layers
    )
    return reg_final, site_final


def solution(mesh):
    def spec(rank):
        return P("grp", "sub", *([None] * (rank - 2)))

    ranks = (4, 4, 4, 4, 4, 4, 6, 6, 0, 0, 3, 3, 4, 4, 4, 4, 3, 3, 2, 4, 4)
    return jax.shard_map(
        shards,
        mesh=mesh,
        in_specs=tuple(spec(rank) if rank else P() for rank in ranks),
        out_specs=(spec(4), spec(4)),
        check_vma=False,
    )
```

time: 603 us -> 149 us (0.25)
  the two profiles are of different devices: /device:TPU:15 before, /device:TPU:6 now
where the time goes in v1:
time: 149 us; the launch traced here: 146 us
  Pallas kernels  66.7 us (45%)
  waiting for transfers between devices  36.7 us (25%)
  starting transfers between devices  27 us (18%)
  local copies, waits for them, and re-layouts  13.4 us (9%)
  between operations  1.84 us (1%)
    pallas_call x2, Pallas kernels, run_sim(): pl.pallas_call(functools.partial(sim_kernel, kind, width, unroll, groups,...  65 us
    ppermute x3, waiting for transfers between devices, shards(): lax.ppermute(layer_out, 'grp', [(m * site_groups + i, reg_groups + i) for...  36.3 us
    ppermute x14, starting transfers between devices, moved(): return lax.ppermute(array, ('grp', 'sub'), route)  23.1 us
    unnamed x70, local copies, waits for them, and re-layouts  10.9 us
    ppermute x3, starting transfers between devices, shards(): lax.ppermute(layer_out, 'grp', [(m * site_groups + i, reg_groups + i) for...  3.86 us
  transfers between devices with their start and end apart: 17, of which 2 were waited for; matrix products, arithmetic and copies ran while one was open for 3% of the time, Pallas kernels for 1%

profile of v1, /device:TPU:6, one launch (start us, length us, event | category | flops | bytes accessed | tf_op | source)
XLA Modules:
  0.0 146.1 jit_solution(7599563938585581955)
XLA Ops:
  1.9 1.3 copy.30.refs_18_
  7.1 1.7 %pack.1 = (f32[96,128]{1,0:T(8,128)}, f32[280,128]{1,0:T(8,128)}) custom-call(f32[1,1,3,384]{3,2,1,0:T(4,128)} %copy.23.refs_0_, f32[1,1,3,384]{3,2,1,0:T(4,128)} %copy.24.refs_1_, f32[1,1,3,1536]{3,2,1,0:T(4,128)} %copy.25.refs_2_, f32[1,1,3,1536]{3,2,1,0:T(4,128)} %copy.26.refs_3_, s32[1,1,10,256]{3,2,1,0:T(8,128)} %copy.27.refs_4_, ...), custom_call_target="tpu_custom_call" | custom-call | tf_op jit(solution)/shard_map/pack/pallas_call | solution.py:530
  9.4 0.7 collective-permute-start.3
  10.1 0.7 collective-permute-start.1
  10.8 0.7 collective-permute-start
  11.4 5.5 %collective-permute-start.12 = (f32[280,128]{1,0:T(8,128)}, f32[280,128]{1,0:T(8,128)S(1)}, u32[]{:S(2)}, u32[]{:S(2)}) collective-permute-start(f32[280,128]{1,0:T(8,128)} %get-tuple-element.8.refs_0_), channel_id=1, source_target_pairs={{24,30},{25,31},{26,24},{27,25},{28,26},{29,27},{30,28},{31,29}} | collective-permute-start | bytes 430088 | tf_op jit(solution)/shard_map/ppermute | solution.py:498
  17.3 0.7 copy-done
  18.3 0.7 collective-permute-start.6
  19.0 0.7 collective-permute-start.4
  19.7 0.7 collective-permute-start.2
  20.4 0.7 copy.34.refs_8_
  21.7 1.9 %collective-permute-start.10 = (f32[280,128]{1,0:T(8,128)S(1)}, f32[280,128]{1,0:T(8,128)S(1)}, u32[]{:S(2)}, u32[]{:S(2)}) collective-permute-start(f32[280,128]{1,0:T(8,128)S(1)} %copy-done.10), channel_id=1, source_target_pairs={{24,28},{25,29},{26,30},{27,31},{28,24},{29,25},{30,26},{31,27}} | collective-permute-start | bytes 430088 | tf_op jit(solution)/shard_map/ppermute | solution.py:498
  23.6 2.9 %collective-permute-start.8 = (f32[280,128]{1,0:T(8,128)S(1)}, f32[280,128]{1,0:T(8,128)S(1)}, u32[]{:S(2)}, u32[]{:S(2)}) collective-permute-start(f32[280,128]{1,0:T(8,128)S(1)} %copy-done.10), channel_id=1, source_target_pairs={{24,26},{25,27},{26,28},{27,29},{28,30},{29,31},{30,24},{31,25}} | collective-permute-start | bytes 430088 | tf_op jit(solution)/shard_map/ppermute | solution.py:498
  26.6 1.9 %collective-permute-start.7 = (f32[280,128]{1,0:T(8,128)S(1)}, f32[280,128]{1,0:T(8,128)S(1)}, u32[]{:S(2)}, u32[]{:S(2)}) collective-permute-start(f32[280,128]{1,0:T(8,128)S(1)} %copy-done.10), channel_id=1, source_target_pairs={{24,25},{25,24},{26,27},{27,26},{28,29},{29,28},{30,31},{31,30}} | collective-permute-start | bytes 430088 | tf_op jit(solution)/shard_map/ppermute | solution.py:498
  29.2 1.4 reg_sim.1
  30.6 1.3 collective-permute-start.16
  32.0 1.3 collective-permute-start.15
  33.7 1.3 collective-permute-start.14
  35.0 2.0 %collective-permute-start.13 = (f32[280,128]{1,0:T(8,128)S(1)}, f32[280,128]{1,0:T(8,128)S(1)}, u32[]{:S(2)}, u32[]{:S(2)}) collective-permute-start(f32[280,128]{1,0:T(8,128)S(1)} %collective-permute-done.12.refs_6_), channel_id=1, source_target_pairs={{24,25},{25,24},{26,27},{27,26},{28,29},{29,28},{30,31},{31,30}} | collective-permute-start | bytes 430088 | tf_op jit(solution)/shard_map/ppermute | solution.py:498
  37.0 2.3 %collective-permute-start.11 = (f32[280,128]{1,0:T(8,128)S(1)}, f32[280,128]{1,0:T(8,128)S(1)}, u32[]{:S(2)}, u32[]{:S(2)}) collective-permute-start(f32[280,128]{1,0:T(8,128)S(1)} %collective-permute-done.10.refs_4_), channel_id=1, source_target_pairs={{24,25},{25,24},{26,27},{27,26},{28,29},{29,28},{30,31},{31,30}} | collective-permute-start | bytes 430088 | tf_op jit(solution)/shard_map/ppermute | solution.py:498
  39.4 36.3 %collective-permute-done.16.refs_12_ = f32[8,8,4,128]{3,2,1,0:T(4,128)S(1)} collective-permute-done((f32[8,8,4,128]{3,2,1,0:T(4,128)}, f32[8,8,4,128]{3,2,1,0:T(4,128)S(1)}, u32[]{:S(2)}, u32[]{:S(2)}) %collective-permute-start.16) | collective-permute-done | bytes 131104 | tf_op jit(solution)/shard_map/ppermute | solution.py:552
  75.6 1.9 %collective-permute-start.9 = (f32[280,128]{1,0:T(8,128)S(1)}, f32[280,128]{1,0:T(8,128)S(1)}, u32[]{:S(2)}, u32[]{:S(2)}) collective-permute-start(f32[280,128]{1,0:T(8,128)S(1)} %collective-permute-done.8.refs_2_), channel_id=1, source_target_pairs={{24,25},{25,24},{26,27},{27,26},{28,29},{29,28},{30,31},{31,30}} | collective-permute-start | bytes 430088 | tf_op jit(solution)/shard_map/ppermute | solution.py:498
  81.1 63.6 %site_sim.1 = f32[1,1,3,1536]{3,2,1,0:T(4,128)} custom-call(f32[280,128]{1,0:T(8,128)} %get-tuple-element.8.refs_0_, f32[280,128]{1,0:T(8,128)} %copy-done.14, f32[280,128]{1,0:T(8,128)} %copy-done.13, f32[280,128]{1,0:T(8,128)} %copy-done.17, f32[280,128]{1,0:T(8,128)} %copy-done.12, f32[280,128]{1,0:T(8,128)} %copy-done.16, f32[280,128]{1,0:T(8,128)} %copy-done.11, ...), custom_call_target="tpu_custom_call" | custom-call | flops 1000000000 | bytes 1000000 | tf_op jit(solution)/shard_map/site_sim/pallas_call | solution.py:434
  144.7 1.4 copy.37
  (97 shorter events, 10.9 us)
Async XLA Ops:
  7.1 9.9 %copy-start.6 = (f32[12,10]{1,0:T(8,128)S(1)}, f32[12,10]{1,0:T(8,128)}, u32[]{:S(2)}) copy-start(f32[12,10]{1,0:T(8,128)} %param.29) | copy-start | bytes 1444
  8.7 9.5 %collective-permute-start.5 = (f32[96,128]{1,0:T(8,128)}, f32[96,128]{1,0:T(8,128)S(1)}, u32[]{:S(2)}, u32[]{:S(2)}) collective-permute-start(f32[96,128]{1,0:T(8,128)} %get-tuple-element.6.refs_0_), channel_id=1, source_target_pairs={{0,6},{1,7},{2,0},{3,1},{4,2},{5,3},{6,4},{7,5},{8,14},{9,15},{10,... | collective-permute-start | bytes 147464 | tf_op jit(solution)/shard_map/ppermute | solution.py:498
  9.4 9.5 %collective-permute-start.3 = (f32[96,128]{1,0:T(8,128)}, f32[96,128]{1,0:T(8,128)S(1)}, u32[]{:S(2)}, u32[]{:S(2)}) collective-permute-start(f32[96,128]{1,0:T(8,128)} %get-tuple-element.6.refs_0_), channel_id=1, source_target_pairs={{0,4},{1,5},{2,6},{3,7},{4,0},{5,1},{6,2},{7,3},{8,12},{9,13},{10,... | collective-permute-start | bytes 147464 | tf_op jit(solution)/shard_map/ppermute | solution.py:498
  10.1 9.6 %collective-permute-start.1 = (f32[96,128]{1,0:T(8,128)}, f32[96,128]{1,0:T(8,128)S(1)}, u32[]{:S(2)}, u32[]{:S(2)}) collective-permute-start(f32[96,128]{1,0:T(8,128)} %get-tuple-element.6.refs_0_), channel_id=1, source_target_pairs={{0,2},{1,3},{2,4},{3,5},{4,6},{5,7},{6,0},{7,1},{8,10},{9,11},{10,... | collective-permute-start | bytes 147464 | tf_op jit(solution)/shard_map/ppermute | solution.py:498
  10.8 10.9 %collective-permute-start = (f32[96,128]{1,0:T(8,128)}, f32[96,128]{1,0:T(8,128)S(1)}, u32[]{:S(2)}, u32[]{:S(2)}) collective-permute-start(f32[96,128]{1,0:T(8,128)} %get-tuple-element.6.refs_0_), channel_id=1, source_target_pairs={{0,1},{1,0},{2,3},{3,2},{4,5},{5,4},{6,7},{7,6},{8,9},{9,8},{10,11... | collective-permute-start | bytes 147464 | tf_op jit(solution)/shard_map/ppermute | solution.py:498
  11.4 20.5 %collective-permute-start.12 = (f32[280,128]{1,0:T(8,128)}, f32[280,128]{1,0:T(8,128)S(1)}, u32[]{:S(2)}, u32[]{:S(2)}) collective-permute-start(f32[280,128]{1,0:T(8,128)} %get-tuple-element.8.refs_0_), channel_id=1, source_target_pairs={{24,30},{25,31},{26,24},{27,25},{28,26},{29,27},{30,28},{31,29}} | collective-permute-start | bytes 430088 | tf_op jit(solution)/shard_map/ppermute | solution.py:498
  18.3 10.2 %copy-start.21 = (f32[96,128]{1,0:T(8,128)}, f32[96,128]{1,0:T(8,128)S(1)}, u32[]{:S(2)}) copy-start(f32[96,128]{1,0:T(8,128)S(1)} %collective-permute-done.5.refs_6_) | copy-start | bytes 147460
  18.3 5.3 %collective-permute-start.6 = (f32[96,128]{1,0:T(8,128)S(1)}, f32[96,128]{1,0:T(8,128)S(1)}, u32[]{:S(2)}, u32[]{:S(2)}) collective-permute-start(f32[96,128]{1,0:T(8,128)S(1)} %collective-permute-done.5.refs_6_), channel_id=1, source_target_pairs={{0,1},{1,0},{2,3},{3,2},{4,5},{5,4},{6,7},{7,6},{8,9},{9,8},{10,11... | collective-permute-start | bytes 147464 | tf_op jit(solution)/shard_map/ppermute | solution.py:498
  19.0 9.6 %copy-start.22 = (f32[96,128]{1,0:T(8,128)}, f32[96,128]{1,0:T(8,128)S(1)}, u32[]{:S(2)}) copy-start(f32[96,128]{1,0:T(8,128)S(1)} %collective-permute-done.3.refs_4_) | copy-start | bytes 147460
  19.0 7.6 %collective-permute-start.4 = (f32[96,128]{1,0:T(8,128)S(1)}, f32[96,128]{1,0:T(8,128)S(1)}, u32[]{:S(2)}, u32[]{:S(2)}) collective-permute-start(f32[96,128]{1,0:T(8,128)S(1)} %collective-permute-done.3.refs_4_), channel_id=1, source_target_pairs={{0,1},{1,0},{2,3},{3,2},{4,5},{5,4},{6,7},{7,6},{8,9},{9,8},{10,11... | collective-permute-start | bytes 147464 | tf_op jit(solution)/shard_map/ppermute | solution.py:498
  19.7 8.8 %collective-permute-start.2 = (f32[96,128]{1,0:T(8,128)S(1)}, f32[96,128]{1,0:T(8,128)S(1)}, u32[]{:S(2)}, u32[]{:S(2)}) collective-permute-start(f32[96,128]{1,0:T(8,128)S(1)} %collective-permute-done.1.refs_2_), channel_id=1, source_target_pairs={{0,1},{1,0},{2,3},{3,2},{4,5},{5,4},{6,7},{7,6},{8,9},{9,8},{10,11... | collective-permute-start | bytes 147464 | tf_op jit(solution)/shard_map/ppermute | solution.py:498
  21.7 12.0 %collective-permute-start.10 = (f32[280,128]{1,0:T(8,128)S(1)}, f32[280,128]{1,0:T(8,128)S(1)}, u32[]{:S(2)}, u32[]{:S(2)}) collective-permute-start(f32[280,128]{1,0:T(8,128)S(1)} %copy-done.10), channel_id=1, source_target_pairs={{24,28},{25,29},{26,30},{27,31},{28,24},{29,25},{30,26},{31,27}} | collective-permute-start | bytes 430088 | tf_op jit(solution)/shard_map/ppermute | solution.py:498
  23.6 11.4 %collective-permute-start.8 = (f32[280,128]{1,0:T(8,128)S(1)}, f32[280,128]{1,0:T(8,128)S(1)}, u32[]{:S(2)}, u32[]{:S(2)}) collective-permute-start(f32[280,128]{1,0:T(8,128)S(1)} %copy-done.10), channel_id=1, source_target_pairs={{24,26},{25,27},{26,28},{27,29},{28,30},{29,31},{30,24},{31,25}} | collective-permute-start | bytes 430088 | tf_op jit(solution)/shard_map/ppermute | solution.py:498
  26.6 10.4 %collective-permute-start.7 = (f32[280,128]{1,0:T(8,128)S(1)}, f32[280,128]{1,0:T(8,128)S(1)}, u32[]{:S(2)}, u32[]{:S(2)}) collective-permute-start(f32[280,128]{1,0:T(8,128)S(1)} %copy-done.10), channel_id=1, source_target_pairs={{24,25},{25,24},{26,27},{27,26},{28,29},{29,28},{30,31},{31,30}} | collective-permute-start | bytes 430088 | tf_op jit(solution)/shard_map/ppermute | solution.py:498
  30.6 45.0 %collective-permute-start.16 = (f32[8,8,4,128]{3,2,1,0:T(4,128)}, f32[8,8,4,128]{3,2,1,0:T(4,128)S(1)}, u32[]{:S(2)}, u32[]{:S(2)}) collective-permute-start(f32[8,8,4,128]{3,2,1,0:T(4,128)} %get-tuple-element.9), channel_id=1, source_target_pairs={{16,24},{17,25},{18,26},{19,27},{20,28},{21,29},{22,30},{23,31}} | collective-permute-start | bytes 393224 | tf_op jit(solution)/shard_map/ppermute | solution.py:552
  31.9 47.8 %copy-start.11 = (f32[280,128]{1,0:T(8,128)}, f32[280,128]{1,0:T(8,128)S(1)}, u32[]{:S(2)}) copy-start(f32[280,128]{1,0:T(8,128)S(1)} %collective-permute-done.12.refs_6_) | copy-start | bytes 430084
  32.0 47.7 %collective-permute-start.15 = (f32[8,8,4,128]{3,2,1,0:T(4,128)}, f32[8,8,4,128]{3,2,1,0:T(4,128)S(1)}, u32[]{:S(2)}, u32[]{:S(2)}) collective-permute-start(f32[8,8,4,128]{3,2,1,0:T(4,128)} %get-tuple-element.9), channel_id=1, source_target_pairs={{8,24},{9,25},{10,26},{11,27},{12,28},{13,29},{14,30},{15,31}} | collective-permute-start | bytes 393224 | tf_op jit(solution)/shard_map/ppermute | solution.py:552
  33.7 46.1 %copy-start.12 = (f32[280,128]{1,0:T(8,128)}, f32[280,128]{1,0:T(8,128)S(1)}, u32[]{:S(2)}) copy-start(f32[280,128]{1,0:T(8,128)S(1)} %collective-permute-done.10.refs_4_) | copy-start | bytes 430084
  33.7 46.0 %collective-permute-start.14 = (f32[8,8,4,128]{3,2,1,0:T(4,128)}, f32[8,8,4,128]{3,2,1,0:T(4,128)S(1)}, u32[]{:S(2)}, u32[]{:S(2)}) collective-permute-start(f32[8,8,4,128]{3,2,1,0:T(4,128)} %get-tuple-element.9), channel_id=1, source_target_pairs={{0,24},{1,25},{2,26},{3,27},{4,28},{5,29},{6,30},{7,31}} | collective-permute-start | bytes 393224 | tf_op jit(solution)/shard_map/ppermute | solution.py:552
  35.0 44.8 %copy-start.13 = (f32[280,128]{1,0:T(8,128)}, f32[280,128]{1,0:T(8,128)S(1)}, u32[]{:S(2)}) copy-start(f32[280,128]{1,0:T(8,128)S(1)} %collective-permute-done.8.refs_2_) | copy-start | bytes 430084
  35.0 44.7 %collective-permute-start.13 = (f32[280,128]{1,0:T(8,128)S(1)}, f32[280,128]{1,0:T(8,128)S(1)}, u32[]{:S(2)}, u32[]{:S(2)}) collective-permute-start(f32[280,128]{1,0:T(8,128)S(1)} %collective-permute-done.12.refs_6_), channel_id=1, source_target_pairs={{24,25},{25,24},{26,27},{27,26},{28,29},{29,28},{30,31},{31,30}} | collective-permute-start | bytes 430088 | tf_op jit(solution)/shard_map/ppermute | solution.py:498
  37.0 42.8 %copy-start.14 = (f32[280,128]{1,0:T(8,128)}, f32[280,128]{1,0:T(8,128)S(1)}, u32[]{:S(2)}) copy-start(f32[280,128]{1,0:T(8,128)S(1)} %collective-permute-done.7.refs_1_) | copy-start | bytes 430084
  37.0 42.7 %collective-permute-start.11 = (f32[280,128]{1,0:T(8,128)S(1)}, f32[280,128]{1,0:T(8,128)S(1)}, u32[]{:S(2)}, u32[]{:S(2)}) collective-permute-start(f32[280,128]{1,0:T(8,128)S(1)} %collective-permute-done.10.refs_4_), channel_id=1, source_target_pairs={{24,25},{25,24},{26,27},{27,26},{28,29},{29,28},{30,31},{31,30}} | collective-permute-start | bytes 430088 | tf_op jit(solution)/shard_map/ppermute | solution.py:498
  75.6 4.1 %collective-permute-start.9 = (f32[280,128]{1,0:T(8,128)S(1)}, f32[280,128]{1,0:T(8,128)S(1)}, u32[]{:S(2)}, u32[]{:S(2)}) collective-permute-start(f32[280,128]{1,0:T(8,128)S(1)} %collective-permute-done.8.refs_2_), channel_id=1, source_target_pairs={{24,25},{25,24},{26,27},{27,26},{28,29},{29,28},{30,31},{31,30}} | collective-permute-start | bytes 430088 | tf_op jit(solution)/shard_map/ppermute | solution.py:498
  (21 other events, 44.9 us)

commit v2 on v1

v2 whole, which is shorter than its diff:
```python
import functools

import jax
import jax.numpy as jnp
from jax import lax
from jax.experimental import pallas as pl
from jax.experimental.pallas import tpu as pltpu
from jax.sharding import PartitionSpec as P

STEPS = 8
UNROLL = 8
LANES = 128
F32 = jnp.float32
BF16 = jnp.bfloat16
PAIRS = ((0, 0), (0, 1), (0, 2), (1, 1), (1, 2), (2, 2))
PAIR_OF = {**{ab: i for i, ab in enumerate(PAIRS)}, **{ab[::-1]: i for i, ab in enumerate(PAIRS)}}


def up_to(value, unit):
    return -(-value // unit) * unit


class Kind:
    def __init__(self, nodes, coefs, disp, sources):
        self.points, self.elems = nodes.shape[-2:]
        self.quads = coefs.shape[-2]
        self.count = disp.shape[-1]
        self.blocks = self.count // LANES
        self.cuts = self.elems // LANES
        self.points_pad = up_to(self.points, 8)
        self.quads_pad = up_to(self.quads, 8)
        self.blocks_pad = up_to(self.blocks, 2)
        self.depth_in = up_to(3 * self.points_pad, 16)
        self.depth_out = up_to(9 * self.quads_pad, 16)
        self.chunks = self.points * self.cuts
        self.sources = sources
        self.tiles = up_to(self.chunks, 4) // 4
        self.extra = 2 + sources
        self.extra_tiles = up_to(self.extra, 4) // 4
        self.table_turned = self.quads_pad == self.quads
        row = 0
        for name, rows in (
            ("coefs", 6 * self.quads * self.cuts),
            ("nodes", self.points * self.cuts),
            ("disp", 3 * self.blocks),
            ("vel", 3 * self.blocks),
            ("minv", self.blocks),
            ("send", 2),
            ("recv", 2),
            ("layer", 2 * sources if sources else 1),
        ):
            setattr(self, "at_" + name, row)
            row += rows
        self.rows = up_to(row, 8)


def pack_kernel(kind, *refs):
    disp, vel, nodes, coefs, minv, send, recv, fill, layer_a, layer_b, table, out, first, second = refs[:14]
    work = refs[14]
    for pair, (a, b) in enumerate(PAIRS):
        for cut in range(kind.cuts):
            at = kind.at_coefs + (pair * kind.cuts + cut) * kind.quads
            out[at : at + kind.quads, :] = coefs[0, 0, a, b, :, cut * LANES : (cut + 1) * LANES]
    for cut in range(kind.cuts):
        for p in range(kind.points):
            at = kind.at_nodes + cut * kind.points + p
            out[at : at + 1, :] = nodes[0, p, :, cut * LANES : (cut + 1) * LANES].astype(F32)
    for block in range(kind.blocks):
        lanes = slice(block * LANES, (block + 1) * LANES)
        for c in range(3):
            for at, ref in ((kind.at_disp, disp), (kind.at_vel, vel)):
                out[at + 3 * block + c : at + 3 * block + c + 1, :] = ref[0, c, :, lanes]
        out[kind.at_minv + block : kind.at_minv + block + 1, :] = minv[0, 0:1, lanes]
    lane = lax.broadcasted_iota(jnp.int32, (1, LANES), 1)
    for side in range(2):
        live = lane < fill[0, 0, (2 if kind.sources else 0) + side]
        row = send[0, 0, side : side + 1, :]
        out[kind.at_send + side : kind.at_send + side + 1, :] = jnp.where(live, row, -1).astype(F32)
    out[kind.at_recv : kind.at_recv + 2, :] = recv[0, 0].astype(F32)
    for m in range(kind.sources):
        at = kind.at_layer + m
        out[at : at + 1, :] = layer_a[0, m].astype(F32)
        out[at + kind.sources : at + kind.sources + 1, :] = layer_b[0, m]
    if not kind.sources:
        row = layer_a[0, 0:1, :]
        live = lane < layer_b[0, 0]
        out[kind.at_layer : kind.at_layer + 1, :] = jnp.where(live, row, -1).astype(F32)
    size = kind.quads_pad
    work[...] = jnp.zeros(work.shape, F32)
    if kind.table_turned:
        work[0 : kind.points, 0 : 3 * kind.quads] = table[...]
        turned = work[...]
        plain = jnp.transpose(turned)
    else:
        for a in range(3):
            work[a * size : a * size + kind.quads, 0 : kind.points] = table[
                a * kind.quads : (a + 1) * kind.quads, :
            ]
        plain = work[...]
        turned = jnp.transpose(plain)
    step = kind.points_pad
    high = high_part(plain)
    low = plain - high
    rows = high + pltpu.roll(low, step, 1) + pltpu.roll(high, 2 * step, 1)
    first[...] = rows[0 : 3 * size, 0 : kind.depth_in].astype(BF16)
    high = high_part(turned)
    low = turned - high
    wide = jnp.zeros((LANES, LANES), F32)
    high = jnp.concatenate([high, wide], axis=1)
    low = jnp.concatenate([low, wide], axis=1)
    rows = high + pltpu.roll(low, 3 * size, 1) + pltpu.roll(high, 6 * size, 1)
    second[...] = (-rows[0 : kind.points_pad, 0 : kind.depth_out]).astype(BF16)


def pack(kind, disp, vel, nodes, coefs, minv, send, recv, fill, layer_a, layer_b, table):
    def thin(array):
        return jnp.transpose(array, (0, 2, 1, 3))

    vmem = pl.BlockSpec(memory_space=pltpu.VMEM)
    smem = pl.BlockSpec(memory_space=pltpu.SMEM)
    if kind.sources:
        layer_a, layer_b = thin(layer_a), thin(layer_b)
    if kind.table_turned:
        table = table.T
    return pl.pallas_call(
        functools.partial(pack_kernel, kind),
        out_shape=[
            jax.ShapeDtypeStruct((kind.rows, LANES), F32),
            jax.ShapeDtypeStruct((3 * kind.quads_pad, kind.depth_in), BF16),
            jax.ShapeDtypeStruct((kind.points_pad, kind.depth_out), BF16),
        ],
        in_specs=[vmem] * 7 + [smem, vmem, vmem if kind.sources else smem, vmem],
        out_specs=[vmem] * 3,
        scratch_shapes=[pltpu.VMEM((LANES, LANES), F32)],
        name="site_pack" if kind.sources else "reg_pack",
    )(thin(disp), thin(vel), thin(nodes), coefs, minv, send, recv, fill, layer_a, layer_b, table)


def split_index(value):
    index = value.astype(jnp.int32)
    return index & (LANES - 1), index >> 7


def high_part(value):
    return value.astype(BF16).astype(F32)


def simulate(kind, width, unroll, buf, lhs_in, lhs_out, layers, emit, s):
    points, cuts, blocks = kind.points, kind.cuts, kind.blocks
    quads_pad = kind.quads_pad
    half_rows = 8 * kind.blocks_pad
    row8 = lax.broadcasted_iota(jnp.int32, (8, LANES), 0)
    low_half = row8 < 4
    row16 = lax.broadcasted_iota(jnp.int32, (16, LANES), 0)
    block_ids = [
        jnp.where(row16 < 8, 2 * j, 2 * j + 1).astype(F32).astype(BF16)
        for j in range(kind.blocks_pad // 2)
    ]
    zero16 = jnp.zeros((16, LANES), BF16)
    zero8 = jnp.zeros((8, LANES), F32)
    lane_ids = lax.broadcasted_iota(jnp.int32, (LANES, LANES), 1).astype(F32).astype(BF16)
    one = jnp.ones((LANES, LANES), BF16)
    none = jnp.zeros((LANES, LANES), BF16)
    main_rows = kind.tiles * 256

    def onehot(q, chunk_no, base_row, columns, at):
        hit = columns[:, at : at + 1] == lane_ids
        tile, half, part = chunk_no // 4, (chunk_no // 2) % 2, chunk_no % 2
        rows = pl.ds(base_row + tile * 256 + part * LANES, LANES)
        s.onehot[q, half, rows, :] = jnp.where(hit, one, none)

    def hold_block(q, chunk_no, hi_row):
        s.block_of[q, chunk_no : chunk_no + 1, :] = hi_row.astype(F32)

    def columns_of(rows):
        count = rows.shape[0]
        if count < LANES:
            rows = jnp.concatenate([rows, jnp.zeros((LANES - count, LANES), F32)], axis=0)
        return jnp.transpose(rows).astype(BF16)

    def setup(q, _):
        for pair in range(6):
            for cut in range(cuts):
                at = kind.at_coefs + (pair * cuts + cut) * kind.quads
                lanes = slice(cut * LANES, (cut + 1) * LANES)
                if kind.quads_pad > kind.quads:
                    s.coefs[q, pair, :, lanes] = jnp.zeros((quads_pad, LANES), F32)
                s.coefs[q, pair, 0 : kind.quads, lanes] = buf[q, at : at + kind.quads, :]
        for cut in range(cuts):
            at = kind.at_nodes + cut * points
            value = buf[q, at : at + points, :]
            lo, hi = split_index(value)
            if kind.points_pad > points:
                s.lo[q, cut] = jnp.zeros((kind.points_pad, LANES), jnp.int32)
                s.hi[q, cut] = jnp.zeros((kind.points_pad, LANES), jnp.int32)
            s.lo[q, cut, 0:points, :] = lo
            s.hi[q, cut, 0:points, :] = hi
            columns = columns_of(lo.astype(F32))
            for p in range(points):
                onehot(q, cut * points + p, 0, columns, p)
                hold_block(q, cut * points + p, hi[p : p + 1, :])
        for chunk in range(kind.chunks, 4 * kind.tiles):
            columns = jnp.zeros((LANES, LANES), BF16)
            onehot(q, chunk, 0, columns, 0)
            hold_block(q, chunk, jnp.zeros((1, LANES), jnp.int32))
        extra = [buf[q, kind.at_recv : kind.at_recv + 2, :]]
        if kind.sources:
            extra.append(buf[q, kind.at_layer : kind.at_layer + kind.sources, :])
        extra.append(jnp.zeros((4 * kind.extra_tiles - kind.extra, LANES), F32))
        lo, hi = split_index(jnp.concatenate([e for e in extra if e.shape[0]], axis=0))
        columns = columns_of(lo.astype(F32))
        for chunk in range(4 * kind.extra_tiles):
            onehot(q, chunk, main_rows, columns, chunk)
            hold_block(q, 4 * kind.tiles + chunk, hi[chunk : chunk + 1, :])
        send_rows = [
            jnp.broadcast_to(buf[q, kind.at_send + side : kind.at_send + side + 1, :], (4, LANES))
            for side in range(2)
        ]
        s.send_lo[q], s.send_hi[q] = split_index(jnp.concatenate(send_rows, axis=0))
        if not kind.sources:
            row = buf[q, kind.at_layer : kind.at_layer + 1, :]
            s.layer_lo[q], s.layer_hi[q] = split_index(jnp.broadcast_to(row, (8, LANES)))
        for block in range(blocks):
            at = kind.at_disp + 3 * block
            now = buf[q, at : at + 3, :]
            at = kind.at_vel + 3 * block
            before = now - buf[q, at : at + 3, :]
            for ref, value in ((s.now, now), (s.before, before)):
                ref[q, block] = zero8
                ref[q, block, 0:3, :] = value
                ref[q, block, 4:7, :] = value
        return 0

    lax.fori_loop(0, width, setup, 0)
    for lane in range(unroll):
        s.parts[lane] = jnp.zeros(s.parts.shape[1:], F32)
    s.sends[0] = zero8
    s.sends[width + 1] = zero8

    def spread(q, first, values):
        blank = jnp.zeros((half_rows, LANES), BF16)
        parts = []
        for number, value8 in enumerate(values):
            doubled = jnp.concatenate([value8, value8], axis=0).astype(BF16)
            held = s.block_of[q, first + number : first + number + 1, :]
            held = jnp.broadcast_to(held, (16, LANES)).astype(BF16)
            parts.append(
                jnp.concatenate(
                    [jnp.where(held == ids, doubled, zero16) for ids in block_ids], axis=0
                )
            )
        parts += [blank] * (4 - len(values))
        return jnp.concatenate(
            [jnp.concatenate(parts[0:2], axis=1), jnp.concatenate(parts[2:4], axis=1)], axis=0
        )

    def scattered(q, first, rows_from, get, count):
        total = None
        for at in range(0, count, 4):
            left = spread(q, first + at, [get(k) for k in range(at, min(at + 4, count))])
            rows = slice(rows_from + at * 64, rows_from + at * 64 + 256)
            right = jnp.concatenate([s.onehot[q, half, rows, :] for half in range(2)], axis=1)
            term = jnp.dot(left, right, preferred_element_type=F32)
            total = term if total is None else total + term
        return total

    def fold(total, block):
        rows = slice(block * 8, block * 8 + 8)
        other = slice(half_rows + block * 8, half_rows + block * 8 + 8)
        value = total[rows, 0:LANES] + total[other, LANES : 2 * LANES]
        return value + pltpu.roll(value, 4, 0)

    def choose(found, bits):
        for bit in bits:
            found = [
                jnp.where(bit, found[k + 1], found[k]) if k + 1 < len(found) else found[k]
                for k in range(0, len(found), 2)
            ]
        return found[0]

    def bits_of(hi):
        count = (blocks - 1).bit_length()
        return [(hi & (1 << k)) != 0 for k in range(count)]

    def lookup(row, lo):
        return jnp.take_along_axis(row, lo, axis=1, mode="promise_in_bounds")

    def pick(source, lo, hi):
        found = [lookup(source(block), lo) for block in range(blocks)]
        return jnp.where(hi < 0, 0.0, choose(found, bits_of(hi)))

    def force(q, lane):
        stacked = []
        picked = {}
        for cut in range(cuts):
            groups = {c: [] for c in range(3)}
            for at in range(0, kind.points_pad, 8):
                lo = s.lo[q, cut, at : at + 8, :]
                bits = bits_of(s.hi[q, cut, at : at + 8, :])
                for c in range(3):
                    found = [
                        lookup(jnp.broadcast_to(s.now[q, block, c : c + 1, :], (8, LANES)), lo)
                        for block in range(blocks)
                    ]
                    groups[c].append(choose(found, bits))
            for c in range(3):
                picked[c, cut] = jnp.concatenate(groups[c], axis=0)
        order = [(c, cut) for c in range(3) for cut in range(cuts)]
        for key in order:
            high = high_part(picked[key])
            rows = [high, high, picked[key] - high]
            pad = kind.depth_in - 3 * kind.points_pad
            if pad:
                rows.append(jnp.zeros((pad, LANES), F32))
            stacked.append(jnp.concatenate(rows, axis=0).astype(BF16))
        grad = jnp.dot(
            lhs_in[...], jnp.concatenate(stacked, axis=1), preferred_element_type=F32
        )
        stacked = []
        for number, (c, cut) in enumerate(order):
            lanes = slice(number * LANES, (number + 1) * LANES)
            cut_lanes = slice(cut * LANES, (cut + 1) * LANES)
            pieces = [grad[b * quads_pad : (b + 1) * quads_pad, lanes] for b in range(3)]
            coef = [s.coefs[q, pair, :, cut_lanes] for pair in range(6)]
            flux = jnp.concatenate(
                [
                    coef[PAIR_OF[a, 0]] * pieces[0]
                    + coef[PAIR_OF[a, 1]] * pieces[1]
                    + coef[PAIR_OF[a, 2]] * pieces[2]
                    for a in range(3)
                ],
                axis=0,
            )
            high = high_part(flux)
            rows = [high, high, flux - high]
            pad = kind.depth_out - 9 * quads_pad
            if pad:
                rows.append(jnp.zeros((pad, LANES), F32))
            stacked.append(jnp.concatenate(rows, axis=0).astype(BF16))
        elem = jnp.dot(
            lhs_out[...], jnp.concatenate(stacked, axis=1), preferred_element_type=F32
        )
        for number, (c, cut) in enumerate(order):
            value = elem[:, number * LANES : (number + 1) * LANES]
            high = high_part(value)
            size = kind.points_pad
            s.parts[lane, cut, c * size : (c + 1) * size, :] = high
            s.parts[lane, cut, (c + 4) * size : (c + 5) * size, :] = value - high
        def entry(chunk):
            cut, p = divmod(chunk, points)
            return s.parts[lane, cut, pl.ds(p, 8, stride=kind.points_pad), :]

        total = scattered(q, 0, 0, entry, kind.chunks)
        folded = [fold(total, block) for block in range(blocks)]
        for block in range(blocks):
            s.force[q, block] = folded[block]
        s.sends[q + 1] = pick(lambda block: folded[block], s.send_lo[q], s.send_hi[q])

    def split8(value):
        high = high_part(value)
        return jnp.where(low_half, high, value - high)

    def update(q, lane, step):
        lower = s.sends[q]
        upper = s.sends[q + 2]
        values = [
            jnp.where(low_half, pltpu.roll(lower, 4, 0), lower),
            jnp.where(low_half, upper, pltpu.roll(upper, 4, 0)),
        ]
        for m in range(kind.sources):
            four = layers[m][step, q]
            at = kind.at_layer + kind.sources + m
            values.append(jnp.concatenate([four, four], axis=0) * buf[q, at : at + 1, :])
        total = scattered(
            q, 4 * kind.tiles, main_rows, lambda k: split8(values[k]), len(values)
        )
        after = []
        for block in range(blocks):
            now = s.now[q, block]
            scale = buf[q, kind.at_minv + block : kind.at_minv + block + 1, :]
            whole = s.force[q, block] + fold(total, block)
            value = 2.0 * now - s.before[q, block] + scale * whole
            s.before[q, block] = now
            s.now[q, block] = value
            after.append(value)
        if emit is not None:
            picked = pick(lambda block: after[block], s.layer_lo[q], s.layer_hi[q])
            emit[step, q] = picked[0:4]

    def one_step(step, _):
        def forces(group, _):
            for lane in range(unroll):
                force(group * unroll + lane, lane)
            return 0

        def updates(group, _):
            for lane in range(unroll):
                update(group * unroll + lane, lane, step)
            return 0

        lax.fori_loop(0, width // unroll, forces, 0)
        lax.fori_loop(0, width // unroll, updates, 0)
        return 0

    lax.fori_loop(0, STEPS, one_step, 0)


SCRATCH = (
    "onehot", "block_of", "coefs", "lo", "hi", "send_lo", "send_hi", "layer_lo", "layer_hi",
    "now", "before", "force", "sends", "parts",
)


def scratch_of(kind, width, unroll):
    tiles = kind.tiles + kind.extra_tiles
    return [
        pltpu.VMEM((width, 2, tiles * 256, LANES), BF16),
        pltpu.VMEM((width, 4 * tiles, LANES), F32),
        pltpu.VMEM((width, 6, kind.quads_pad, kind.elems), F32),
        pltpu.VMEM((width, kind.cuts, kind.points_pad, LANES), jnp.int32),
        pltpu.VMEM((width, kind.cuts, kind.points_pad, LANES), jnp.int32),
        pltpu.VMEM((width, 8, LANES), jnp.int32),
        pltpu.VMEM((width, 8, LANES), jnp.int32),
        pltpu.VMEM((width, 8, LANES), jnp.int32),
        pltpu.VMEM((width, 8, LANES), jnp.int32),
        pltpu.VMEM((width, kind.blocks, 8, LANES), F32),
        pltpu.VMEM((width, kind.blocks, 8, LANES), F32),
        pltpu.VMEM((width, kind.blocks, 8, LANES), F32),
        pltpu.VMEM((width + 2, 8, LANES), F32),
        pltpu.VMEM((unroll, kind.cuts, 8 * kind.points_pad, LANES), F32),
    ]


class Refs:
    pass


def window_base(index, count, width):
    return jnp.clip(index - STEPS, 0, count - width)


def sim_kernel(kind, width, unroll, offsets, spare, *refs):
    sub = lax.axis_index("sub")
    count = lax.axis_size("sub")
    chips = count // 2
    n_bufs = 2 * len(offsets)
    bufs, refs = refs[:n_bufs], refs[n_bufs:]
    lhs_in, lhs_out, refs = refs[0], refs[1], refs[2:]
    layers, refs = refs[: kind.sources], refs[kind.sources :]
    final, refs = refs[0], refs[1:]
    emit = None
    if not kind.sources:
        emit, refs = refs[0], refs[1:]
    refs = refs[spare:]
    buf, sem, refs = refs[0], refs[1], refs[2:]
    s = Refs()
    for name, ref in zip(SCRATCH, refs, strict=True):
        setattr(s, name, ref)
    base = window_base(sub, count, width)
    if width < count:
        buf[...] = jnp.zeros(buf.shape, F32)
    copies = []
    for number, offset in enumerate(offsets):
        for other in range(2):
            chip = lax.rem(sub // 2 - offset + chips, chips)
            core = lax.rem(sub, 2)
            slot = chip * 2 + (core if other == 0 else 1 - core) - base
            at = 2 * number + other
            inside = jnp.logical_and(slot >= 0, slot < width)
            slot = jnp.clip(slot, 0, width - 1)
            copy = pltpu.make_async_copy(bufs[at], buf.at[slot], sem.at[at])
            copies.append((inside, copy))
    for phase in ("start", "wait"):
        for inside, copy in copies:
            if width < count:
                pl.when(inside)(getattr(copy, phase))
            else:
                getattr(copy, phase)()
    simulate(kind, width, unroll, buf, lhs_in, lhs_out, layers, emit, s)
    for block in range(kind.blocks):
        for c in range(3):
            final[0, c, :, block * LANES : (block + 1) * LANES] = s.now[
                sub - base, block, c : c + 1, :
            ]


def run_sim(kind, width, unroll, offsets, bufs, tables, layers, spare):
    out_shape = [jax.ShapeDtypeStruct((1, 3, 1, kind.count), F32)]
    if not kind.sources:
        out_shape.append(jax.ShapeDtypeStruct((STEPS, width, 4, LANES), F32))
    vmem = pl.BlockSpec(memory_space=pltpu.VMEM)
    hbm = pl.BlockSpec(memory_space=pl.ANY)
    return pl.pallas_call(
        functools.partial(sim_kernel, kind, width, unroll, offsets, len(spare)),
        out_shape=out_shape + spare,
        in_specs=[hbm] * len(bufs) + [vmem] * (2 + len(layers)),
        out_specs=[vmem] * len(out_shape) + [hbm] * len(spare),
        scratch_shapes=[
            pltpu.VMEM((width, kind.rows, LANES), F32),
            pltpu.SemaphoreType.DMA((len(bufs),)),
        ]
        + scratch_of(kind, width, unroll),
        name="site_sim" if kind.sources else "reg_sim",
    )(*bufs, *tables, *layers)


def blank_kernel(final, *rest):
    final[...] = jnp.zeros(final.shape, F32)


def gather_window(value, groups, offsets, count):
    chips = count // 2
    low, high = groups

    def moved(array, chip_shift, flip):
        route = []
        for grp in range(low, high):
            for index in range(count):
                chip, core = divmod(index, 2)
                target = ((chip + chip_shift) % chips) * 2 + (core ^ flip)
                route.append((grp * count + index, grp * count + target))
        return lax.ppermute(array, ("grp", "sub"), route)

    by_chip = [value if shift % chips == 0 else moved(value, shift, 0) for shift in offsets]
    result = []
    for array in by_chip:
        result += [array, moved(array, 0, 1)]
    return result


def shards(
    reg_disp, reg_vel, site_disp, site_vel, reg_nodes, site_nodes, reg_coefs, site_coefs,
    reg_table, site_table, reg_minv, site_minv, reg_send, reg_recv, site_send, site_recv,
    slot_fill, layer_src, layer_fill, layer_dst, layer_stiff,
):
    group_count = lax.axis_size("grp")
    count = lax.axis_size("sub")
    site_groups = group_count // 4
    reg_groups = 3 * site_groups
    reg = Kind(reg_nodes, reg_coefs, reg_disp, 0)
    site = Kind(site_nodes, site_coefs, site_disp, 3)
    unroll = min(UNROLL, count)
    width = min(count, up_to(2 * STEPS + 1, unroll))
    chips = count // 2
    reach = STEPS // 2
    if 2 * reach + 1 >= chips:
        offsets = tuple(range(chips))
    else:
        offsets = tuple(range(-reach, reach + 1))
    is_site = lax.axis_index("grp") >= reg_groups
    vmem = pl.BlockSpec(memory_space=pltpu.VMEM)
    hbm = pl.BlockSpec(memory_space=pl.ANY)
    site_spare = [jax.ShapeDtypeStruct((site.rows, LANES), F32)] * (2 * len(offsets)) + [
        jax.ShapeDtypeStruct((3 * site.quads_pad, site.depth_in), BF16),
        jax.ShapeDtypeStruct((site.points_pad, site.depth_out), BF16),
    ]

    def regional():
        buf, *tables = pack(
            reg, reg_disp, reg_vel, reg_nodes, reg_coefs, reg_minv, reg_send, reg_recv,
            slot_fill, layer_src, layer_fill, reg_table,
        )
        bufs = gather_window(buf, (0, reg_groups), offsets, count)
        final, layer, *spare = run_sim(reg, width, unroll, offsets, bufs, tables, (), site_spare)
        return (final, layer, *spare)

    def prepare_site():
        buf, *tables = pack(
            site, site_disp, site_vel, site_nodes, site_coefs, site_minv, site_send, site_recv,
            slot_fill, layer_dst, layer_stiff, site_table,
        )
        bufs = gather_window(buf, (reg_groups, group_count), offsets, count)
        final, layer = pl.pallas_call(
            blank_kernel,
            out_shape=[
                jax.ShapeDtypeStruct((1, 3, 1, reg.count), F32),
                jax.ShapeDtypeStruct((STEPS, width, 4, LANES), F32),
            ],
            out_specs=[vmem, hbm],
            name="blank",
        )()
        return (final, layer, *bufs, *tables)

    reg_final, layer_out, *rest = lax.cond(is_site, prepare_site, regional)
    site_bufs, site_tables = rest[:-2], rest[-2:]
    layers = [
        lax.ppermute(
            layer_out,
            "grp",
            [(m * site_groups + i, reg_groups + i) for i in range(site_groups)],
        )
        for m in range(3)
    ]

    def run_site():
        return run_sim(site, width, unroll, offsets, site_bufs, site_tables, layers, [])[0]

    def no_site():
        return jnp.zeros((1, 3, 1, site.count), F32)

    site_final = lax.cond(is_site, run_site, no_site)
    return jnp.transpose(reg_final, (0, 2, 1, 3)), jnp.transpose(site_final, (0, 2, 1, 3))


def solution(mesh):
    def spec(rank):
        return P("grp", "sub", *([None] * (rank - 2)))

    ranks = (4, 4, 4, 4, 4, 4, 6, 6, 0, 0, 3, 3, 4, 4, 4, 4, 3, 3, 2, 4, 4)
    return jax.shard_map(
        shards,
        mesh=mesh,
        in_specs=tuple(spec(rank) if rank else P() for rank in ranks),
        out_specs=(spec(4), spec(4)),
        check_vma=False,
    )
```

time: 149 us -> 103 us (0.69); the launches traced: 146 us -> 102 us
  Pallas kernels: 66.7 us -> 43.1 us
  local copies, waits for them, and re-layouts: 13.4 us -> 1.99 us
  starting transfers between devices: 27 us -> 22.8 us
  waiting for transfers between devices: 36.7 us -> 32.8 us
    pallas_call x3, Pallas kernels: 66.7 us -> 43.1 us  [the longest x1 40.8 us: run_sim(): pl.pallas_call(functools.partial(sim_kernel, kind, width, unroll, offsets...]
    unnamed x70 -> x10, local copies, waits for them, and re-layouts: 10.9 us -> 1.29 us
    ppermute x3, waiting for transfers between devices: 36.3 us -> 27.9 us  [shards(): lax.ppermute(layer_out, 'grp', [(m * site_groups + i, reg_groups + i) for...]
    ppermute x14 -> x7, waiting for transfers between devices: 0.47 us -> 4.93 us  [moved(): return lax.ppermute(array, ('grp', 'sub'), route)]
    ppermute x14 -> x7, starting transfers between devices: 23.1 us -> 19 us  [moved(): return lax.ppermute(array, ('grp', 'sub'), route)]
    pad x3 -> x0, local copies, waits for them, and re-layouts: 1.84 us -> none  [the longest x2 1.22 us: tables_of(): second = jnp.pad(second, ((0, 0), (0, kind.depth_out - second.shape[1])))]
  transfers between devices with their start and end apart: 17 -> 10, of which waited for: 2 -> 4; matrix products, arithmetic and copies ran while one was open for 3% -> 0% of each run, Pallas kernels for 1% -> 1%
where the time goes in v2:
time: 103 us; the launch traced here: 102 us
  Pallas kernels  43.1 us (42%)
  waiting for transfers between devices  32.8 us (32%)
  starting transfers between devices  22.8 us (22%)
  local copies, waits for them, and re-layouts  1.99 us (2%)
    pallas_call x1, Pallas kernels, run_sim(): pl.pallas_call(functools.partial(sim_kernel, kind, width, unroll, offsets...  40.8 us
    ppermute x3, waiting for transfers between devices, shards(): lax.ppermute(layer_out, 'grp', [(m * site_groups + i, reg_groups + i) for...  27.9 us
    ppermute x7, starting transfers between devices, moved(): return lax.ppermute(array, ('grp', 'sub'), route)  19 us
    ppermute x7, waiting for transfers between devices, moved(): return lax.ppermute(array, ('grp', 'sub'), route)  4.93 us
    ppermute x3, starting transfers between devices, shards(): lax.ppermute(layer_out, 'grp', [(m * site_groups + i, reg_groups + i) for...  3.86 us
  transfers between devices with their start and end apart: 10, of which 4 were waited for; matrix products, arithmetic and copies ran while one was open for 0% of the time, Pallas kernels for 1%

profile of v2, /device:TPU:6, one launch (start us, length us, event | category | flops | bytes accessed | tf_op | source)
XLA Modules:
  0.0 101.6 jit_solution(6666735672092544177)
XLA Ops:
  0.7 0.7 copy-done.9
  1.3 0.0 copy-done.18
  1.4 27.1 %conditional.2 = (f32[8,8,4,128]{3,2,1,0:T(4,128)S(1)}, f32[280,128]{1,0:T(8,128)}, f32[280,128]{1,0:T(8,128)}, f32[280,128]{1,0:T(8,128)}, f32[280,128]{1,0:T(8...) conditional(s32[]{:T(128)} %convert_element_type.4, ...), branch_computations={%region_0.0_spmd, %region_1.0_spmd} | conditional | bytes 4093828 | solution.py:584
  1.4 0.7 copy-done.7
  2.1 0.0 copy-done.20
  2.1 1.8 %site_pack.1 = (f32[280,128]{1,0:T(8,128)}, bf16[72,128]{1,0:T(8,128)(2,1)S(1)}, bf16[40,224]{1,0:T(8,128)(2,1)S(1)}) custom-call(f32[1,3,1,1536]{3,2,1,0:T(1,128)} %bitcast.31, f32[1,3,1,1536]{3,2,1,0:T(1,128)} %bitcast.32, s32[1,35,1,128]{3,2,1,0:T(1,128)} %bitcast.34, f32[1,1,3,3,24,128]{5,4,3,2,1,0:T(8,128)} %get-tuple-element.216.refs_3_, ...), custom_call_target="tpu_custom_call" | custom-call | tf_op jit(solution)/shard_map/cond/branch_1_fun/site_pack/pallas_call | solution.py:125
  3.9 5.5 %collective-permute-start.12 = (f32[280,128]{1,0:T(8,128)}, f32[280,128]{1,0:T(8,128)}, u32[]{:S(2)}, u32[]{:S(2)}) collective-permute-start(f32[280,128]{1,0:T(8,128)} %get-tuple-element.258), channel_id=1, source_target_pairs={{24,30},{25,31},{26,24},{27,25},{28,26},{29,27},{30,28},{31,29}} | collective-permute-start | bytes 430088 | tf_op jit(solution)/shard_map/cond/branch_1_fun/ppermute | solution.py:522
  9.4 1.9 %collective-permute-start.10 = (f32[280,128]{1,0:T(8,128)}, f32[280,128]{1,0:T(8,128)}, u32[]{:S(2)}, u32[]{:S(2)}) collective-permute-start(f32[280,128]{1,0:T(8,128)} %get-tuple-element.258), channel_id=1, source_target_pairs={{24,28},{25,29},{26,30},{27,31},{28,24},{29,25},{30,26},{31,27}} | collective-permute-start | bytes 430088 | tf_op jit(solution)/shard_map/cond/branch_1_fun/ppermute | solution.py:522
  11.3 2.9 %collective-permute-start.8 = (f32[280,128]{1,0:T(8,128)}, f32[280,128]{1,0:T(8,128)}, u32[]{:S(2)}, u32[]{:S(2)}) collective-permute-start(f32[280,128]{1,0:T(8,128)} %get-tuple-element.258), channel_id=1, source_target_pairs={{24,26},{25,27},{26,28},{27,29},{28,30},{29,31},{30,24},{31,25}} | collective-permute-start | bytes 430088 | tf_op jit(solution)/shard_map/cond/branch_1_fun/ppermute | solution.py:522
  14.2 1.9 %collective-permute-start.7 = (f32[280,128]{1,0:T(8,128)}, f32[280,128]{1,0:T(8,128)}, u32[]{:S(2)}, u32[]{:S(2)}) collective-permute-start(f32[280,128]{1,0:T(8,128)} %get-tuple-element.258), channel_id=1, source_target_pairs={{24,25},{25,24},{26,27},{27,26},{28,29},{29,28},{30,31},{31,30}} | collective-permute-start | bytes 430088 | tf_op jit(solution)/shard_map/cond/branch_1_fun/ppermute | solution.py:522
  16.2 2.4 %collective-permute-start.13 = (f32[280,128]{1,0:T(8,128)}, f32[280,128]{1,0:T(8,128)}, u32[]{:S(2)}, u32[]{:S(2)}) collective-permute-start(f32[280,128]{1,0:T(8,128)} %collective-permute-done.12), channel_id=1, source_target_pairs={{24,25},{25,24},{26,27},{27,26},{28,29},{29,28},{30,31},{31,30}} | collective-permute-start | bytes 430088 | tf_op jit(solution)/shard_map/cond/branch_1_fun/ppermute | solution.py:522
  18.6 4.2 %collective-permute-done.10 = f32[280,128]{1,0:T(8,128)} collective-permute-done((f32[280,128]{1,0:T(8,128)}, f32[280,128]{1,0:T(8,128)}, u32[]{:S(2)}, u32[]{:S(2)}) %collective-permute-start.10) | collective-permute-done | bytes 143392 | tf_op jit(solution)/shard_map/cond/branch_1_fun/ppermute | solution.py:522
  22.8 1.9 %collective-permute-start.11 = (f32[280,128]{1,0:T(8,128)}, f32[280,128]{1,0:T(8,128)}, u32[]{:S(2)}, u32[]{:S(2)}) collective-permute-start(f32[280,128]{1,0:T(8,128)} %collective-permute-done.10), channel_id=1, source_target_pairs={{24,25},{25,24},{26,27},{27,26},{28,29},{29,28},{30,31},{31,30}} | collective-permute-start | bytes 430088 | tf_op jit(solution)/shard_map/cond/branch_1_fun/ppermute | solution.py:522
  24.7 2.4 %collective-permute-start.9 = (f32[280,128]{1,0:T(8,128)}, f32[280,128]{1,0:T(8,128)}, u32[]{:S(2)}, u32[]{:S(2)}) collective-permute-start(f32[280,128]{1,0:T(8,128)} %collective-permute-done.8), channel_id=1, source_target_pairs={{24,25},{25,24},{26,27},{27,26},{28,29},{29,28},{30,31},{31,30}} | collective-permute-start | bytes 430088 | tf_op jit(solution)/shard_map/cond/branch_1_fun/ppermute | solution.py:522
  27.1 0.6 blank.1
  27.7 0.7 collective-permute-done.9
  28.5 1.3 %collective-permute-start.16 = (f32[8,8,4,128]{3,2,1,0:T(4,128)S(1)}, f32[8,8,4,128]{3,2,1,0:T(4,128)S(1)}, u32[]{:S(2)}, u32[]{:S(2)}) collective-permute-start(f32[8,8,4,128]{3,2,1,0:T(4,128)S(1)} %get-tuple-element.179), channel_id=1, source_target_pairs={{16,24},{17,25},{18,26},{19,27},{20,28},{21,29},{22,30},{23,31}} | collective-permute-start | bytes 393224 | tf_op jit(solution)/shard_map/ppermute | solution.py:587
  29.7 1.3 %collective-permute-start.15 = (f32[8,8,4,128]{3,2,1,0:T(4,128)S(1)}, f32[8,8,4,128]{3,2,1,0:T(4,128)S(1)}, u32[]{:S(2)}, u32[]{:S(2)}) collective-permute-start(f32[8,8,4,128]{3,2,1,0:T(4,128)S(1)} %get-tuple-element.179), channel_id=1, source_target_pairs={{8,24},{9,25},{10,26},{11,27},{12,28},{13,29},{14,30},{15,31}} | collective-permute-start | bytes 393224 | tf_op jit(solution)/shard_map/ppermute | solution.py:587
  31.0 1.3 %collective-permute-start.14 = (f32[8,8,4,128]{3,2,1,0:T(4,128)S(1)}, f32[8,8,4,128]{3,2,1,0:T(4,128)S(1)}, u32[]{:S(2)}, u32[]{:S(2)}) collective-permute-start(f32[8,8,4,128]{3,2,1,0:T(4,128)S(1)} %get-tuple-element.179), channel_id=1, source_target_pairs={{0,24},{1,25},{2,26},{3,27},{4,28},{5,29},{6,30},{7,31}} | collective-permute-start | bytes 393224 | tf_op jit(solution)/shard_map/ppermute | solution.py:587
  32.3 24.4 %collective-permute-done.16 = f32[8,8,4,128]{3,2,1,0:T(4,128)S(1)} collective-permute-done((f32[8,8,4,128]{3,2,1,0:T(4,128)S(1)}, f32[8,8,4,128]{3,2,1,0:T(4,128)S(1)}, u32[]{:S(2)}, u32[]{:S(2)}) %collective-permute-start.16) | collective-permute-done | bytes 131104 | tf_op jit(solution)/shard_map/ppermute | solution.py:587
  56.8 3.5 %collective-permute-done.15 = f32[8,8,4,128]{3,2,1,0:T(4,128)S(1)} collective-permute-done((f32[8,8,4,128]{3,2,1,0:T(4,128)S(1)}, f32[8,8,4,128]{3,2,1,0:T(4,128)S(1)}, u32[]{:S(2)}, u32[]{:S(2)}) %collective-permute-start.15) | collective-permute-done | bytes 131104 | tf_op jit(solution)/shard_map/ppermute | solution.py:587
  60.2 40.8 %conditional.3 = (f32[1,1,3,1536]{3,1,2,0:T(1,128)S(1)}) conditional(s32[]{:T(128)} %convert_element_type.4, () %tuple.31, (f32[280,128]{1,0:T(8,128)}, f32[280,128]{1,0:T(8,128)}, f32[280,128]{1,0:T(8,128)}, f32[280,128]{1,0:T(8,128)}, f32[280,128]{1,0:T(8,128)}, /*index=5*/f32[280,128]{1,0:T(8,128)}, f32[280,128]{1,0:T(8,128)}, ...), branch_computations={%region_2.0_spmd, %region_3.0_spmd} | conditional | bytes 18444 | solution.py:601
  60.2 40.8 %site_sim.1 = f32[1,3,1,1536]{3,2,1,0:T(1,128)S(1)} custom-call(f32[280,128]{1,0:T(8,128)} %get-tuple-element.141.refs_0_, f32[280,128]{1,0:T(8,128)} %get-tuple-element.142.refs_1_, f32[280,128]{1,0:T(8,128)} %get-tuple-element.143.refs_2_, f32[280,128]{1,0:T(8,128)} %get-tuple-element.144.refs_3_, f32[280,128]{1,0:T(8,128)} %get-tuple-element.145.refs_4_, ...), custom_call_target="tpu_custom_call" | custom-call | tf_op jit(solution)/shard_map/cond/branch_1_fun/site_sim/pallas_call | solution.py:493
  101.0 0.6 copy-done.8
  (21 shorter events, 0.1 us)
Async XLA Ops:
  0.6 0.7 copy-start.9
  0.7 0.7 copy-start.15
  0.7 0.7 copy-start.14
  0.7 0.7 copy-start.18
  1.4 0.7 copy-start.7
  1.4 0.7 copy-start.11
  1.4 0.7 copy-start.16
  1.4 0.7 copy-start.21
  1.4 0.7 copy-start.20
  3.9 12.3 %collective-permute-start.12 = (f32[280,128]{1,0:T(8,128)}, f32[280,128]{1,0:T(8,128)}, u32[]{:S(2)}, u32[]{:S(2)}) collective-permute-start(f32[280,128]{1,0:T(8,128)} %get-tuple-element.258), channel_id=1, source_target_pairs={{24,30},{25,31},{26,24},{27,25},{28,26},{29,27},{30,28},{31,29}} | collective-permute-start | bytes 430088 | tf_op jit(solution)/shard_map/cond/branch_1_fun/ppermute | solution.py:522
  9.4 13.4 %collective-permute-start.10 = (f32[280,128]{1,0:T(8,128)}, f32[280,128]{1,0:T(8,128)}, u32[]{:S(2)}, u32[]{:S(2)}) collective-permute-start(f32[280,128]{1,0:T(8,128)} %get-tuple-element.258), channel_id=1, source_target_pairs={{24,28},{25,29},{26,30},{27,31},{28,24},{29,25},{30,26},{31,27}} | collective-permute-start | bytes 430088 | tf_op jit(solution)/shard_map/cond/branch_1_fun/ppermute | solution.py:522
  11.3 13.4 %collective-permute-start.8 = (f32[280,128]{1,0:T(8,128)}, f32[280,128]{1,0:T(8,128)}, u32[]{:S(2)}, u32[]{:S(2)}) collective-permute-start(f32[280,128]{1,0:T(8,128)} %get-tuple-element.258), channel_id=1, source_target_pairs={{24,26},{25,27},{26,28},{27,29},{28,30},{29,31},{30,24},{31,25}} | collective-permute-start | bytes 430088 | tf_op jit(solution)/shard_map/cond/branch_1_fun/ppermute | solution.py:522
  14.2 13.5 %collective-permute-start.7 = (f32[280,128]{1,0:T(8,128)}, f32[280,128]{1,0:T(8,128)}, u32[]{:S(2)}, u32[]{:S(2)}) collective-permute-start(f32[280,128]{1,0:T(8,128)} %get-tuple-element.258), channel_id=1, source_target_pairs={{24,25},{25,24},{26,27},{27,26},{28,29},{29,28},{30,31},{31,30}} | collective-permute-start | bytes 430088 | tf_op jit(solution)/shard_map/cond/branch_1_fun/ppermute | solution.py:522
  16.2 11.6 %collective-permute-start.13 = (f32[280,128]{1,0:T(8,128)}, f32[280,128]{1,0:T(8,128)}, u32[]{:S(2)}, u32[]{:S(2)}) collective-permute-start(f32[280,128]{1,0:T(8,128)} %collective-permute-done.12), channel_id=1, source_target_pairs={{24,25},{25,24},{26,27},{27,26},{28,29},{29,28},{30,31},{31,30}} | collective-permute-start | bytes 430088 | tf_op jit(solution)/shard_map/cond/branch_1_fun/ppermute | solution.py:522
  22.8 4.9 %collective-permute-start.11 = (f32[280,128]{1,0:T(8,128)}, f32[280,128]{1,0:T(8,128)}, u32[]{:S(2)}, u32[]{:S(2)}) collective-permute-start(f32[280,128]{1,0:T(8,128)} %collective-permute-done.10), channel_id=1, source_target_pairs={{24,25},{25,24},{26,27},{27,26},{28,29},{29,28},{30,31},{31,30}} | collective-permute-start | bytes 430088 | tf_op jit(solution)/shard_map/cond/branch_1_fun/ppermute | solution.py:522
  24.7 3.7 %collective-permute-start.9 = (f32[280,128]{1,0:T(8,128)}, f32[280,128]{1,0:T(8,128)}, u32[]{:S(2)}, u32[]{:S(2)}) collective-permute-start(f32[280,128]{1,0:T(8,128)} %collective-permute-done.8), channel_id=1, source_target_pairs={{24,25},{25,24},{26,27},{27,26},{28,29},{29,28},{30,31},{31,30}} | collective-permute-start | bytes 430088 | tf_op jit(solution)/shard_map/cond/branch_1_fun/ppermute | solution.py:522
  28.5 28.3 %collective-permute-start.16 = (f32[8,8,4,128]{3,2,1,0:T(4,128)S(1)}, f32[8,8,4,128]{3,2,1,0:T(4,128)S(1)}, u32[]{:S(2)}, u32[]{:S(2)}) collective-permute-start(f32[8,8,4,128]{3,2,1,0:T(4,128)S(1)} %get-tuple-element.179), channel_id=1, source_target_pairs={{16,24},{17,25},{18,26},{19,27},{20,28},{21,29},{22,30},{23,31}} | collective-permute-start | bytes 393224 | tf_op jit(solution)/shard_map/ppermute | solution.py:587
  29.7 30.5 %collective-permute-start.15 = (f32[8,8,4,128]{3,2,1,0:T(4,128)S(1)}, f32[8,8,4,128]{3,2,1,0:T(4,128)S(1)}, u32[]{:S(2)}, u32[]{:S(2)}) collective-permute-start(f32[8,8,4,128]{3,2,1,0:T(4,128)S(1)} %get-tuple-element.179), channel_id=1, source_target_pairs={{8,24},{9,25},{10,26},{11,27},{12,28},{13,29},{14,30},{15,31}} | collective-permute-start | bytes 393224 | tf_op jit(solution)/shard_map/ppermute | solution.py:587
  31.0 29.2 %collective-permute-start.14 = (f32[8,8,4,128]{3,2,1,0:T(4,128)S(1)}, f32[8,8,4,128]{3,2,1,0:T(4,128)S(1)}, u32[]{:S(2)}, u32[]{:S(2)}) collective-permute-start(f32[8,8,4,128]{3,2,1,0:T(4,128)S(1)} %get-tuple-element.179), channel_id=1, source_target_pairs={{0,24},{1,25},{2,26},{3,27},{4,28},{5,29},{6,30},{7,31}} | collective-permute-start | bytes 393224 | tf_op jit(solution)/shard_map/ppermute | solution.py:587
  101.0 0.6 copy-start.8

commit v3 on v2

--- a/solution.py
+++ b/solution.py
@@ -34,6 +34,7 @@
         self.depth_out = up_to(9 * self.quads_pad, 16)
         self.chunks = self.points * self.cuts
         self.sources = sources
+        self.dense = self.blocks >= 8 and self.blocks % 4 == 0
         self.tiles = up_to(self.chunks, 4) // 4
         self.extra = 2 + sources
         self.extra_tiles = up_to(self.extra, 4) // 4
@@ -145,10 +146,10 @@
     return value.astype(BF16).astype(F32)
 
 
-def simulate(kind, width, unroll, buf, lhs_in, lhs_out, layers, emit, s):
+def simulate(kind, width, unroll, own, mode, buf, lhs_in, lhs_out, layers, emit, begun, s):
     points, cuts, blocks = kind.points, kind.cuts, kind.blocks
     quads_pad = kind.quads_pad
-    half_rows = 8 * kind.blocks_pad
+    half_rows = 6 * blocks if kind.dense else 8 * kind.blocks_pad
     row8 = lax.broadcasted_iota(jnp.int32, (8, LANES), 0)
     low_half = row8 < 4
     row16 = lax.broadcasted_iota(jnp.int32, (16, LANES), 0)
@@ -231,11 +232,48 @@
                 ref[q, block, 4:7, :] = value
         return 0
 
-    lax.fori_loop(0, width, setup, 0)
+    def setup_pair(pair, _):
+        for k in range(2):
+            setup(2 * pair + k, 0)
+        return 0
+
+    lax.fori_loop(0, width // 2, setup_pair, 0)
     for lane in range(unroll):
         s.parts[lane] = jnp.zeros(s.parts.shape[1:], F32)
+        s.turn[lane] = jnp.zeros(s.turn.shape[1:], F32)
     s.sends[0] = zero8
     s.sends[width + 1] = zero8
+
+    slabs = half_rows // 8
+    slab_rows = [
+        [divmod(8 * slab + row, blocks) for row in range(8)] for slab in range(slabs)
+    ]
+    slab_ids = {}
+    for slab in range(slabs if kind.dense else 0):
+        number = slab_rows[slab][0][1]
+        if number not in slab_ids:
+            slab_ids[number] = lax.rem(row8 + number, blocks).astype(F32)
+
+    def dense_rows(q, chunk, rows):
+        held = jnp.broadcast_to(s.block_of[q, chunk : chunk + 1, :], (8, LANES))
+        hits = {number: held == ids for number, ids in slab_ids.items()}
+        result = []
+        for slab in range(slabs):
+            places = slab_rows[slab]
+            value = jnp.broadcast_to(rows[places[0][0]], (8, LANES))
+            if places[7][0] != places[0][0]:
+                other = jnp.broadcast_to(rows[places[7][0]], (8, LANES))
+                value = jnp.where(row8 < places.index((places[7][0], 0)), value, other)
+            result.append(jnp.where(hits[places[0][1]], value, 0.0))
+        return result
+
+    def dense_spread(q, first, values):
+        parts = [dense_rows(q, first + number, rows) for number, rows in enumerate(values)]
+        parts += [[zero8] * slabs] * (4 - len(values))
+        columns = [
+            jnp.concatenate(parts[k] + parts[k + 2], axis=0).astype(BF16) for k in range(2)
+        ]
+        return jnp.concatenate(columns, axis=1)
 
     def spread(q, first, values):
         blank = jnp.zeros((half_rows, LANES), BF16)
@@ -257,18 +295,34 @@
     def scattered(q, first, rows_from, get, count):
         total = None
         for at in range(0, count, 4):
-            left = spread(q, first + at, [get(k) for k in range(at, min(at + 4, count))])
+            build = dense_spread if kind.dense else spread
+            left = build(q, first + at, [get(k) for k in range(at, min(at + 4, count))])
             rows = slice(rows_from + at * 64, rows_from + at * 64 + 256)
             right = jnp.concatenate([s.onehot[q, half, rows, :] for half in range(2)], axis=1)
             term = jnp.dot(left, right, preferred_element_type=F32)
             total = term if total is None else total + term
         return total
 
-    def fold(total, block):
-        rows = slice(block * 8, block * 8 + 8)
-        other = slice(half_rows + block * 8, half_rows + block * 8 + 8)
-        value = total[rows, 0:LANES] + total[other, LANES : 2 * LANES]
-        return value + pltpu.roll(value, 4, 0)
+    def fold(total, lane):
+        if kind.dense:
+            value = total[0:half_rows, 0:LANES] + total[half_rows:, LANES:]
+            for c in range(3):
+                at = (c + 3) * blocks
+                whole = value[c * blocks : (c + 1) * blocks, :] + value[at : at + blocks, :]
+                for copy in (0, 4):
+                    at = (c + copy) * kind.blocks_pad
+                    s.turn[lane, at : at + blocks, :] = whole
+            return [
+                s.turn[lane, pl.ds(block, 8, stride=kind.blocks_pad), :]
+                for block in range(blocks)
+            ]
+        folded = []
+        for block in range(blocks):
+            rows = slice(block * 8, block * 8 + 8)
+            other = slice(half_rows + block * 8, half_rows + block * 8 + 8)
+            value = total[rows, 0:LANES] + total[other, LANES : 2 * LANES]
+            folded.append(value + pltpu.roll(value, 4, 0))
+        return folded
 
     def choose(found, bits):
         for bit in bits:
@@ -345,24 +399,30 @@
             high = high_part(value)
             size = kind.points_pad
             s.parts[lane, cut, c * size : (c + 1) * size, :] = high
-            s.parts[lane, cut, (c + 4) * size : (c + 5) * size, :] = value - high
+            at = (c + (3 if kind.dense else 4)) * size
+            s.parts[lane, cut, at : at + size, :] = value - high
         def entry(chunk):
             cut, p = divmod(chunk, points)
+            if kind.dense:
+                rows = [part * kind.points_pad + p for part in range(6)]
+                return [s.parts[lane, cut, row : row + 1, :] for row in rows]
             return s.parts[lane, cut, pl.ds(p, 8, stride=kind.points_pad), :]
 
         total = scattered(q, 0, 0, entry, kind.chunks)
-        folded = [fold(total, block) for block in range(blocks)]
+        folded = fold(total, lane)
         for block in range(blocks):
             s.force[q, block] = folded[block]
         s.sends[q + 1] = pick(lambda block: folded[block], s.send_lo[q], s.send_hi[q])
 
     def split8(value):
         high = high_part(value)
+        if kind.dense:
+            return [part[c : c + 1, :] for part in (high, value - high) for c in range(3)]
         return jnp.where(low_half, high, value - high)
 
-    def update(q, lane, step):
-        lower = s.sends[q]
-        upper = s.sends[q + 2]
+    def update(q, lane, step, forces, sends):
+        lower = sends[q]
+        upper = sends[q + 2]
         values = [
             jnp.where(low_half, pltpu.roll(lower, 4, 0), lower),
             jnp.where(low_half, upper, pltpu.roll(upper, 4, 0)),
@@ -374,11 +434,12 @@
         total = scattered(
             q, 4 * kind.tiles, main_rows, lambda k: split8(values[k]), len(values)
         )
+        folded = fold(total, lane)
         after = []
         for block in range(blocks):
             now = s.now[q, block]
             scale = buf[q, kind.at_minv + block : kind.at_minv + block + 1, :]
-            whole = s.force[q, block] + fold(total, block)
+            whole = forces[q, block] + folded[block]
             value = 2.0 * now - s.before[q, block] + scale * whole
             s.before[q, block] = now
             s.now[q, block] = value
@@ -387,27 +448,47 @@
             picked = pick(lambda block: after[block], s.layer_lo[q], s.layer_hi[q])
             emit[step, q] = picked[0:4]
 
-    def one_step(step, _):
+    def all_forces():
         def forces(group, _):
             for lane in range(unroll):
                 force(group * unroll + lane, lane)
             return 0
 
+        lax.fori_loop(0, width // unroll, forces, 0)
+
+    def all_updates(step, forces, sends):
         def updates(group, _):
             for lane in range(unroll):
-                update(group * unroll + lane, lane, step)
+                update(group * unroll + lane, lane, step, forces, sends)
             return 0
 
-        lax.fori_loop(0, width // unroll, forces, 0)
         lax.fori_loop(0, width // unroll, updates, 0)
+
+    def one_step(step, _):
+        all_forces()
+        all_updates(step, s.force, s.sends)
         return 0
 
-    lax.fori_loop(0, STEPS, one_step, 0)
+    if mode == "first":
+        all_forces()
+        begun[0][...] = s.force[...]
+        begun[1][...] = s.sends[...]
+        return
+    done = 0
+    if mode == "rest":
+        all_updates(0, *begun)
+        done = 1
+    lax.fori_loop(done, STEPS - 1, one_step, 0)
+    span = min(4, unroll)
+    first = jnp.clip(own - 1, 0, width - span)
+    for lane in range(span):
+        force(first + lane, lane)
+    update(own, 0, STEPS - 1, s.force, s.sends)
 
 
 SCRATCH = (
     "onehot", "block_of", "coefs", "lo", "hi", "send_lo", "send_hi", "layer_lo", "layer_hi",
-    "now", "before", "force", "sends", "parts",
+    "now", "before", "force", "sends", "parts", "turn",
 )
 
 
@@ -428,6 +509,7 @@
         pltpu.VMEM((width, kind.blocks, 8, LANES), F32),
         pltpu.VMEM((width + 2, 8, LANES), F32),
         pltpu.VMEM((unroll, kind.cuts, 8 * kind.points_pad, LANES), F32),
+        pltpu.VMEM((unroll, 8 * kind.blocks_pad, LANES), F32),
     ]
 
 
@@ -439,17 +521,21 @@
     return jnp.clip(index - STEPS, 0, count - width)
 
 
-def sim_kernel(kind, width, unroll, offsets, spare, *refs):
+def sim_kernel(kind, width, unroll, offsets, mode, spare, *refs):
     sub = lax.axis_index("sub")
     count = lax.axis_size("sub")
     chips = count // 2
-    n_bufs = 2 * len(offsets)
-    bufs, refs = refs[:n_bufs], refs[n_bufs:]
+    bufs, refs = refs[:2], refs[2:]
     lhs_in, lhs_out, refs = refs[0], refs[1], refs[2:]
-    layers, refs = refs[: kind.sources], refs[kind.sources :]
-    final, refs = refs[0], refs[1:]
-    emit = None
-    if not kind.sources:
+    layers = begun = emit = final = None
+    if mode == "rest":
+        layers, refs = refs[: kind.sources], refs[kind.sources :]
+        begun, refs = refs[:2], refs[2:]
+    if mode == "first":
+        begun, refs = refs[:2], refs[2:]
+    else:
+        final, refs = refs[0], refs[1:]
+    if mode == "all":
         emit, refs = refs[0], refs[1:]
     refs = refs[spare:]
     buf, sem, refs = refs[0], refs[1], refs[2:]
@@ -468,7 +554,7 @@
             at = 2 * number + other
             inside = jnp.logical_and(slot >= 0, slot < width)
             slot = jnp.clip(slot, 0, width - 1)
-            copy = pltpu.make_async_copy(bufs[at], buf.at[slot], sem.at[at])
+            copy = pltpu.make_async_copy(bufs[other].at[number], buf.at[slot], sem.at[at])
             copies.append((inside, copy))
     for phase in ("start", "wait"):
         for inside, copy in copies:
@@ -476,7 +562,11 @@
                 pl.when(inside)(getattr(copy, phase))
             else:
                 getattr(copy, phase)()
-    simulate(kind, width, unroll, buf, lhs_in, lhs_out, layers, emit, s)
+    simulate(
+        kind, width, unroll, sub - base, mode, buf, lhs_in, lhs_out, layers, emit, begun, s
+    )
+    if final is None:
+        return
     for block in range(kind.blocks):
         for c in range(3):
             final[0, c, :, block * LANES : (block + 1) * LANES] = s.now[
@@ -484,24 +574,38 @@
             ]
 
 
-def run_sim(kind, width, unroll, offsets, bufs, tables, layers, spare):
-    out_shape = [jax.ShapeDtypeStruct((1, 3, 1, kind.count), F32)]
-    if not kind.sources:
-        out_shape.append(jax.ShapeDtypeStruct((STEPS, width, 4, LANES), F32))
+def begun_shapes(kind, width):
+    return [
+        jax.ShapeDtypeStruct((width, kind.blocks, 8, LANES), F32),
+        jax.ShapeDtypeStruct((width + 2, 8, LANES), F32),
+    ]
+
+
+def layer_shape(width):
+    return jax.ShapeDtypeStruct((STEPS, width, 4, LANES), F32)
+
+
+def run_sim(kind, width, unroll, offsets, mode, bufs, tables, more, spare):
+    if mode == "first":
+        out_shape = begun_shapes(kind, width)
+    else:
+        out_shape = [jax.ShapeDtypeStruct((1, 3, 1, kind.count), F32)]
+    if mode == "all":
+        out_shape.append(layer_shape(width))
     vmem = pl.BlockSpec(memory_space=pltpu.VMEM)
     hbm = pl.BlockSpec(memory_space=pl.ANY)
     return pl.pallas_call(
-        functools.partial(sim_kernel, kind, width, unroll, offsets, len(spare)),
+        functools.partial(sim_kernel, kind, width, unroll, offsets, mode, len(spare)),
         out_shape=out_shape + spare,
-        in_specs=[hbm] * len(bufs) + [vmem] * (2 + len(layers)),
+        in_specs=[hbm] * len(bufs) + [vmem] * (2 + len(more)),
         out_specs=[vmem] * len(out_shape) + [hbm] * len(spare),
         scratch_shapes=[
             pltpu.VMEM((width, kind.rows, LANES), F32),
-            pltpu.SemaphoreType.DMA((len(bufs),)),
+            pltpu.SemaphoreType.DMA((2 * len(offsets),)),
         ]
         + scratch_of(kind, width, unroll),
-        name="site_sim" if kind.sources else "reg_sim",
-    )(*bufs, *tables, *layers)
+        name="sim_" + mode,
+    )(*bufs, *tables, *more)
 
 
 def blank_kernel(final, *rest):
@@ -521,11 +625,23 @@
                 route.append((grp * count + index, grp * count + target))
         return lax.ppermute(array, ("grp", "sub"), route)
 
+    if len(offsets) == 1:
+        joined = value[None]
+        return [joined, moved(joined, 0, 1)]
     by_chip = [value if shift % chips == 0 else moved(value, shift, 0) for shift in offsets]
-    result = []
-    for array in by_chip:
-        result += [array, moved(array, 0, 1)]
-    return result
+    joined = pl.pallas_call(
+        join_kernel,
+        out_shape=jax.ShapeDtypeStruct((len(offsets), *value.shape), F32),
+        in_specs=[pl.BlockSpec(memory_space=pltpu.VMEM)] * len(offsets),
+        out_specs=pl.BlockSpec(memory_space=pltpu.VMEM),
+        name="join",
+    )(*by_chip)
+    return [joined, moved(joined, 0, 1)]
+
+
+def join_kernel(*refs):
+    for number, ref in enumerate(refs[:-1]):
+        refs[-1][number] = ref[...]
 
 
 def shards(
@@ -550,9 +666,10 @@
     is_site = lax.axis_index("grp") >= reg_groups
     vmem = pl.BlockSpec(memory_space=pltpu.VMEM)
     hbm = pl.BlockSpec(memory_space=pl.ANY)
-    site_spare = [jax.ShapeDtypeStruct((site.rows, LANES), F32)] * (2 * len(offsets)) + [
+    site_spare = [jax.ShapeDtypeStruct((len(offsets), site.rows, LANES), F32)] * 2 + [
         jax.ShapeDtypeStruct((3 * site.quads_pad, site.depth_in), BF16),
         jax.ShapeDtypeStruct((site.points_pad, site.depth_out), BF16),
+        *begun_shapes(site, width),
     ]
 
     def regional():
@@ -561,7 +678,9 @@
             slot_fill, layer_src, layer_fill, reg_table,
         )
         bufs = gather_window(buf, (0, reg_groups), offsets, count)
-        final, layer, *spare = run_sim(reg, width, unroll, offsets, bufs, tables, (), site_spare)
+        final, layer, *spare = run_sim(
+            reg, width, unroll, offsets, "all", bufs, tables, (), site_spare
+        )
         return (final, layer, *spare)
 
     def prepare_site():
@@ -574,15 +693,16 @@
             blank_kernel,
             out_shape=[
                 jax.ShapeDtypeStruct((1, 3, 1, reg.count), F32),
-                jax.ShapeDtypeStruct((STEPS, width, 4, LANES), F32),
+                layer_shape(width),
             ],
             out_specs=[vmem, hbm],
             name="blank",
         )()
-        return (final, layer, *bufs, *tables)
+        begun = run_sim(site, width, unroll, offsets, "first", bufs, tables, (), [])
+        return (final, layer, *bufs, *tables, *begun)
 
     reg_final, layer_out, *rest = lax.cond(is_site, prepare_site, regional)
-    site_bufs, site_tables = rest[:-2], rest[-2:]
+    site_bufs, site_tables, begun = rest[:2], rest[2:4], rest[4:]
     layers = [
         lax.ppermute(
             layer_out,
@@ -593,7 +713,8 @@
     ]
 
     def run_site():
-        return run_sim(site, width, unroll, offsets, site_bufs, site_tables, layers, [])[0]
+        more = (*layers, *begun)
+        return run_sim(site, width, unroll, offsets, "rest", site_bufs, site_tables, more, [])[0]
 
     def no_site():
         return jnp.zeros((1, 3, 1, site.count), F32)

time: 103 us -> 94.2 us (0.915)
  waiting for transfers between devices: 32.8 us -> 25.1 us
  starting transfers between devices: 22.8 us -> 16.1 us
  Pallas kernels: 43.1 us -> 48.3 us
  local copies, waits for them, and re-layouts: 1.99 us -> 3.31 us
    ppermute x3, waiting for transfers between devices: 27.9 us -> 15 us  [shards(): lax.ppermute(layer_out, 'grp', [(m * site_groups + i, reg_groups + i) for...]
    ppermute x7 -> x4, starting transfers between devices: 19 us -> 12.2 us  [moved(): return lax.ppermute(array, ('grp', 'sub'), route)]
    ppermute x7 -> x4, waiting for transfers between devices: 4.93 us -> 10.1 us  [moved(): return lax.ppermute(array, ('grp', 'sub'), route)]
    pallas_call x1 -> x2, Pallas kernels: 40.8 us -> 44 us  [run_sim(): pl.pallas_call(functools.partial(sim_kernel, kind, width, unroll, offsets...]
    pallas_call x0 -> x1, Pallas kernels: none -> 1.97 us  [gather_window(): pl.pallas_call(join_kernel, out_shape=jax.ShapeDtypeStruct((len(offsets),...]
    cond x10 -> x16, local copies, waits for them, and re-layouts: 0.7 us -> 2.03 us
  transfers between devices with their start and end apart: 10 -> 7, of which waited for: 4 -> 4; matrix products, arithmetic and copies ran while one was open for 0% -> 0% of each run, Pallas kernels for 1% -> 1%
where the time goes in v3:
time: 94.2 us; the launch traced here: 93.6 us
  Pallas kernels  48.3 us (51%)
  waiting for transfers between devices  25.1 us (27%)
  starting transfers between devices  16.1 us (17%)
  local copies, waits for them, and re-layouts  3.31 us (4%)
    pallas_call x2, Pallas kernels, run_sim(): pl.pallas_call(functools.partial(sim_kernel, kind, width, unroll, offsets...  44 us
    ppermute x3, waiting for transfers between devices, shards(): lax.ppermute(layer_out, 'grp', [(m * site_groups + i, reg_groups + i) for...  15 us
    ppermute x4, starting transfers between devices, moved(): return lax.ppermute(array, ('grp', 'sub'), route)  12.2 us
    ppermute x4, waiting for transfers between devices, moved(): return lax.ppermute(array, ('grp', 'sub'), route)  10.1 us
    ppermute x3, starting transfers between devices, shards(): lax.ppermute(layer_out, 'grp', [(m * site_groups + i, reg_groups + i) for...  3.88 us
    cond x16, local copies, waits for them, and re-layouts  2.03 us
    pallas_call x1, Pallas kernels, gather_window(): pl.pallas_call(join_kernel, out_shape=jax.ShapeDtypeStruct((len(offsets),...  1.97 us
  transfers between devices with their start and end apart: 7, of which 4 were waited for; matrix products, arithmetic and copies ran while one was open for 0% of the time, Pallas kernels for 1%

profile of v3, /device:TPU:6, one launch (start us, length us, event | category | flops | bytes accessed | tf_op | source)
XLA Modules:
  0.0 93.6 jit_solution(10288155047235383425)
XLA Ops:
  0.7 0.7 copy-done.9
  1.3 0.0 copy-done.18
  1.4 39.5 %conditional.2 = (f32[8,8,4,128]{3,2,1,0:T(4,128)S(1)}, f32[4,280,128]{2,1,0:T(8,128)}, f32[4,280,128]{2,1,0:T(8,128)}, bf16[72,128]{1,0:T(8,128)(2,1)}, bf16[40...) conditional(s32[]{:T(128)} %convert_element_type.4, ...), branch_computations={%region_0.0_spmd, %region_1.0_spmd} | conditional | bytes 5814080 | solution.py:704
  1.4 0.7 copy-done.7
  2.1 1.8 %site_pack.1 = (f32[280,128]{1,0:T(8,128)}, bf16[72,128]{1,0:T(8,128)(2,1)}, bf16[40,224]{1,0:T(8,128)(2,1)}) custom-call(f32[1,3,1,1536]{3,2,1,0:T(1,128)} %bitcast.31, f32[1,3,1,1536]{3,2,1,0:T(1,128)} %bitcast.32, s32[1,35,1,128]{3,2,1,0:T(1,128)} %bitcast.34, f32[1,1,3,3,24,128]{5,4,3,2,1,0:T(8,128)} %get-tuple-element.186.refs_3_, ...), custom_call_target="tpu_custom_call" | custom-call | tf_op jit(solution)/shard_map/cond/branch_1_fun/site_pack/pallas_call | solution.py:126
  3.9 5.5 %collective-permute-start.6 = (f32[280,128]{1,0:T(8,128)}, f32[280,128]{1,0:T(8,128)S(1)}, u32[]{:S(2)}, u32[]{:S(2)}) collective-permute-start(f32[280,128]{1,0:T(8,128)} %get-tuple-element.117.refs_0_), channel_id=1, source_target_pairs={{24,30},{25,31},{26,24},{27,25},{28,26},{29,27},{30,28},{31,29}} | collective-permute-start | bytes 430088 | tf_op jit(solution)/shard_map/cond/branch_1_fun/ppermute | solution.py:626
  9.4 1.9 %collective-permute-start.5 = (f32[280,128]{1,0:T(8,128)}, f32[280,128]{1,0:T(8,128)S(1)}, u32[]{:S(2)}, u32[]{:S(2)}) collective-permute-start(f32[280,128]{1,0:T(8,128)} %get-tuple-element.117.refs_0_), channel_id=1, source_target_pairs={{24,28},{25,29},{26,30},{27,31},{28,24},{29,25},{30,26},{31,27}} | collective-permute-start | bytes 430088 | tf_op jit(solution)/shard_map/cond/branch_1_fun/ppermute | solution.py:626
  11.3 2.9 %collective-permute-start.4 = (f32[280,128]{1,0:T(8,128)}, f32[280,128]{1,0:T(8,128)S(1)}, u32[]{:S(2)}, u32[]{:S(2)}) collective-permute-start(f32[280,128]{1,0:T(8,128)} %get-tuple-element.117.refs_0_), channel_id=1, source_target_pairs={{24,26},{25,27},{26,28},{27,29},{28,30},{29,31},{30,24},{31,25}} | collective-permute-start | bytes 430088 | tf_op jit(solution)/shard_map/cond/branch_1_fun/ppermute | solution.py:626
  14.2 8.4 %collective-permute-done.5.refs_2_ = f32[280,128]{1,0:T(8,128)S(1)} collective-permute-done((f32[280,128]{1,0:T(8,128)}, f32[280,128]{1,0:T(8,128)S(1)}, u32[]{:S(2)}, u32[]{:S(2)}) %collective-permute-start.5) | collective-permute-done | bytes 143392 | tf_op jit(solution)/shard_map/cond/branch_1_fun/ppermute | solution.py:626
  22.7 0.7 copy-done.2
  23.3 0.7 copy-done.3
  24.0 2.0 %join.3.refs_0_ = f32[4,280,128]{2,1,0:T(8,128)} custom-call(f32[280,128]{1,0:T(8,128)} %get-tuple-element.117.refs_0_, f32[280,128]{1,0:T(8,128)} %copy-done.3, f32[280,128]{1,0:T(8,128)} %copy-done.2, f32[280,128]{1,0:T(8,128)} %copy-done.1), custom_call_target="tpu_custom_call" | custom-call | tf_op jit(solution)/shard_map/cond/branch_1_fun/join/pallas_call | solution.py:632
  26.0 1.9 %collective-permute-start.7 = (f32[4,280,128]{2,1,0:T(8,128)}, f32[4,280,128]{2,1,0:T(8,128)}, u32[]{:S(2)}, u32[]{:S(2)}) collective-permute-start(f32[4,280,128]{2,1,0:T(8,128)} %join.3.refs_0_), channel_id=1, source_target_pairs={{24,25},{25,24},{26,27},{27,26},{28,29},{29,28},{30,31},{31,30}} | collective-permute-start | bytes 1720328 | tf_op jit(solution)/shard_map/cond/branch_1_fun/ppermute | solution.py:626
  27.9 0.6 blank.1
  28.5 1.7 %collective-permute-done.7.refs_1_ = f32[4,280,128]{2,1,0:T(8,128)} collective-permute-done((f32[4,280,128]{2,1,0:T(8,128)}, f32[4,280,128]{2,1,0:T(8,128)}, u32[]{:S(2)}, u32[]{:S(2)}) %collective-permute-start.7) | collective-permute-done | bytes 573472 | tf_op jit(solution)/shard_map/cond/branch_1_fun/ppermute | solution.py:626
  30.2 10.7 %sim_first.1 = (f32[8,12,8,128]{3,2,1,0:T(8,128)S(1)}, f32[10,8,128]{2,1,0:T(8,128)S(1)}) custom-call(f32[4,280,128]{2,1,0:T(8,128)} %join.3.refs_0_, f32[4,280,128]{2,1,0:T(8,128)} %collective-permute-done.7.refs_1_, bf16[72,128]{1,0:T(8,128)(2,1)} %get-tuple-element.226.refs_2_, bf16[40,224]{1,0:T(8,128)(2,1)} %get-tuple-element.227.refs_3_), custom_call_target="tpu_custom_call" | custom-call | tf_op jit(solution)/shard_map/cond/branch_1_fun/sim_first/pallas_call | solution.py:597
  40.9 1.3 %collective-permute-start.10 = (f32[8,8,4,128]{3,2,1,0:T(4,128)S(1)}, f32[8,8,4,128]{3,2,1,0:T(4,128)S(1)}, u32[]{:S(2)}, u32[]{:S(2)}) collective-permute-start(f32[8,8,4,128]{3,2,1,0:T(4,128)S(1)} %get-tuple-element.147), channel_id=1, source_target_pairs={{16,24},{17,25},{18,26},{19,27},{20,28},{21,29},{22,30},{23,31}} | collective-permute-start | bytes 393224 | tf_op jit(solution)/shard_map/ppermute | solution.py:707
  42.2 1.3 %collective-permute-start.9 = (f32[8,8,4,128]{3,2,1,0:T(4,128)S(1)}, f32[8,8,4,128]{3,2,1,0:T(4,128)S(1)}, u32[]{:S(2)}, u32[]{:S(2)}) collective-permute-start(f32[8,8,4,128]{3,2,1,0:T(4,128)S(1)} %get-tuple-element.147), channel_id=1, source_target_pairs={{8,24},{9,25},{10,26},{11,27},{12,28},{13,29},{14,30},{15,31}} | collective-permute-start | bytes 393224 | tf_op jit(solution)/shard_map/ppermute | solution.py:707
  43.5 1.3 %collective-permute-start.8 = (f32[8,8,4,128]{3,2,1,0:T(4,128)S(1)}, f32[8,8,4,128]{3,2,1,0:T(4,128)S(1)}, u32[]{:S(2)}, u32[]{:S(2)}) collective-permute-start(f32[8,8,4,128]{3,2,1,0:T(4,128)S(1)} %get-tuple-element.147), channel_id=1, source_target_pairs={{0,24},{1,25},{2,26},{3,27},{4,28},{5,29},{6,30},{7,31}} | collective-permute-start | bytes 393224 | tf_op jit(solution)/shard_map/ppermute | solution.py:707
  44.8 11.5 %collective-permute-done.10 = f32[8,8,4,128]{3,2,1,0:T(4,128)S(1)} collective-permute-done((f32[8,8,4,128]{3,2,1,0:T(4,128)S(1)}, f32[8,8,4,128]{3,2,1,0:T(4,128)S(1)}, u32[]{:S(2)}, u32[]{:S(2)}) %collective-permute-start.10) | collective-permute-done | bytes 131104 | tf_op jit(solution)/shard_map/ppermute | solution.py:707
  56.3 3.5 %collective-permute-done.9 = f32[8,8,4,128]{3,2,1,0:T(4,128)S(1)} collective-permute-done((f32[8,8,4,128]{3,2,1,0:T(4,128)S(1)}, f32[8,8,4,128]{3,2,1,0:T(4,128)S(1)}, u32[]{:S(2)}, u32[]{:S(2)}) %collective-permute-start.9) | collective-permute-done | bytes 131104 | tf_op jit(solution)/shard_map/ppermute | solution.py:707
  59.7 33.3 %conditional.3 = (f32[1,1,3,1536]{3,1,2,0:T(1,128)S(1)}) conditional(s32[]{:T(128)} %convert_element_type.4, () %tuple.31, (f32[4,280,128]{2,1,0:T(8,128)}, f32[4,280,128]{2,1,0:T(8,128)}, bf16[72,128]{1,0:T(8,128)(2,1)}, bf16[40,224]{1,0:T(8,128)(2,1)}, f32[8,8,4,128]{3,2,1,0:T(4,128)S(1)}, /*index=5*/f32[8,8,4,128]{3,2,1,0:T(4,128)S(1)}, ...), branch_computations={%region_2.0_spmd, %region_3.0_spmd} | conditional | bytes 18444 | solution.py:722
  59.7 33.3 %sim_rest.1 = f32[1,3,1,1536]{3,2,1,0:T(1,128)S(1)} custom-call(f32[4,280,128]{2,1,0:T(8,128)} %get-tuple-element.123.refs_0_, f32[4,280,128]{2,1,0:T(8,128)} %get-tuple-element.124.refs_1_, bf16[72,128]{1,0:T(8,128)(2,1)} %get-tuple-element.125.refs_2_, bf16[40,224]{1,0:T(8,128)(2,1)} %get-tuple-element.126.refs_3_, ...), custom_call_target="tpu_custom_call" | custom-call | tf_op jit(solution)/shard_map/cond/branch_1_fun/sim_rest/pallas_call | solution.py:597
  93.0 0.6 copy-done.8
  (23 shorter events, 0.1 us)
Async XLA Ops:
  0.6 0.7 copy-start.9
  0.7 0.7 copy-start.15
  0.7 0.7 copy-start.14
  0.7 0.7 copy-start.18
  1.4 0.7 copy-start.7
  1.4 0.7 copy-start.11
  1.4 0.7 copy-start.16
  1.4 0.7 copy-start.21
  1.4 0.7 copy-start.20
  3.9 10.4 %collective-permute-start.6 = (f32[280,128]{1,0:T(8,128)}, f32[280,128]{1,0:T(8,128)S(1)}, u32[]{:S(2)}, u32[]{:S(2)}) collective-permute-start(f32[280,128]{1,0:T(8,128)} %get-tuple-element.117.refs_0_), channel_id=1, source_target_pairs={{24,30},{25,31},{26,24},{27,25},{28,26},{29,27},{30,28},{31,29}} | collective-permute-start | bytes 430088 | tf_op jit(solution)/shard_map/cond/branch_1_fun/ppermute | solution.py:626
  9.4 13.3 %collective-permute-start.5 = (f32[280,128]{1,0:T(8,128)}, f32[280,128]{1,0:T(8,128)S(1)}, u32[]{:S(2)}, u32[]{:S(2)}) collective-permute-start(f32[280,128]{1,0:T(8,128)} %get-tuple-element.117.refs_0_), channel_id=1, source_target_pairs={{24,28},{25,29},{26,30},{27,31},{28,24},{29,25},{30,26},{31,27}} | collective-permute-start | bytes 430088 | tf_op jit(solution)/shard_map/cond/branch_1_fun/ppermute | solution.py:626
  11.3 11.4 %collective-permute-start.4 = (f32[280,128]{1,0:T(8,128)}, f32[280,128]{1,0:T(8,128)S(1)}, u32[]{:S(2)}, u32[]{:S(2)}) collective-permute-start(f32[280,128]{1,0:T(8,128)} %get-tuple-element.117.refs_0_), channel_id=1, source_target_pairs={{24,26},{25,27},{26,28},{27,29},{28,30},{29,31},{30,24},{31,25}} | collective-permute-start | bytes 430088 | tf_op jit(solution)/shard_map/cond/branch_1_fun/ppermute | solution.py:626
  14.2 8.4 %copy-start.1 = (f32[280,128]{1,0:T(8,128)}, f32[280,128]{1,0:T(8,128)S(1)}, u32[]{:S(2)}) copy-start(f32[280,128]{1,0:T(8,128)S(1)} %collective-permute-done.6.refs_3_) | copy-start | bytes 430084 | tf_op jit(solution)/shard_map/cond
  22.7 0.7 copy-start.2
  23.3 0.7 copy-start.3
  26.0 4.2 %collective-permute-start.7 = (f32[4,280,128]{2,1,0:T(8,128)}, f32[4,280,128]{2,1,0:T(8,128)}, u32[]{:S(2)}, u32[]{:S(2)}) collective-permute-start(f32[4,280,128]{2,1,0:T(8,128)} %join.3.refs_0_), channel_id=1, source_target_pairs={{24,25},{25,24},{26,27},{27,26},{28,29},{29,28},{30,31},{31,30}} | collective-permute-start | bytes 1720328 | tf_op jit(solution)/shard_map/cond/branch_1_fun/ppermute | solution.py:626
  40.9 15.4 %collective-permute-start.10 = (f32[8,8,4,128]{3,2,1,0:T(4,128)S(1)}, f32[8,8,4,128]{3,2,1,0:T(4,128)S(1)}, u32[]{:S(2)}, u32[]{:S(2)}) collective-permute-start(f32[8,8,4,128]{3,2,1,0:T(4,128)S(1)} %get-tuple-element.147), channel_id=1, source_target_pairs={{16,24},{17,25},{18,26},{19,27},{20,28},{21,29},{22,30},{23,31}} | collective-permute-start | bytes 393224 | tf_op jit(solution)/shard_map/ppermute | solution.py:707
  42.2 17.6 %collective-permute-start.9 = (f32[8,8,4,128]{3,2,1,0:T(4,128)S(1)}, f32[8,8,4,128]{3,2,1,0:T(4,128)S(1)}, u32[]{:S(2)}, u32[]{:S(2)}) collective-permute-start(f32[8,8,4,128]{3,2,1,0:T(4,128)S(1)} %get-tuple-element.147), channel_id=1, source_target_pairs={{8,24},{9,25},{10,26},{11,27},{12,28},{13,29},{14,30},{15,31}} | collective-permute-start | bytes 393224 | tf_op jit(solution)/shard_map/ppermute | solution.py:707
  43.5 16.3 %collective-permute-start.8 = (f32[8,8,4,128]{3,2,1,0:T(4,128)S(1)}, f32[8,8,4,128]{3,2,1,0:T(4,128)S(1)}, u32[]{:S(2)}, u32[]{:S(2)}) collective-permute-start(f32[8,8,4,128]{3,2,1,0:T(4,128)S(1)} %get-tuple-element.147), channel_id=1, source_target_pairs={{0,24},{1,25},{2,26},{3,27},{4,28},{5,29},{6,30},{7,31}} | collective-permute-start | bytes 393224 | tf_op jit(solution)/shard_map/ppermute | solution.py:707
  93.0 0.6 copy-start.8

commit v4 on v3

--- a/solution.py
+++ b/solution.py
@@ -56,6 +56,21 @@
 
 
 def pack_kernel(kind, *refs):
+    inputs, refs = refs[:11], refs[11:]
+    outputs, work, held, sem = refs[:3], refs[3], refs[4:15], refs[15]
+    copies = [
+        pltpu.make_async_copy(source, target, sem.at[number])
+        for number, (source, target) in enumerate(zip(inputs, held, strict=True))
+    ]
+    for copy in copies:
+        copy.start()
+    work[...] = jnp.zeros(work.shape, F32)
+    for copy in copies:
+        copy.wait()
+    fill_packed(kind, *held, *outputs, work)
+
+
+def fill_packed(kind, *refs):
     disp, vel, nodes, coefs, minv, send, recv, fill, layer_a, layer_b, table, out, first, second = refs[:14]
     work = refs[14]
     for pair, (a, b) in enumerate(PAIRS):
@@ -74,7 +89,8 @@
         out[kind.at_minv + block : kind.at_minv + block + 1, :] = minv[0, 0:1, lanes]
     lane = lax.broadcasted_iota(jnp.int32, (1, LANES), 1)
     for side in range(2):
-        live = lane < fill[0, 0, (2 if kind.sources else 0) + side]
+        at = (2 if kind.sources else 0) + side
+        live = lane < jnp.broadcast_to(fill[0, 0:1, at : at + 1], (1, LANES))
         row = send[0, 0, side : side + 1, :]
         out[kind.at_send + side : kind.at_send + side + 1, :] = jnp.where(live, row, -1).astype(F32)
     out[kind.at_recv : kind.at_recv + 2, :] = recv[0, 0].astype(F32)
@@ -84,10 +100,9 @@
         out[at + kind.sources : at + kind.sources + 1, :] = layer_b[0, m]
     if not kind.sources:
         row = layer_a[0, 0:1, :]
-        live = lane < layer_b[0, 0]
+        live = lane < jnp.broadcast_to(layer_b[0:1, 0:1], (1, LANES))
         out[kind.at_layer : kind.at_layer + 1, :] = jnp.where(live, row, -1).astype(F32)
     size = kind.quads_pad
-    work[...] = jnp.zeros(work.shape, F32)
     if kind.table_turned:
         work[0 : kind.points, 0 : 3 * kind.quads] = table[...]
         turned = work[...]
@@ -118,11 +133,14 @@
         return jnp.transpose(array, (0, 2, 1, 3))
 
     vmem = pl.BlockSpec(memory_space=pltpu.VMEM)
-    smem = pl.BlockSpec(memory_space=pltpu.SMEM)
+    hbm = pl.BlockSpec(memory_space=pl.ANY)
     if kind.sources:
         layer_a, layer_b = thin(layer_a), thin(layer_b)
     if kind.table_turned:
         table = table.T
+    inputs = (
+        thin(disp), thin(vel), thin(nodes), coefs, minv, send, recv, fill, layer_a, layer_b, table,
+    )
     return pl.pallas_call(
         functools.partial(pack_kernel, kind),
         out_shape=[
@@ -130,11 +148,15 @@
             jax.ShapeDtypeStruct((3 * kind.quads_pad, kind.depth_in), BF16),
             jax.ShapeDtypeStruct((kind.points_pad, kind.depth_out), BF16),
         ],
-        in_specs=[vmem] * 7 + [smem, vmem, vmem if kind.sources else smem, vmem],
+        in_specs=[hbm] * len(inputs),
         out_specs=[vmem] * 3,
-        scratch_shapes=[pltpu.VMEM((LANES, LANES), F32)],
+        scratch_shapes=[
+            pltpu.VMEM((LANES, LANES), F32),
+            *[pltpu.VMEM(array.shape, array.dtype) for array in inputs],
+            pltpu.SemaphoreType.DMA((len(inputs),)),
+        ],
         name="site_pack" if kind.sources else "reg_pack",
-    )(thin(disp), thin(vel), thin(nodes), coefs, minv, send, recv, fill, layer_a, layer_b, table)
+    )(*inputs)
 
 
 def split_index(value):
@@ -428,9 +450,10 @@
             jnp.where(low_half, upper, pltpu.roll(upper, 4, 0)),
         ]
         for m in range(kind.sources):
-            four = layers[m][step, q]
             at = kind.at_layer + kind.sources + m
-            values.append(jnp.concatenate([four, four], axis=0) * buf[q, at : at + 1, :])
+            rows = [layers[m][step, c, pl.ds(q, 1), :] for c in range(3)]
+            rows = jnp.concatenate([*rows, jnp.zeros((1, LANES), F32)] * 2, axis=0)
+            values.append(rows * buf[q, at : at + 1, :])
         total = scattered(
             q, 4 * kind.tiles, main_rows, lambda k: split8(values[k]), len(values)
         )
@@ -446,7 +469,8 @@
             after.append(value)
         if emit is not None:
             picked = pick(lambda block: after[block], s.layer_lo[q], s.layer_hi[q])
-            emit[step, q] = picked[0:4]
+            for c in range(3):
+                emit[step, c, pl.ds(q, 1), :] = picked[c : c + 1, :]
 
     def all_forces():
         def forces(group, _):
@@ -478,12 +502,17 @@
     if mode == "rest":
         all_updates(0, *begun)
         done = 1
-    lax.fori_loop(done, STEPS - 1, one_step, 0)
-    span = min(4, unroll)
-    first = jnp.clip(own - 1, 0, width - span)
-    for lane in range(span):
-        force(first + lane, lane)
-    update(own, 0, STEPS - 1, s.force, s.sends)
+    tail = max(done, STEPS - 2)
+    lax.fori_loop(done, tail, one_step, 0)
+    for step in range(tail, STEPS):
+        reach = STEPS - step
+        for span, run in (
+            (min(2 * reach + 1, width), force),
+            (min(2 * reach - 1, width), functools.partial(update, step=step, forces=s.force, sends=s.sends)),
+        ):
+            first = jnp.clip(own - span // 2, 0, width - span)
+            for lane in range(span):
+                run(first + lane, lane % unroll)
 
 
 SCRATCH = (
@@ -582,7 +611,7 @@
 
 
 def layer_shape(width):
-    return jax.ShapeDtypeStruct((STEPS, width, 4, LANES), F32)
+    return jax.ShapeDtypeStruct((STEPS, 3, width, LANES), F32)
 
 
 def run_sim(kind, width, unroll, offsets, mode, bufs, tables, more, spare):

time: 94.2 us -> 91.1 us (0.967)
  waiting for transfers between devices: 25.1 us -> 23 us
  Pallas kernels: 48.3 us -> 47.3 us
    ppermute x3, waiting for transfers between devices: 15 us -> 12.9 us  [shards(): lax.ppermute(layer_out, 'grp', [(m * site_groups + i, reg_groups + i) for...]
    pallas_call x2, Pallas kernels: 44 us -> 42.9 us  [run_sim(): pl.pallas_call(functools.partial(sim_kernel, kind, width, unroll, offsets...]
where the time goes in v4:
time: 91.1 us; the launch traced here: 90.5 us
  Pallas kernels  47.3 us (52%)
  waiting for transfers between devices  23 us (25%)
  starting transfers between devices  16.1 us (18%)
  local copies, waits for them, and re-layouts  3.31 us (4%)
    pallas_call x2, Pallas kernels, run_sim(): pl.pallas_call(functools.partial(sim_kernel, kind, width, unroll, offsets...  42.9 us
    ppermute x3, waiting for transfers between devices, shards(): lax.ppermute(layer_out, 'grp', [(m * site_groups + i, reg_groups + i) for...  12.9 us
    ppermute x4, starting transfers between devices, moved(): return lax.ppermute(array, ('grp', 'sub'), route)  12.2 us
    ppermute x4, waiting for transfers between devices, moved(): return lax.ppermute(array, ('grp', 'sub'), route)  10.1 us
    ppermute x3, starting transfers between devices, shards(): lax.ppermute(layer_out, 'grp', [(m * site_groups + i, reg_groups + i) for...  3.88 us
    cond x16, local copies, waits for them, and re-layouts  2.03 us
    pallas_call x1, Pallas kernels, gather_window(): pl.pallas_call(join_kernel, out_shape=jax.ShapeDtypeStruct((len(offsets),...  1.97 us
    pallas_call x1, Pallas kernels, pack(): pl.pallas_call(functools.partial(pack_kernel, kind), out_shape=[jax.Shape...  1.85 us
  transfers between devices with their start and end apart: 7, of which 4 were waited for; matrix products, arithmetic and copies ran while one was open for 0% of the time, Pallas kernels for 1%

profile of v4, /device:TPU:6, one launch (start us, length us, event | category | flops | bytes accessed | tf_op | source)
XLA Modules:
  0.0 90.5 jit_solution(10185053078991901639)
XLA Ops:
  0.7 0.7 copy-done.9
  1.3 0.0 copy-done.18
  1.4 39.6 %conditional.2 = (f32[8,3,8,128]{3,2,1,0:T(8,128)S(1)}, f32[4,280,128]{2,1,0:T(8,128)}, f32[4,280,128]{2,1,0:T(8,128)}, bf16[72,128]{1,0:T(8,128)(2,1)}, bf16[40...) conditional(s32[]{:T(128)} %convert_element_type.4, ...), branch_computations={%region_0.0_spmd, %region_1.0_spmd} | conditional | bytes 5814080 | solution.py:733
  1.4 0.7 copy-done.7
  2.1 1.8 %site_pack.1 = (f32[280,128]{1,0:T(8,128)}, bf16[72,128]{1,0:T(8,128)(2,1)}, bf16[40,224]{1,0:T(8,128)(2,1)}) custom-call(f32[1,3,1,1536]{3,2,1,0:T(1,128)} %bitcast.31, f32[1,3,1,1536]{3,2,1,0:T(1,128)} %bitcast.32, s32[1,35,1,128]{3,2,1,0:T(1,128)} %bitcast.34, f32[1,1,3,3,24,128]{5,4,3,2,1,0:T(8,128)} %get-tuple-element.186.refs_3_, ...), custom_call_target="tpu_custom_call" | custom-call | tf_op jit(solution)/shard_map/cond/branch_1_fun/site_pack/pallas_call | solution.py:144
  4.0 5.5 %collective-permute-start.6 = (f32[280,128]{1,0:T(8,128)}, f32[280,128]{1,0:T(8,128)S(1)}, u32[]{:S(2)}, u32[]{:S(2)}) collective-permute-start(f32[280,128]{1,0:T(8,128)} %get-tuple-element.117.refs_0_), channel_id=1, source_target_pairs={{24,30},{25,31},{26,24},{27,25},{28,26},{29,27},{30,28},{31,29}} | collective-permute-start | bytes 430088 | tf_op jit(solution)/shard_map/cond/branch_1_fun/ppermute | solution.py:655
  9.5 1.9 %collective-permute-start.5 = (f32[280,128]{1,0:T(8,128)}, f32[280,128]{1,0:T(8,128)S(1)}, u32[]{:S(2)}, u32[]{:S(2)}) collective-permute-start(f32[280,128]{1,0:T(8,128)} %get-tuple-element.117.refs_0_), channel_id=1, source_target_pairs={{24,28},{25,29},{26,30},{27,31},{28,24},{29,25},{30,26},{31,27}} | collective-permute-start | bytes 430088 | tf_op jit(solution)/shard_map/cond/branch_1_fun/ppermute | solution.py:655
  11.4 2.9 %collective-permute-start.4 = (f32[280,128]{1,0:T(8,128)}, f32[280,128]{1,0:T(8,128)S(1)}, u32[]{:S(2)}, u32[]{:S(2)}) collective-permute-start(f32[280,128]{1,0:T(8,128)} %get-tuple-element.117.refs_0_), channel_id=1, source_target_pairs={{24,26},{25,27},{26,28},{27,29},{28,30},{29,31},{30,24},{31,25}} | collective-permute-start | bytes 430088 | tf_op jit(solution)/shard_map/cond/branch_1_fun/ppermute | solution.py:655
  14.3 8.4 %collective-permute-done.5.refs_2_ = f32[280,128]{1,0:T(8,128)S(1)} collective-permute-done((f32[280,128]{1,0:T(8,128)}, f32[280,128]{1,0:T(8,128)S(1)}, u32[]{:S(2)}, u32[]{:S(2)}) %collective-permute-start.5) | collective-permute-done | bytes 143392 | tf_op jit(solution)/shard_map/cond/branch_1_fun/ppermute | solution.py:655
  22.8 0.7 copy-done.2
  23.4 0.7 copy-done.3
  24.1 2.0 %join.3.refs_0_ = f32[4,280,128]{2,1,0:T(8,128)} custom-call(f32[280,128]{1,0:T(8,128)} %get-tuple-element.117.refs_0_, f32[280,128]{1,0:T(8,128)} %copy-done.3, f32[280,128]{1,0:T(8,128)} %copy-done.2, f32[280,128]{1,0:T(8,128)} %copy-done.1), custom_call_target="tpu_custom_call" | custom-call | tf_op jit(solution)/shard_map/cond/branch_1_fun/join/pallas_call | solution.py:661
  26.1 1.9 %collective-permute-start.7 = (f32[4,280,128]{2,1,0:T(8,128)}, f32[4,280,128]{2,1,0:T(8,128)}, u32[]{:S(2)}, u32[]{:S(2)}) collective-permute-start(f32[4,280,128]{2,1,0:T(8,128)} %join.3.refs_0_), channel_id=1, source_target_pairs={{24,25},{25,24},{26,27},{27,26},{28,29},{29,28},{30,31},{31,30}} | collective-permute-start | bytes 1720328 | tf_op jit(solution)/shard_map/cond/branch_1_fun/ppermute | solution.py:655
  28.0 0.6 blank.1
  28.6 1.7 %collective-permute-done.7.refs_1_ = f32[4,280,128]{2,1,0:T(8,128)} collective-permute-done((f32[4,280,128]{2,1,0:T(8,128)}, f32[4,280,128]{2,1,0:T(8,128)}, u32[]{:S(2)}, u32[]{:S(2)}) %collective-permute-start.7) | collective-permute-done | bytes 573472 | tf_op jit(solution)/shard_map/cond/branch_1_fun/ppermute | solution.py:655
  30.3 10.7 %sim_first.1 = (f32[8,12,8,128]{3,2,1,0:T(8,128)S(1)}, f32[10,8,128]{2,1,0:T(8,128)S(1)}) custom-call(f32[4,280,128]{2,1,0:T(8,128)} %join.3.refs_0_, f32[4,280,128]{2,1,0:T(8,128)} %collective-permute-done.7.refs_1_, bf16[72,128]{1,0:T(8,128)(2,1)} %get-tuple-element.226.refs_2_, bf16[40,224]{1,0:T(8,128)(2,1)} %get-tuple-element.227.refs_3_), custom_call_target="tpu_custom_call" | custom-call | tf_op jit(solution)/shard_map/cond/branch_1_fun/sim_first/pallas_call | solution.py:626
  41.0 1.3 %collective-permute-start.10 = (f32[8,3,8,128]{3,2,1,0:T(8,128)S(1)}, f32[8,3,8,128]{3,2,1,0:T(8,128)S(1)}, u32[]{:S(2)}, u32[]{:S(2)}) collective-permute-start(f32[8,3,8,128]{3,2,1,0:T(8,128)S(1)} %get-tuple-element.147), channel_id=1, source_target_pairs={{16,24},{17,25},{18,26},{19,27},{20,28},{21,29},{22,30},{23,31}} | collective-permute-start | bytes 294920 | tf_op jit(solution)/shard_map/ppermute | solution.py:736
  42.3 1.3 %collective-permute-start.9 = (f32[8,3,8,128]{3,2,1,0:T(8,128)S(1)}, f32[8,3,8,128]{3,2,1,0:T(8,128)S(1)}, u32[]{:S(2)}, u32[]{:S(2)}) collective-permute-start(f32[8,3,8,128]{3,2,1,0:T(8,128)S(1)} %get-tuple-element.147), channel_id=1, source_target_pairs={{8,24},{9,25},{10,26},{11,27},{12,28},{13,29},{14,30},{15,31}} | collective-permute-start | bytes 294920 | tf_op jit(solution)/shard_map/ppermute | solution.py:736
  43.6 1.3 %collective-permute-start.8 = (f32[8,3,8,128]{3,2,1,0:T(8,128)S(1)}, f32[8,3,8,128]{3,2,1,0:T(8,128)S(1)}, u32[]{:S(2)}, u32[]{:S(2)}) collective-permute-start(f32[8,3,8,128]{3,2,1,0:T(8,128)S(1)} %get-tuple-element.147), channel_id=1, source_target_pairs={{0,24},{1,25},{2,26},{3,27},{4,28},{5,29},{6,30},{7,31}} | collective-permute-start | bytes 294920 | tf_op jit(solution)/shard_map/ppermute | solution.py:736
  44.9 10.1 %collective-permute-done.10 = f32[8,3,8,128]{3,2,1,0:T(8,128)S(1)} collective-permute-done((f32[8,3,8,128]{3,2,1,0:T(8,128)S(1)}, f32[8,3,8,128]{3,2,1,0:T(8,128)S(1)}, u32[]{:S(2)}, u32[]{:S(2)}) %collective-permute-start.10) | collective-permute-done | bytes 98336 | tf_op jit(solution)/shard_map/ppermute | solution.py:736
  55.0 2.8 %collective-permute-done.9 = f32[8,3,8,128]{3,2,1,0:T(8,128)S(1)} collective-permute-done((f32[8,3,8,128]{3,2,1,0:T(8,128)S(1)}, f32[8,3,8,128]{3,2,1,0:T(8,128)S(1)}, u32[]{:S(2)}, u32[]{:S(2)}) %collective-permute-start.9) | collective-permute-done | bytes 98336 | tf_op jit(solution)/shard_map/ppermute | solution.py:736
  57.7 32.2 %conditional.3 = (f32[1,1,3,1536]{3,1,2,0:T(1,128)S(1)}) conditional(s32[]{:T(128)} %convert_element_type.4, () %tuple.31, (f32[4,280,128]{2,1,0:T(8,128)}, f32[4,280,128]{2,1,0:T(8,128)}, bf16[72,128]{1,0:T(8,128)(2,1)}, bf16[40,224]{1,0:T(8,128)(2,1)}, f32[8,3,8,128]{3,2,1,0:T(8,128)S(1)}, /*index=5*/f32[8,3,8,128]{3,2,1,0:T(8,128)S(1)}, ...), branch_computations={%region_2.0_spmd, %region_3.0_spmd} | conditional | bytes 18444 | solution.py:751
  57.7 32.2 %sim_rest.1 = f32[1,3,1,1536]{3,2,1,0:T(1,128)S(1)} custom-call(f32[4,280,128]{2,1,0:T(8,128)} %get-tuple-element.123.refs_0_, f32[4,280,128]{2,1,0:T(8,128)} %get-tuple-element.124.refs_1_, bf16[72,128]{1,0:T(8,128)(2,1)} %get-tuple-element.125.refs_2_, bf16[40,224]{1,0:T(8,128)(2,1)} %get-tuple-element.126.refs_3_, ...), custom_call_target="tpu_custom_call" | custom-call | tf_op jit(solution)/shard_map/cond/branch_1_fun/sim_rest/pallas_call | solution.py:626
  89.9 0.6 copy-done.8
  (23 shorter events, 0.1 us)
Async XLA Ops:
  0.6 0.7 copy-start.9
  0.7 0.7 copy-start.15
  0.7 0.7 copy-start.14
  0.7 0.7 copy-start.18
  1.4 0.7 copy-start.7
  1.4 0.7 copy-start.11
  1.4 0.7 copy-start.16
  1.4 0.7 copy-start.21
  1.4 0.7 copy-start.20
  4.0 10.4 %collective-permute-start.6 = (f32[280,128]{1,0:T(8,128)}, f32[280,128]{1,0:T(8,128)S(1)}, u32[]{:S(2)}, u32[]{:S(2)}) collective-permute-start(f32[280,128]{1,0:T(8,128)} %get-tuple-element.117.refs_0_), channel_id=1, source_target_pairs={{24,30},{25,31},{26,24},{27,25},{28,26},{29,27},{30,28},{31,29}} | collective-permute-start | bytes 430088 | tf_op jit(solution)/shard_map/cond/branch_1_fun/ppermute | solution.py:655
  9.5 13.3 %collective-permute-start.5 = (f32[280,128]{1,0:T(8,128)}, f32[280,128]{1,0:T(8,128)S(1)}, u32[]{:S(2)}, u32[]{:S(2)}) collective-permute-start(f32[280,128]{1,0:T(8,128)} %get-tuple-element.117.refs_0_), channel_id=1, source_target_pairs={{24,28},{25,29},{26,30},{27,31},{28,24},{29,25},{30,26},{31,27}} | collective-permute-start | bytes 430088 | tf_op jit(solution)/shard_map/cond/branch_1_fun/ppermute | solution.py:655
  11.4 11.4 %collective-permute-start.4 = (f32[280,128]{1,0:T(8,128)}, f32[280,128]{1,0:T(8,128)S(1)}, u32[]{:S(2)}, u32[]{:S(2)}) collective-permute-start(f32[280,128]{1,0:T(8,128)} %get-tuple-element.117.refs_0_), channel_id=1, source_target_pairs={{24,26},{25,27},{26,28},{27,29},{28,30},{29,31},{30,24},{31,25}} | collective-permute-start | bytes 430088 | tf_op jit(solution)/shard_map/cond/branch_1_fun/ppermute | solution.py:655
  14.3 8.4 %copy-start.1 = (f32[280,128]{1,0:T(8,128)}, f32[280,128]{1,0:T(8,128)S(1)}, u32[]{:S(2)}) copy-start(f32[280,128]{1,0:T(8,128)S(1)} %collective-permute-done.6.refs_3_) | copy-start | bytes 430084 | tf_op jit(solution)/shard_map/cond
  22.8 0.7 copy-start.2
  23.4 0.7 copy-start.3
  26.1 4.2 %collective-permute-start.7 = (f32[4,280,128]{2,1,0:T(8,128)}, f32[4,280,128]{2,1,0:T(8,128)}, u32[]{:S(2)}, u32[]{:S(2)}) collective-permute-start(f32[4,280,128]{2,1,0:T(8,128)} %join.3.refs_0_), channel_id=1, source_target_pairs={{24,25},{25,24},{26,27},{27,26},{28,29},{29,28},{30,31},{31,30}} | collective-permute-start | bytes 1720328 | tf_op jit(solution)/shard_map/cond/branch_1_fun/ppermute | solution.py:655
  41.0 14.0 %collective-permute-start.10 = (f32[8,3,8,128]{3,2,1,0:T(8,128)S(1)}, f32[8,3,8,128]{3,2,1,0:T(8,128)S(1)}, u32[]{:S(2)}, u32[]{:S(2)}) collective-permute-start(f32[8,3,8,128]{3,2,1,0:T(8,128)S(1)} %get-tuple-element.147), channel_id=1, source_target_pairs={{16,24},{17,25},{18,26},{19,27},{20,28},{21,29},{22,30},{23,31}} | collective-permute-start | bytes 294920 | tf_op jit(solution)/shard_map/ppermute | solution.py:736
  42.3 15.5 %collective-permute-start.9 = (f32[8,3,8,128]{3,2,1,0:T(8,128)S(1)}, f32[8,3,8,128]{3,2,1,0:T(8,128)S(1)}, u32[]{:S(2)}, u32[]{:S(2)}) collective-permute-start(f32[8,3,8,128]{3,2,1,0:T(8,128)S(1)} %get-tuple-element.147), channel_id=1, source_target_pairs={{8,24},{9,25},{10,26},{11,27},{12,28},{13,29},{14,30},{15,31}} | collective-permute-start | bytes 294920 | tf_op jit(solution)/shard_map/ppermute | solution.py:736
  43.6 14.2 %collective-permute-start.8 = (f32[8,3,8,128]{3,2,1,0:T(8,128)S(1)}, f32[8,3,8,128]{3,2,1,0:T(8,128)S(1)}, u32[]{:S(2)}, u32[]{:S(2)}) collective-permute-start(f32[8,3,8,128]{3,2,1,0:T(8,128)S(1)} %get-tuple-element.147), channel_id=1, source_target_pairs={{0,24},{1,25},{2,26},{3,27},{4,28},{5,29},{6,30},{7,31}} | collective-permute-start | bytes 294920 | tf_op jit(solution)/shard_map/ppermute | solution.py:736
  89.9 0.6 copy-start.8

commit v5 on v4

--- a/solution.py
+++ b/solution.py
@@ -187,6 +187,8 @@
     main_rows = kind.tiles * 256
 
     def onehot(q, chunk_no, base_row, columns, at):
+        if mode == "rest":
+            return
         hit = columns[:, at : at + 1] == lane_ids
         tile, half, part = chunk_no // 4, (chunk_no // 2) % 2, chunk_no % 2
         rows = pl.ds(base_row + tile * 256 + part * LANES, LANES)
@@ -196,6 +198,8 @@
         s.block_of[q, chunk_no : chunk_no + 1, :] = hi_row.astype(F32)
 
     def columns_of(rows):
+        if mode == "rest":
+            return None
         count = rows.shape[0]
         if count < LANES:
             rows = jnp.concatenate([rows, jnp.zeros((LANES - count, LANES), F32)], axis=0)
@@ -524,7 +528,7 @@
 def scratch_of(kind, width, unroll):
     tiles = kind.tiles + kind.extra_tiles
     return [
-        pltpu.VMEM((width, 2, tiles * 256, LANES), BF16),
+        pltpu.VMEM(onehot_shape(kind, width), BF16),
         pltpu.VMEM((width, 4 * tiles, LANES), F32),
         pltpu.VMEM((width, 6, kind.quads_pad, kind.elems), F32),
         pltpu.VMEM((width, kind.cuts, kind.points_pad, LANES), jnp.int32),
@@ -559,9 +563,9 @@
     layers = begun = emit = final = None
     if mode == "rest":
         layers, refs = refs[: kind.sources], refs[kind.sources :]
-        begun, refs = refs[:2], refs[2:]
+        begun, refs = refs[:3], refs[3:]
     if mode == "first":
-        begun, refs = refs[:2], refs[2:]
+        begun, refs = refs[:3], refs[3:]
     else:
         final, refs = refs[0], refs[1:]
     if mode == "all":
@@ -569,7 +573,9 @@
     refs = refs[spare:]
     buf, sem, refs = refs[0], refs[1], refs[2:]
     s = Refs()
-    for name, ref in zip(SCRATCH, refs, strict=True):
+    if mode != "all":
+        s.onehot, begun = begun[2], begun[:2]
+    for name, ref in zip(SCRATCH[mode != "all" :], refs, strict=True):
         setattr(s, name, ref)
     base = window_base(sub, count, width)
     if width < count:
@@ -603,11 +609,20 @@
             ]
 
 
+def onehot_shape(kind, width):
+    return (width, 2, (kind.tiles + kind.extra_tiles) * 256, LANES)
+
+
 def begun_shapes(kind, width):
     return [
         jax.ShapeDtypeStruct((width, kind.blocks, 8, LANES), F32),
         jax.ShapeDtypeStruct((width + 2, 8, LANES), F32),
+        jax.ShapeDtypeStruct(onehot_shape(kind, width), BF16),
     ]
+
+
+def vmem_limit(width):
+    return (24 if width <= 8 else 60) * 1024 * 1024
 
 
 def layer_shape(width):
@@ -632,7 +647,8 @@
             pltpu.VMEM((width, kind.rows, LANES), F32),
             pltpu.SemaphoreType.DMA((2 * len(offsets),)),
         ]
-        + scratch_of(kind, width, unroll),
+        + scratch_of(kind, width, unroll)[mode != "all" :],
+        compiler_params=pltpu.CompilerParams(vmem_limit_bytes=vmem_limit(width)),
         name="sim_" + mode,
     )(*bufs, *tables, *more)
 

time: 91.1 us -> 87.2 us (0.957)
  Pallas kernels: 47.3 us -> 44.7 us
  local copies, waits for them, and re-layouts: 3.31 us -> 1.92 us
    pallas_call x2, Pallas kernels: 42.9 us -> 40.2 us  [run_sim(): pl.pallas_call(functools.partial(sim_kernel, kind, width, unroll, offsets...]
    cond x16 -> x6, local copies, waits for them, and re-layouts: 2.03 us -> 1.32 us
where the time goes in v5:
time: 87.2 us; the launch traced here: 86.7 us
  Pallas kernels  44.7 us (51%)
  waiting for transfers between devices  23.2 us (27%)
  starting transfers between devices  16.1 us (18%)
  local copies, waits for them, and re-layouts  1.92 us (2%)
    pallas_call x2, Pallas kernels, run_sim(): pl.pallas_call(functools.partial(sim_kernel, kind, width, unroll, offsets...  40.2 us
    ppermute x3, waiting for transfers between devices, shards(): lax.ppermute(layer_out, 'grp', [(m * site_groups + i, reg_groups + i) for...  13.1 us
    ppermute x4, starting transfers between devices, moved(): return lax.ppermute(array, ('grp', 'sub'), route)  12.2 us
    ppermute x4, waiting for transfers between devices, moved(): return lax.ppermute(array, ('grp', 'sub'), route)  10.1 us
    ppermute x3, starting transfers between devices, shards(): lax.ppermute(layer_out, 'grp', [(m * site_groups + i, reg_groups + i) for...  3.88 us
    pallas_call x1, Pallas kernels, gather_window(): pl.pallas_call(join_kernel, out_shape=jax.ShapeDtypeStruct((len(offsets),...  1.98 us
    pallas_call x1, Pallas kernels, pack(): pl.pallas_call(functools.partial(pack_kernel, kind), out_shape=[jax.Shape...  1.85 us
  transfers between devices with their start and end apart: 7, of which 4 were waited for; matrix products, arithmetic and copies ran while one was open for 0% of the time, Pallas kernels for 1%

profile of v5, /device:TPU:6, one launch (start us, length us, event | category | flops | bytes accessed | tf_op | source)
XLA Modules:
  0.0 86.7 jit_solution(6963332389380951746)
XLA Ops:
  0.6 39.1 %conditional.2 = (f32[8,3,8,128]{3,2,1,0:T(8,128)S(1)}, f32[4,280,128]{2,1,0:T(8,128)}, f32[4,280,128]{2,1,0:T(8,128)}, bf16[72,128]{1,0:T(8,128)(2,1)}, bf16[40...) conditional(s32[]{:T(128)} %convert_element_type.4, ...), branch_computations={%region_0.0_spmd, %region_1.0_spmd} | conditional | bytes 5734716 | solution.py:749
  0.7 1.9 %site_pack.1 = (f32[280,128]{1,0:T(8,128)}, bf16[72,128]{1,0:T(8,128)(2,1)}, bf16[40,224]{1,0:T(8,128)(2,1)}) custom-call(f32[1,3,1,1536]{3,2,1,0:T(1,128)} %bitcast.31, f32[1,3,1,1536]{3,2,1,0:T(1,128)} %bitcast.32, s32[1,35,1,128]{3,2,1,0:T(1,128)} %bitcast.34, f32[1,1,3,3,24,128]{5,4,3,2,1,0:T(8,128)} %get-tuple-element.195.refs_3_, ...), custom_call_target="tpu_custom_call" | custom-call | tf_op jit(solution)/shard_map/cond/branch_1_fun/site_pack/pallas_call | solution.py:144
  2.5 5.5 %collective-permute-start.6 = (f32[280,128]{1,0:T(8,128)}, f32[280,128]{1,0:T(8,128)S(1)}, u32[]{:S(2)}, u32[]{:S(2)}) collective-permute-start(f32[280,128]{1,0:T(8,128)} %get-tuple-element.122.refs_0_), channel_id=1, source_target_pairs={{24,30},{25,31},{26,24},{27,25},{28,26},{29,27},{30,28},{31,29}} | collective-permute-start | bytes 430088 | tf_op jit(solution)/shard_map/cond/branch_1_fun/ppermute | solution.py:671
  8.0 1.9 %collective-permute-start.5 = (f32[280,128]{1,0:T(8,128)}, f32[280,128]{1,0:T(8,128)S(1)}, u32[]{:S(2)}, u32[]{:S(2)}) collective-permute-start(f32[280,128]{1,0:T(8,128)} %get-tuple-element.122.refs_0_), channel_id=1, source_target_pairs={{24,28},{25,29},{26,30},{27,31},{28,24},{29,25},{30,26},{31,27}} | collective-permute-start | bytes 430088 | tf_op jit(solution)/shard_map/cond/branch_1_fun/ppermute | solution.py:671
  10.0 2.9 %collective-permute-start.4 = (f32[280,128]{1,0:T(8,128)}, f32[280,128]{1,0:T(8,128)S(1)}, u32[]{:S(2)}, u32[]{:S(2)}) collective-permute-start(f32[280,128]{1,0:T(8,128)} %get-tuple-element.122.refs_0_), channel_id=1, source_target_pairs={{24,26},{25,27},{26,28},{27,29},{28,30},{29,31},{30,24},{31,25}} | collective-permute-start | bytes 430088 | tf_op jit(solution)/shard_map/cond/branch_1_fun/ppermute | solution.py:671
  12.9 0.0 collective-permute-done.6.refs_3_
  12.9 8.4 %collective-permute-done.5.refs_2_ = f32[280,128]{1,0:T(8,128)S(1)} collective-permute-done((f32[280,128]{1,0:T(8,128)}, f32[280,128]{1,0:T(8,128)S(1)}, u32[]{:S(2)}, u32[]{:S(2)}) %collective-permute-start.5) | collective-permute-done | bytes 143392 | tf_op jit(solution)/shard_map/cond/branch_1_fun/ppermute | solution.py:671
  21.3 0.0 collective-permute-done.4.refs_1_
  21.3 0.7 copy-done.4
  22.0 0.7 copy-done.5
  22.7 2.0 %join.3.refs_0_ = f32[4,280,128]{2,1,0:T(8,128)} custom-call(f32[280,128]{1,0:T(8,128)} %get-tuple-element.122.refs_0_, f32[280,128]{1,0:T(8,128)} %copy-done.5, f32[280,128]{1,0:T(8,128)} %copy-done.4, f32[280,128]{1,0:T(8,128)} %copy-done.3), custom_call_target="tpu_custom_call" | custom-call | tf_op jit(solution)/shard_map/cond/branch_1_fun/join/pallas_call | solution.py:677
  24.6 1.9 %collective-permute-start.7 = (f32[4,280,128]{2,1,0:T(8,128)}, f32[4,280,128]{2,1,0:T(8,128)}, u32[]{:S(2)}, u32[]{:S(2)}) collective-permute-start(f32[4,280,128]{2,1,0:T(8,128)} %join.3.refs_0_), channel_id=1, source_target_pairs={{24,25},{25,24},{26,27},{27,26},{28,29},{29,28},{30,31},{31,30}} | collective-permute-start | bytes 1720328 | tf_op jit(solution)/shard_map/cond/branch_1_fun/ppermute | solution.py:671
  26.6 0.6 blank.1
  27.2 1.7 %collective-permute-done.7.refs_1_ = f32[4,280,128]{2,1,0:T(8,128)} collective-permute-done((f32[4,280,128]{2,1,0:T(8,128)}, f32[4,280,128]{2,1,0:T(8,128)}, u32[]{:S(2)}, u32[]{:S(2)}) %collective-permute-start.7) | collective-permute-done | bytes 573472 | tf_op jit(solution)/shard_map/cond/branch_1_fun/ppermute | solution.py:671
  28.8 10.9 %sim_first.1 = (f32[8,12,8,128]{3,2,1,0:T(8,128)S(1)}, f32[10,8,128]{2,1,0:T(8,128)S(1)}, bf16[8,2,2816,128]{3,2,1,0:T(8,128)(2,1)S(1)}) custom-call(f32[4,280,128]{2,1,0:T(8,128)} %join.3.refs_0_, f32[4,280,128]{2,1,0:T(8,128)} %collective-permute-done.7.refs_1_, bf16[72,128]{1,0:T(8,128)(2,1)} %get-tuple-element.236.refs_2_, ...), custom_call_target="tpu_custom_call" | custom-call | tf_op jit(solution)/shard_map/cond/branch_1_fun/sim_first/pallas_call | solution.py:641
  39.8 1.3 %collective-permute-start.10 = (f32[8,3,8,128]{3,2,1,0:T(8,128)S(1)}, f32[8,3,8,128]{3,2,1,0:T(8,128)S(1)}, u32[]{:S(2)}, u32[]{:S(2)}) collective-permute-start(f32[8,3,8,128]{3,2,1,0:T(8,128)S(1)} %get-tuple-element.155), channel_id=1, source_target_pairs={{16,24},{17,25},{18,26},{19,27},{20,28},{21,29},{22,30},{23,31}} | collective-permute-start | bytes 294920 | tf_op jit(solution)/shard_map/ppermute | solution.py:752
  41.1 1.3 %collective-permute-start.9 = (f32[8,3,8,128]{3,2,1,0:T(8,128)S(1)}, f32[8,3,8,128]{3,2,1,0:T(8,128)S(1)}, u32[]{:S(2)}, u32[]{:S(2)}) collective-permute-start(f32[8,3,8,128]{3,2,1,0:T(8,128)S(1)} %get-tuple-element.155), channel_id=1, source_target_pairs={{8,24},{9,25},{10,26},{11,27},{12,28},{13,29},{14,30},{15,31}} | collective-permute-start | bytes 294920 | tf_op jit(solution)/shard_map/ppermute | solution.py:752
  42.4 1.3 %collective-permute-start.8 = (f32[8,3,8,128]{3,2,1,0:T(8,128)S(1)}, f32[8,3,8,128]{3,2,1,0:T(8,128)S(1)}, u32[]{:S(2)}, u32[]{:S(2)}) collective-permute-start(f32[8,3,8,128]{3,2,1,0:T(8,128)S(1)} %get-tuple-element.155), channel_id=1, source_target_pairs={{0,24},{1,25},{2,26},{3,27},{4,28},{5,29},{6,30},{7,31}} | collective-permute-start | bytes 294920 | tf_op jit(solution)/shard_map/ppermute | solution.py:752
  43.7 10.3 %collective-permute-done.10 = f32[8,3,8,128]{3,2,1,0:T(8,128)S(1)} collective-permute-done((f32[8,3,8,128]{3,2,1,0:T(8,128)S(1)}, f32[8,3,8,128]{3,2,1,0:T(8,128)S(1)}, u32[]{:S(2)}, u32[]{:S(2)}) %collective-permute-start.10) | collective-permute-done | bytes 98336 | tf_op jit(solution)/shard_map/ppermute | solution.py:752
  54.0 2.8 %collective-permute-done.9 = f32[8,3,8,128]{3,2,1,0:T(8,128)S(1)} collective-permute-done((f32[8,3,8,128]{3,2,1,0:T(8,128)S(1)}, f32[8,3,8,128]{3,2,1,0:T(8,128)S(1)}, u32[]{:S(2)}, u32[]{:S(2)}) %collective-permute-start.9) | collective-permute-done | bytes 98336 | tf_op jit(solution)/shard_map/ppermute | solution.py:752
  56.7 29.3 %conditional.3 = (f32[1,1,3,1536]{3,1,2,0:T(1,128)S(1)}) conditional(s32[]{:T(128)} %convert_element_type.4, () %tuple.31, (f32[4,280,128]{2,1,0:T(8,128)}, f32[4,280,128]{2,1,0:T(8,128)}, bf16[72,128]{1,0:T(8,128)(2,1)}, bf16[40,224]{1,0:T(8,128)(2,1)}, f32[8,3,8,128]{3,2,1,0:T(8,128)S(1)}, /*index=5*/f32[8,3,8,128]{3,2,1,0:T(8,128)S(1)}, ...), branch_computations={%region_2.0_spmd, %region_3.0_spmd} | conditional | bytes 18444 | solution.py:767
  56.7 29.3 %sim_rest.1 = f32[1,3,1,1536]{3,2,1,0:T(1,128)S(1)} custom-call(f32[4,280,128]{2,1,0:T(8,128)} %get-tuple-element.129.refs_0_, f32[4,280,128]{2,1,0:T(8,128)} %get-tuple-element.130.refs_1_, bf16[72,128]{1,0:T(8,128)(2,1)} %get-tuple-element.131.refs_2_, bf16[40,224]{1,0:T(8,128)(2,1)} %get-tuple-element.132.refs_3_, ...), custom_call_target="tpu_custom_call" | custom-call | tf_op jit(solution)/shard_map/cond/branch_1_fun/sim_rest/pallas_call | solution.py:641
  86.1 0.0 copy-start.9
  86.1 0.6 copy-done.9
  (5 shorter events, 0.0 us)
Async XLA Ops:
  2.5 10.4 %collective-permute-start.6 = (f32[280,128]{1,0:T(8,128)}, f32[280,128]{1,0:T(8,128)S(1)}, u32[]{:S(2)}, u32[]{:S(2)}) collective-permute-start(f32[280,128]{1,0:T(8,128)} %get-tuple-element.122.refs_0_), channel_id=1, source_target_pairs={{24,30},{25,31},{26,24},{27,25},{28,26},{29,27},{30,28},{31,29}} | collective-permute-start | bytes 430088 | tf_op jit(solution)/shard_map/cond/branch_1_fun/ppermute | solution.py:671
  8.0 13.3 %collective-permute-start.5 = (f32[280,128]{1,0:T(8,128)}, f32[280,128]{1,0:T(8,128)S(1)}, u32[]{:S(2)}, u32[]{:S(2)}) collective-permute-start(f32[280,128]{1,0:T(8,128)} %get-tuple-element.122.refs_0_), channel_id=1, source_target_pairs={{24,28},{25,29},{26,30},{27,31},{28,24},{29,25},{30,26},{31,27}} | collective-permute-start | bytes 430088 | tf_op jit(solution)/shard_map/cond/branch_1_fun/ppermute | solution.py:671
  10.0 11.4 %collective-permute-start.4 = (f32[280,128]{1,0:T(8,128)}, f32[280,128]{1,0:T(8,128)S(1)}, u32[]{:S(2)}, u32[]{:S(2)}) collective-permute-start(f32[280,128]{1,0:T(8,128)} %get-tuple-element.122.refs_0_), channel_id=1, source_target_pairs={{24,26},{25,27},{26,28},{27,29},{28,30},{29,31},{30,24},{31,25}} | collective-permute-start | bytes 430088 | tf_op jit(solution)/shard_map/cond/branch_1_fun/ppermute | solution.py:671
  12.9 8.4 %copy-start.3 = (f32[280,128]{1,0:T(8,128)}, f32[280,128]{1,0:T(8,128)S(1)}, u32[]{:S(2)}) copy-start(f32[280,128]{1,0:T(8,128)S(1)} %collective-permute-done.6.refs_3_) | copy-start | bytes 430084 | tf_op jit(solution)/shard_map/cond
  21.3 0.7 copy-start.4
  22.0 0.7 copy-start.5
  24.6 4.2 %collective-permute-start.7 = (f32[4,280,128]{2,1,0:T(8,128)}, f32[4,280,128]{2,1,0:T(8,128)}, u32[]{:S(2)}, u32[]{:S(2)}) collective-permute-start(f32[4,280,128]{2,1,0:T(8,128)} %join.3.refs_0_), channel_id=1, source_target_pairs={{24,25},{25,24},{26,27},{27,26},{28,29},{29,28},{30,31},{31,30}} | collective-permute-start | bytes 1720328 | tf_op jit(solution)/shard_map/cond/branch_1_fun/ppermute | solution.py:671
  39.8 14.2 %collective-permute-start.10 = (f32[8,3,8,128]{3,2,1,0:T(8,128)S(1)}, f32[8,3,8,128]{3,2,1,0:T(8,128)S(1)}, u32[]{:S(2)}, u32[]{:S(2)}) collective-permute-start(f32[8,3,8,128]{3,2,1,0:T(8,128)S(1)} %get-tuple-element.155), channel_id=1, source_target_pairs={{16,24},{17,25},{18,26},{19,27},{20,28},{21,29},{22,30},{23,31}} | collective-permute-start | bytes 294920 | tf_op jit(solution)/shard_map/ppermute | solution.py:752
  41.1 15.7 %collective-permute-start.9 = (f32[8,3,8,128]{3,2,1,0:T(8,128)S(1)}, f32[8,3,8,128]{3,2,1,0:T(8,128)S(1)}, u32[]{:S(2)}, u32[]{:S(2)}) collective-permute-start(f32[8,3,8,128]{3,2,1,0:T(8,128)S(1)} %get-tuple-element.155), channel_id=1, source_target_pairs={{8,24},{9,25},{10,26},{11,27},{12,28},{13,29},{14,30},{15,31}} | collective-permute-start | bytes 294920 | tf_op jit(solution)/shard_map/ppermute | solution.py:752
  42.4 14.4 %collective-permute-start.8 = (f32[8,3,8,128]{3,2,1,0:T(8,128)S(1)}, f32[8,3,8,128]{3,2,1,0:T(8,128)S(1)}, u32[]{:S(2)}, u32[]{:S(2)}) collective-permute-start(f32[8,3,8,128]{3,2,1,0:T(8,128)S(1)} %get-tuple-element.155), channel_id=1, source_target_pairs={{0,24},{1,25},{2,26},{3,27},{4,28},{5,29},{6,30},{7,31}} | collective-permute-start | bytes 294920 | tf_op jit(solution)/shard_map/ppermute | solution.py:752
  86.1 0.6 copy-start.9
